TPU v7x, 512 devices: a whole 4x4x16 slice. The times are simulated.
512 devices in a mesh: grp: 4 (over y), row: 128 (over x, z, core).
Axes of the slice: x: 4, y: 4, z: 16, core: 2. Of those that a mesh axis runs over, the one named last changes fastest.
Arguments:
- a_tiles: bfloat16 [1024, 4, 7, 128, 128], P('row', 'grp'), may hold values from -0.5 to 0.5
- a_cols: int32 [1024, 4, 7], P('row', 'grp'), may hold values from 0 to 1023, as said below
- p_tiles: bfloat16 [1024, 4, 128, 128], P('row'), may hold values from -0.5 to 0.5
- p_cols: int32 [1024, 4], replicated, may hold values from 0 to 511, as said below
- c_cols: int32 [512, 16], replicated, may hold values from 0 to 511, as said below
Outputs:
- coarse: float32 [512, 16, 128, 128], P('row', 'grp')
Inputs may be any that keep to these rules, and one draw needn't show every extreme that they name: For fine tile row i in block b = i // 8, every entry of a_cols[i] lies in [max(b - 2, 0) * 8, min(b + 3, 128) * 8). For fine tile row i in block b = i // 8, the entries of p_cols[i] are distinct and lie in [(b - 1) * 4, (b + 2) * 4). For coarse tile row c in block t = c // 4, the entries of c_cols[c] are distinct and lie among the 20 coarse tile rows that start at min(max(t - 2, 0), 123) * 4.
All inputs are finite; a program needn't handle non-finite values.
Results may differ from a plain program's by a relative error of at most 0.0003.
Values may be sent and summed in bfloat16 or wider, within the bound.
No kernel may reach another device: no remote copies, remote signals or barrier semaphores. Data moves between devices by JAX's collectives and lax.ppermute only.
A program may use at most 128 MiB of HBM per device.

v0:
```python
import jax
import jax.numpy as jnp
from jax import lax
from jax.sharding import PartitionSpec as P

RATIO = 2


highest = lax.Precision.HIGHEST


def passed_along(x, axis, by):
    size = lax.axis_size(axis)
    pairs = [(i, i + by) for i in range(size) if 0 <= i + by < size]
    return lax.ppermute(x, axis, pairs)


def in_blocks(x, dim, size):
    shape = x.shape
    tiles = x.reshape(*shape[:dim], size, shape[dim] // size, *shape[dim + 1 :])
    return jnp.moveaxis(tiles, dim, 0)


def summed_on_arrival(x, axis, dim):
    tiles = in_blocks(x, dim, lax.axis_size(axis))
    arrived = lax.all_to_all(tiles, axis, split_axis=0, concat_axis=0, tiled=True)
    return arrived.sum(axis=0)


def body(a_tiles, a_cols, p_tiles, p_cols, c_cols):
    fine_rows = a_tiles.shape[0]
    coarse_rows = fine_rows // RATIO
    tile_size = a_tiles.shape[-1]
    position = lax.axis_index("row")
    first_row = position * fine_rows
    fetched_rows = []
    for offset in (2, 1, -1, -2):
        fetched_rows.append(passed_along(p_tiles, "row", offset))
    band_tiles = jnp.concatenate(
        [fetched_rows[0], fetched_rows[1], p_tiles, fetched_rows[2], fetched_rows[3]], axis=0
    )
    padded = jnp.pad(p_cols, ((2 * fine_rows, 2 * fine_rows), (0, 0)), constant_values=-1)
    band_cols = lax.dynamic_slice_in_dim(padded, first_row, 5 * fine_rows, 0)
    own_cols = lax.dynamic_slice_in_dim(p_cols, first_row, fine_rows, 0)
    window = (position - 3) * coarse_rows + jnp.arange(7 * coarse_rows, dtype=jnp.int32)
    base_coarse = (position - 1) * coarse_rows
    local_cols = a_cols[:, 0, :] - (first_row - 2 * fine_rows)

    def fine_row(total, inputs):
        a_row, local_row, own_tiles, own_row_cols = inputs
        fetched = band_tiles[local_row]
        fetched_cols = band_cols[local_row]
        products = jnp.einsum("sxy,spyz->spxz", a_row, fetched, preferred_element_type=jnp.float32)
        placing = (fetched_cols[:, :, None] == window[None, None, :]).astype(jnp.float32)
        spread = jnp.einsum("spxz,spw->wxz", products, placing, precision=highest)
        targets = c_cols[own_row_cols]
        choose = (targets[:, :, None] == window[None, None, :]).astype(jnp.float32)
        chosen = jnp.einsum("qkw,wxz->qkxz", choose, spread, precision=highest)
        row_terms = jnp.einsum(
            "qyx,qkyz->qkxz", own_tiles.astype(jnp.float32), chosen, precision=highest
        )
        local_index = own_row_cols - base_coarse
        return (total.at[local_index].add(row_terms), None)

    initial = jnp.zeros((3 * coarse_rows, c_cols.shape[1], tile_size, tile_size), jnp.float32)
    total = lax.scan(fine_row, initial, (a_tiles[:, 0], local_cols, p_tiles, own_cols))[0]
    center = total[coarse_rows : 2 * coarse_rows]
    for offset, side_block in ((-1, total[:coarse_rows]), (1, total[2 * coarse_rows :])):
        center = center + passed_along(side_block, "row", offset)
    result = summed_on_arrival(center, "grp", 1)
    return result


def solution(mesh):
    return jax.shard_map(
        body,
        mesh=mesh,
        in_specs=(
            P("row", "grp", None, None, None),
            P("row", "grp", None),
            P("row", None, None, None),
            P(),
            P(),
        ),
        out_specs=P("row", "grp", None, None),
        check_vma=False,
    )
```

profile of v0, /device:TPU:6, one launch (start us, length us, event | category | flops | bytes accessed | tf_op | source)
XLA Modules:
  0.0 433.1 jit_solution(5140706142570658629)
XLA Ops:
  0.0 3.9 collective-permute-start
  5.9 9.2 %collective-permute-start.2 = (bf16[8,4,128,128]{3,2,1,0:T(8,128)(2,1)}, bf16[8,4,128,128]{3,2,1,0:T(8,128)(2,1)}, u32[]{:S(2)}, u32[]{:S(2)}) collective-permute-start(bf16[8,4,128,128]{3,2,1,0:T(8,128)(2,1)} %param.9), channel_id=1, source_target_pairs={{1,0},{2,1},{3,2},{4,3},{5,4},{6,5},{7,6},{8,7},{9,8},{10,9},{11,1... | collective-permute-start | bytes 3145736 | tf_op jit(solution)/shard_map/ppermute | solution.py:15
  15.1 4.2 collective-permute-start.3
  22.0 14.1 %collective-permute-done = bf16[8,4,128,128]{3,2,1,0:T(8,128)(2,1)} collective-permute-done((bf16[8,4,128,128]{3,2,1,0:T(8,128)(2,1)}, bf16[8,4,128,128]{3,2,1,0:T(8,128)(2,1)}, u32[]{:S(2)}, u32[]{:S(2)}) %collective-permute-start) | collective-permute-done | bytes 1048608 | tf_op jit(solution)/shard_map/ppermute | solution.py:15
  38.5 8.0 %collective-permute-done.1 = bf16[8,4,128,128]{3,2,1,0:T(8,128)(2,1)} collective-permute-done((bf16[8,4,128,128]{3,2,1,0:T(8,128)(2,1)}, bf16[8,4,128,128]{3,2,1,0:T(8,128)(2,1)}, u32[]{:S(2)}, u32[]{:S(2)}) %collective-permute-start.1) | collective-permute-done | bytes 1048608 | tf_op jit(solution)/shard_map/ppermute | solution.py:15
  53.3 6.1 %broadcast_in_dim.2 = f32[12,16,128,128]{3,2,1,0:T(8,128)} broadcast(f32[]{:T(128)} %constant.23.clone.1), dimensions={} | broadcast | bytes 12582916 | tf_op jit(solution)/shard_map/broadcast_in_dim | solution.py:65
  59.4 258.8 %while.11 = (s32[]{:T(128)}, f32[12,16,128,128]{3,2,1,0:T(8,128)}, s32[8,4]{1,0:T(8,128)S(1)}, s32[]{:T(128)}, s32[512,16]{1,0:T(8,128)S(1)}, /*index=5*/s32[8,7...) while((s32[]{:T(128)}, f32[12,16,128,128]{3,2,1,0:T(8,128)}, ...), condition=%wide.region_2.3_spmd.clone, body=%wide.region_0.2_spmd.clone.sunk | while | flops 2235568640 | bytes 51881796 | solution.py:66
  60.6 3.2 gather_fusion
  67.2 3.2 fusion.55
  72.3 5.1 %fusion.57 = f32[4,16,128,128]{2,3,1,0:T(8,128)} fusion(f32[4,16,128,128]{3,1,2,0:T(8,128)S(1)} %fusion.56, bf16[8,4,128,128]{3,2,1,0:T(8,128)(2,1)S(1)} %copy-done.1, s32[]{:T(128)S(6)} %copy.47), kind=kOutput, calls=%fused_computation.7.clone.1 | convolution fusion | flops 1610612736 | bytes 8519684 | tf_op jit(solution)/shard_map/while/body/eval_jaxpr/qyx,qkyz->qkxz/dot_general | solution.py:59
  77.4 5.4 %copy.39 = f32[4,16,128,128]{3,2,1,0:T(8,128)} copy(f32[4,16,128,128]{2,3,1,0:T(8,128)} %fusion.57) | data formatting | bytes 8388608 | tf_op jit(solution)/shard_map/while/body/eval_jaxpr/qyx,qkyz->qkxz/transpose | solution.py:59
  82.8 9.0 %scatter_fusion = f32[12,16,128,128]{3,2,1,0:T(8,128)} fusion(f32[12,16,128,128]{3,2,1,0:T(8,128)} %get-tuple-element.231, s32[4]{0:T(128)S(1)} %get-tuple-element.216, f32[4,16,128,128]{3,2,1,0:T(8,128)} %copy.39), kind=kCustom, calls=%fused_computation.3.clone.clone.1 | custom fusion | flops 1048576 | bytes 12582928 | tf_op jit(solution)/shard_map/while/body/eval_jaxpr/scatter-add | solution.py:63
  92.9 3.2 gather_fusion
  99.5 3.2 fusion.55
  104.7 5.1 %fusion.57 = f32[4,16,128,128]{2,3,1,0:T(8,128)} fusion(f32[4,16,128,128]{3,1,2,0:T(8,128)S(1)} %fusion.56, bf16[8,4,128,128]{3,2,1,0:T(8,128)(2,1)S(1)} %copy-done.1, s32[]{:T(128)S(6)} %copy.47), kind=kOutput, calls=%fused_computation.7.clone.1 | convolution fusion | flops 1610612736 | bytes 8519684 | tf_op jit(solution)/shard_map/while/body/eval_jaxpr/qyx,qkyz->qkxz/dot_general | solution.py:59
  109.8 5.4 %copy.39 = f32[4,16,128,128]{3,2,1,0:T(8,128)} copy(f32[4,16,128,128]{2,3,1,0:T(8,128)} %fusion.57) | data formatting | bytes 8388608 | tf_op jit(solution)/shard_map/while/body/eval_jaxpr/qyx,qkyz->qkxz/transpose | solution.py:59
  115.1 8.9 %scatter_fusion = f32[12,16,128,128]{3,2,1,0:T(8,128)} fusion(f32[12,16,128,128]{3,2,1,0:T(8,128)} %get-tuple-element.231, s32[4]{0:T(128)S(1)} %get-tuple-element.216, f32[4,16,128,128]{3,2,1,0:T(8,128)} %copy.39), kind=kCustom, calls=%fused_computation.3.clone.clone.1 | custom fusion | flops 1048576 | bytes 12582928 | tf_op jit(solution)/shard_map/while/body/eval_jaxpr/scatter-add | solution.py:63
  125.2 3.2 gather_fusion
  131.9 3.2 fusion.55
  137.0 5.1 %fusion.57 = f32[4,16,128,128]{2,3,1,0:T(8,128)} fusion(f32[4,16,128,128]{3,1,2,0:T(8,128)S(1)} %fusion.56, bf16[8,4,128,128]{3,2,1,0:T(8,128)(2,1)S(1)} %copy-done.1, s32[]{:T(128)S(6)} %copy.47), kind=kOutput, calls=%fused_computation.7.clone.1 | convolution fusion | flops 1610612736 | bytes 8519684 | tf_op jit(solution)/shard_map/while/body/eval_jaxpr/qyx,qkyz->qkxz/dot_general | solution.py:59
  142.1 5.4 %copy.39 = f32[4,16,128,128]{3,2,1,0:T(8,128)} copy(f32[4,16,128,128]{2,3,1,0:T(8,128)} %fusion.57) | data formatting | bytes 8388608 | tf_op jit(solution)/shard_map/while/body/eval_jaxpr/qyx,qkyz->qkxz/transpose | solution.py:59
  147.4 9.0 %scatter_fusion = f32[12,16,128,128]{3,2,1,0:T(8,128)} fusion(f32[12,16,128,128]{3,2,1,0:T(8,128)} %get-tuple-element.231, s32[4]{0:T(128)S(1)} %get-tuple-element.216, f32[4,16,128,128]{3,2,1,0:T(8,128)} %copy.39), kind=kCustom, calls=%fused_computation.3.clone.clone.1 | custom fusion | flops 1048576 | bytes 12582928 | tf_op jit(solution)/shard_map/while/body/eval_jaxpr/scatter-add | solution.py:63
  164.2 3.2 fusion.55
  169.3 5.1 %fusion.57 = f32[4,16,128,128]{2,3,1,0:T(8,128)} fusion(f32[4,16,128,128]{3,1,2,0:T(8,128)S(1)} %fusion.56, bf16[8,4,128,128]{3,2,1,0:T(8,128)(2,1)S(1)} %copy-done.1, s32[]{:T(128)S(6)} %copy.47), kind=kOutput, calls=%fused_computation.7.clone.1 | convolution fusion | flops 1610612736 | bytes 8519684 | tf_op jit(solution)/shard_map/while/body/eval_jaxpr/qyx,qkyz->qkxz/dot_general | solution.py:59
  174.4 5.4 %copy.39 = f32[4,16,128,128]{3,2,1,0:T(8,128)} copy(f32[4,16,128,128]{2,3,1,0:T(8,128)} %fusion.57) | data formatting | bytes 8388608 | tf_op jit(solution)/shard_map/while/body/eval_jaxpr/qyx,qkyz->qkxz/transpose | solution.py:59
  179.8 8.9 %scatter_fusion = f32[12,16,128,128]{3,2,1,0:T(8,128)} fusion(f32[12,16,128,128]{3,2,1,0:T(8,128)} %get-tuple-element.231, s32[4]{0:T(128)S(1)} %get-tuple-element.216, f32[4,16,128,128]{3,2,1,0:T(8,128)} %copy.39), kind=kCustom, calls=%fused_computation.3.clone.clone.1 | custom fusion | flops 1048576 | bytes 12582928 | tf_op jit(solution)/shard_map/while/body/eval_jaxpr/scatter-add | solution.py:63
  196.5 3.2 fusion.55
  201.6 5.1 %fusion.57 = f32[4,16,128,128]{2,3,1,0:T(8,128)} fusion(f32[4,16,128,128]{3,1,2,0:T(8,128)S(1)} %fusion.56, bf16[8,4,128,128]{3,2,1,0:T(8,128)(2,1)S(1)} %copy-done.1, s32[]{:T(128)S(6)} %copy.47), kind=kOutput, calls=%fused_computation.7.clone.1 | convolution fusion | flops 1610612736 | bytes 8519684 | tf_op jit(solution)/shard_map/while/body/eval_jaxpr/qyx,qkyz->qkxz/dot_general | solution.py:59
  206.7 5.4 %copy.39 = f32[4,16,128,128]{3,2,1,0:T(8,128)} copy(f32[4,16,128,128]{2,3,1,0:T(8,128)} %fusion.57) | data formatting | bytes 8388608 | tf_op jit(solution)/shard_map/while/body/eval_jaxpr/qyx,qkyz->qkxz/transpose | solution.py:59
  212.1 9.0 %scatter_fusion = f32[12,16,128,128]{3,2,1,0:T(8,128)} fusion(f32[12,16,128,128]{3,2,1,0:T(8,128)} %get-tuple-element.231, s32[4]{0:T(128)S(1)} %get-tuple-element.216, f32[4,16,128,128]{3,2,1,0:T(8,128)} %copy.39), kind=kCustom, calls=%fused_computation.3.clone.clone.1 | custom fusion | flops 1048576 | bytes 12582928 | tf_op jit(solution)/shard_map/while/body/eval_jaxpr/scatter-add | solution.py:63
  228.9 3.2 fusion.55
  234.0 5.1 %fusion.57 = f32[4,16,128,128]{2,3,1,0:T(8,128)} fusion(f32[4,16,128,128]{3,1,2,0:T(8,128)S(1)} %fusion.56, bf16[8,4,128,128]{3,2,1,0:T(8,128)(2,1)S(1)} %copy-done.1, s32[]{:T(128)S(6)} %copy.47), kind=kOutput, calls=%fused_computation.7.clone.1 | convolution fusion | flops 1610612736 | bytes 8519684 | tf_op jit(solution)/shard_map/while/body/eval_jaxpr/qyx,qkyz->qkxz/dot_general | solution.py:59
  239.1 5.4 %copy.39 = f32[4,16,128,128]{3,2,1,0:T(8,128)} copy(f32[4,16,128,128]{2,3,1,0:T(8,128)} %fusion.57) | data formatting | bytes 8388608 | tf_op jit(solution)/shard_map/while/body/eval_jaxpr/qyx,qkyz->qkxz/transpose | solution.py:59
  244.4 9.0 %scatter_fusion = f32[12,16,128,128]{3,2,1,0:T(8,128)} fusion(f32[12,16,128,128]{3,2,1,0:T(8,128)} %get-tuple-element.231, s32[4]{0:T(128)S(1)} %get-tuple-element.216, f32[4,16,128,128]{3,2,1,0:T(8,128)} %copy.39), kind=kCustom, calls=%fused_computation.3.clone.clone.1 | custom fusion | flops 1048576 | bytes 12582928 | tf_op jit(solution)/shard_map/while/body/eval_jaxpr/scatter-add | solution.py:63
  261.2 3.2 fusion.55
  266.4 5.1 %fusion.57 = f32[4,16,128,128]{2,3,1,0:T(8,128)} fusion(f32[4,16,128,128]{3,1,2,0:T(8,128)S(1)} %fusion.56, bf16[8,4,128,128]{3,2,1,0:T(8,128)(2,1)S(1)} %copy-done.1, s32[]{:T(128)S(6)} %copy.47), kind=kOutput, calls=%fused_computation.7.clone.1 | convolution fusion | flops 1610612736 | bytes 8519684 | tf_op jit(solution)/shard_map/while/body/eval_jaxpr/qyx,qkyz->qkxz/dot_general | solution.py:59
  271.4 5.4 %copy.39 = f32[4,16,128,128]{3,2,1,0:T(8,128)} copy(f32[4,16,128,128]{2,3,1,0:T(8,128)} %fusion.57) | data formatting | bytes 8388608 | tf_op jit(solution)/shard_map/while/body/eval_jaxpr/qyx,qkyz->qkxz/transpose | solution.py:59
  276.8 9.0 %scatter_fusion = f32[12,16,128,128]{3,2,1,0:T(8,128)} fusion(f32[12,16,128,128]{3,2,1,0:T(8,128)} %get-tuple-element.231, s32[4]{0:T(128)S(1)} %get-tuple-element.216, f32[4,16,128,128]{3,2,1,0:T(8,128)} %copy.39), kind=kCustom, calls=%fused_computation.3.clone.clone.1 | custom fusion | flops 1048576 | bytes 12582928 | tf_op jit(solution)/shard_map/while/body/eval_jaxpr/scatter-add | solution.py:63
  293.6 3.2 fusion.55
  298.7 5.1 %fusion.57 = f32[4,16,128,128]{2,3,1,0:T(8,128)} fusion(f32[4,16,128,128]{3,1,2,0:T(8,128)S(1)} %fusion.56, bf16[8,4,128,128]{3,2,1,0:T(8,128)(2,1)S(1)} %copy-done.1, s32[]{:T(128)S(6)} %copy.47), kind=kOutput, calls=%fused_computation.7.clone.1 | convolution fusion | flops 1610612736 | bytes 8519684 | tf_op jit(solution)/shard_map/while/body/eval_jaxpr/qyx,qkyz->qkxz/dot_general | solution.py:59
  303.8 5.4 %copy.39 = f32[4,16,128,128]{3,2,1,0:T(8,128)} copy(f32[4,16,128,128]{2,3,1,0:T(8,128)} %fusion.57) | data formatting | bytes 8388608 | tf_op jit(solution)/shard_map/while/body/eval_jaxpr/qyx,qkyz->qkxz/transpose | solution.py:59
  309.1 9.1 %scatter_fusion = f32[12,16,128,128]{3,2,1,0:T(8,128)} fusion(f32[12,16,128,128]{3,2,1,0:T(8,128)} %get-tuple-element.231, s32[4]{0:T(128)S(1)} %get-tuple-element.216, f32[4,16,128,128]{3,2,1,0:T(8,128)} %copy.39), kind=kCustom, calls=%fused_computation.3.clone.clone.1 | custom fusion | flops 1048576 | bytes 12582928 | tf_op jit(solution)/shard_map/while/body/eval_jaxpr/scatter-add | solution.py:63
  318.2 4.0 fusion.29
  326.6 43.6 %collective-permute-done.4 = f32[4,16,128,128]{3,2,1,0:T(8,128)S(1)} collective-permute-done((f32[4,16,128,128]{3,2,1,0:T(8,128)S(1)}, f32[4,16,128,128]{3,2,1,0:T(8,128)S(1)}, u32[]{:S(2)}, u32[]{:S(2)}) %collective-permute-start.4) | collective-permute-done | bytes 4194336 | tf_op jit(solution)/shard_map/ppermute | solution.py:15
  370.2 5.9 %collective-permute-done.5 = f32[4,16,128,128]{3,2,1,0:T(8,128)S(1)} collective-permute-done((f32[4,16,128,128]{3,2,1,0:T(8,128)S(1)}, f32[4,16,128,128]{3,2,1,0:T(8,128)S(1)}, u32[]{:S(2)}, u32[]{:S(2)}) %collective-permute-start.5) | collective-permute-done | bytes 4194336 | tf_op jit(solution)/shard_map/ppermute | solution.py:15
  376.1 3.6 add_add_fusion
  380.2 49.2 %all_to_all.5 = f32[4,4,4,128,128]{4,3,2,1,0:T(8,128)} all-to-all(f32[4,4,4,128,128]{4,3,2,1,0:T(8,128)S(1)} %copy.24), channel_id=1, replica_groups=mesh['grp'=4,'row'=128] {'grp'}, dimensions={0} | all-to-all | bytes 8388608 | tf_op jit(solution)/shard_map/all_to_all | solution.py:26
  429.5 3.6 reduce_sum.9
  (120 shorter events, 85.7 us)
Async XLA Ops:
  0.0 48.8 %copy-start = (bf16[8,4,128,128]{3,2,1,0:T(8,128)(2,1)S(1)}, bf16[8,4,128,128]{3,2,1,0:T(8,128)(2,1)}, u32[]{:S(2)}) copy-start(bf16[8,4,128,128]{3,2,1,0:T(8,128)(2,1)} %param.9) | copy-start | bytes 3145732
  0.0 36.1 %collective-permute-start = (bf16[8,4,128,128]{3,2,1,0:T(8,128)(2,1)}, bf16[8,4,128,128]{3,2,1,0:T(8,128)(2,1)}, u32[]{:S(2)}, u32[]{:S(2)}) collective-permute-start(bf16[8,4,128,128]{3,2,1,0:T(8,128)(2,1)} %param.9), channel_id=1, source_target_pairs={{0,2},{1,3},{2,4},{3,5},{4,6},{5,7},{6,8},{7,9},{8,10},{9,11},{10,... | collective-permute-start | bytes 3145736 | tf_op jit(solution)/shard_map/ppermute | solution.py:15
  4.0 42.5 %collective-permute-start.1 = (bf16[8,4,128,128]{3,2,1,0:T(8,128)(2,1)}, bf16[8,4,128,128]{3,2,1,0:T(8,128)(2,1)}, u32[]{:S(2)}, u32[]{:S(2)}) collective-permute-start(bf16[8,4,128,128]{3,2,1,0:T(8,128)(2,1)} %param.9), channel_id=1, source_target_pairs={{0,1},{1,2},{2,3},{3,4},{4,5},{5,6},{6,7},{7,8},{8,9},{9,10},{10,1... | collective-permute-start | bytes 3145736 | tf_op jit(solution)/shard_map/ppermute | solution.py:15
  5.9 44.0 %collective-permute-start.2 = (bf16[8,4,128,128]{3,2,1,0:T(8,128)(2,1)}, bf16[8,4,128,128]{3,2,1,0:T(8,128)(2,1)}, u32[]{:S(2)}, u32[]{:S(2)}) collective-permute-start(bf16[8,4,128,128]{3,2,1,0:T(8,128)(2,1)} %param.9), channel_id=1, source_target_pairs={{1,0},{2,1},{3,2},{4,3},{5,4},{6,5},{7,6},{8,7},{9,8},{10,9},{11,1... | collective-permute-start | bytes 3145736 | tf_op jit(solution)/shard_map/ppermute | solution.py:15
  15.1 37.1 %collective-permute-start.3 = (bf16[8,4,128,128]{3,2,1,0:T(8,128)(2,1)}, bf16[8,4,128,128]{3,2,1,0:T(8,128)(2,1)S(1)}, u32[]{:S(2)}, u32[]{:S(2)}) collective-permute-start(bf16[8,4,128,128]{3,2,1,0:T(8,128)(2,1)} %param.9), channel_id=1, source_target_pairs={{2,0},{3,1},{4,2},{5,3},{6,4},{7,5},{8,6},{9,7},{10,8},{11,9},{12,... | collective-permute-start | bytes 3145736 | tf_op jit(solution)/shard_map/ppermute | solution.py:15
  70.4 1.9 copy-start.1
  102.8 1.9 copy-start.1
  135.1 1.9 copy-start.1
  167.4 1.9 copy-start.1
  199.7 1.9 copy-start.1
  232.1 1.9 copy-start.1
  264.5 1.9 copy-start.1
  296.8 1.9 copy-start.1
  322.3 47.9 %collective-permute-start.4 = (f32[4,16,128,128]{3,2,1,0:T(8,128)S(1)}, f32[4,16,128,128]{3,2,1,0:T(8,128)S(1)}, u32[]{:S(2)}, u32[]{:S(2)}) collective-permute-start(f32[4,16,128,128]{3,2,1,0:T(8,128)S(1)} %get-tuple-element.145), channel_id=1, source_target_pairs={{1,0},{2,1},{3,2},{4,3},{5,4},{6,5},{7,6},{8,7},{9,8},{10,9},{11,1... | collective-permute-start | bytes 12582920 | tf_op jit(solution)/shard_map/ppermute | solution.py:15
  324.2 51.9 %collective-permute-start.5 = (f32[4,16,128,128]{3,2,1,0:T(8,128)S(1)}, f32[4,16,128,128]{3,2,1,0:T(8,128)S(1)}, u32[]{:S(2)}, u32[]{:S(2)}) collective-permute-start(f32[4,16,128,128]{3,2,1,0:T(8,128)S(1)} %get-tuple-element.146), channel_id=1, source_target_pairs={{0,1},{1,2},{2,3},{3,4},{4,5},{5,6},{6,7},{7,8},{8,9},{9,10},{10,1... | collective-permute-start | bytes 12582920 | tf_op jit(solution)/shard_map/ppermute | solution.py:15
where the time goes:
time: 435 us; the launch traced here: 433 us
  local copies, waits for them, and re-layouts  116 us (27%)
  matrix products  92.8 us (21%)
  other arithmetic  79.4 us (18%)
  waiting for transfers between devices  71.7 us (16%)
  blocking collectives  49.2 us (11%)
  starting transfers between devices  23.6 us (5%)
    scatter-add x8, other arithmetic, fine_row(): return (total.at[local_index].add(row_terms), None)  71.9 us
    ppermute x6, waiting for transfers between devices, passed_along(): return lax.ppermute(x, axis, pairs)  71.7 us
    all_to_all x1, blocking collectives, summed_on_arrival(): lax.all_to_all(tiles, axis, split_axis=0, concat_axis=0, tiled=True)  49.2 us
    transpose x8, local copies, waits for them, and re-layouts, fine_row(): jnp.einsum('qyx,qkyz->qkxz', own_tiles.astype(jnp.float32), chosen, preci...  42.9 us
    dot_general x8, matrix products, fine_row(): jnp.einsum('qyx,qkyz->qkxz', own_tiles.astype(jnp.float32), chosen, preci...  40.7 us
    dot_general x8, matrix products, fine_row(): spread = jnp.einsum('spxz,spw->wxz', products, placing, precision=highest)  25.8 us
    gather x8, local copies, waits for them, and re-layouts, fine_row(): fetched = band_tiles[local_row]  25.7 us
    ppermute x6, starting transfers between devices, passed_along(): return lax.ppermute(x, axis, pairs)  23.6 us
  transfers between devices with their start and end apart: 6, of which 4 were waited for; matrix products, arithmetic and copies ran while one was open for 2% of the time, Pallas kernels for 0%

commit v1 on v0

v1 whole, which is shorter than its diff:
```python
import functools

import jax
import jax.numpy as jnp
from jax import lax
from jax.experimental import pallas as pl
from jax.experimental.pallas import tpu as pltpu
from jax.sharding import PartitionSpec as P


T = 128
F = 8
C = 4
S = 7
KP = 4
KC = 16
G = 4
KG = KC // G
NW = 7 * C
HC = 2
ROWS = HC * KG * T
SCALES = 16
PACK = ROWS + SCALES
LEVELS = 32760.0


def code(x, scratch, row):
    top = jnp.maximum(jnp.max(jnp.abs(x), axis=0, keepdims=True), 1e-37)
    exponent = jnp.floor(jnp.log2(top)) + 1.0
    scratch[pl.ds(row, 1), :] = exponent
    return jnp.round(x * (jnp.exp2(-exponent) * LEVELS)).astype(jnp.int32).astype(jnp.int16)


def widen(x):
    return x.astype(jnp.int32).astype(jnp.float32)


def products_kernel(
    part, pidx, wcol, first, lrow, sidx, odd, a_hbm, l_hbm, o_hbm, r_hbm, x_hbm, y_hbm, pt_hbm,
    *refs,
):
    if part == "outer":
        out0, out1, a_v, p_v, pt_v, acc, sp, tot, ex, sem = refs
    else:
        inner, own, a_v, p_v, pt_v, acc, sp, tot, ex, sem = refs
    copies = [pltpu.make_async_copy(a_hbm, a_v, sem.at[0])]
    for n, ref in enumerate((l_hbm, o_hbm, r_hbm, x_hbm, y_hbm)):
        copies.append(pltpu.make_async_copy(ref, p_v.at[n], sem.at[n + 1]))
    copies.append(pltpu.make_async_copy(pt_hbm, pt_v, sem.at[6]))
    for c in copies:
        c.start()
    nc = C if part == "outer" else 2 * C
    if part == "outer":
        base = odd[0] * (2 * C)
    else:
        base = (1 - odd[0]) * C

    def zero(c, _):
        tot[c] = jnp.zeros((KC, T, T), jnp.float32)
        return 0

    lax.fori_loop(0, nc, zero, 0)
    sp[NW] = jnp.zeros((2 * T, T), jnp.bfloat16)
    for c in copies:
        c.wait()

    def row(i, _):
        for s in range(S):
            a = a_v[i, s]
            j = pidx[i, s]
            blk, r = j // F, j % F
            for h in range(KP // 2):
                rhs = jnp.concatenate([p_v[blk, r, 2 * h], p_v[blk, r, 2 * h + 1]], axis=1)
                prod = jnp.dot(a, rhs, preferred_element_type=jnp.float32)
                for e in range(2):
                    m = s * KP + 2 * h + e
                    w = wcol[i, m]
                    old = jnp.where(first[i, m] == 1, 0.0, acc[w])
                    acc[w] = old + prod[:, e * T : (e + 1) * T]

        def split(w, _):
            x = acc[w]
            hi = x.astype(jnp.bfloat16)
            sp[w, 0:T, :] = hi
            sp[w, T : 2 * T, :] = (x - hi.astype(jnp.float32)).astype(jnp.bfloat16)
            return 0

        lax.fori_loop(0, NW, split, 0, unroll=4)
        for q in range(KP):
            c = lrow[i, q] - base

            @pl.when((c >= 0) & (c < nc))
            def _():
                pt = pt_v[i, q]
                lhs = jnp.concatenate([pt, pt], axis=1)
                for kk in range(KC // 2):
                    s0 = sidx[i * KP + q, 2 * kk]
                    s1 = sidx[i * KP + q, 2 * kk + 1]
                    rhs = jnp.concatenate([sp[s0], sp[s1]], axis=1)
                    prod = jnp.dot(lhs, rhs, preferred_element_type=jnp.float32)
                    tot[c, 2 * kk] += prod[:, :T]
                    tot[c, 2 * kk + 1] += prod[:, T:]

        return 0

    lax.fori_loop(0, F, row, 0)

    if part == "outer":
        start = 0
        dests = (out0, out1)
    else:
        start = odd[0] * 0 + (1 - odd[0]) * C
        dests = (inner.at[0], inner.at[1])
    for h in range(2):
        def group(g, _):
            for c in range(HC):
                for k in range(KG):
                    t = c * KG + k
                    dests[h][g, t * T : (t + 1) * T, :] = code(
                        tot[start + h * HC + c, g * KG + k], ex, t
                    )
            dests[h][g, ROWS:PACK, :] = ex[...].astype(jnp.int32).astype(jnp.int16)
            return 0

        lax.fori_loop(0, G, group, 0)
    if part == "rest":
        mine = odd[0] * C
        for c in range(C):
            own[c] = tot[mine + c]


def sum_kernel(own, inner, outer, out, ex_i, ex_o, ex):
    ex_i[...] = jnp.exp2(widen(inner[0, 0, ROWS:PACK, :])) * (1.0 / LEVELS)
    ex_o[...] = jnp.exp2(widen(outer[0, ROWS:PACK, :])) * (1.0 / LEVELS)
    for c in range(HC):
        for k in range(KG):
            t = c * KG + k
            rows = slice(t * T, (t + 1) * T)
            x = own[c, k] + widen(inner[0, 0, rows, :]) * ex_i[t : t + 1, :]
            x = x + widen(outer[0, rows, :]) * ex_o[t : t + 1, :]
            out[0, rows, :] = code(x, ex, t)
    out[0, ROWS:PACK, :] = ex[...].astype(jnp.int32).astype(jnp.int16)


def final_kernel(r0, r1, out, ex):
    for h, r in enumerate((r0, r1)):
        for g in range(G):
            ex[g] = jnp.exp2(widen(r[g, ROWS:PACK, :])) * (1.0 / LEVELS)
        for c in range(HC):
            for k in range(KG):
                t = c * KG + k
                rows = slice(t * T, (t + 1) * T)
                x = widen(r[0, rows, :]) * ex[0, t : t + 1, :]
                for g in range(1, G):
                    x = x + widen(r[g, rows, :]) * ex[g, t : t + 1, :]
                out[h * HC + c, k] = x


def permuted(x, to):
    n = lax.axis_size("row")
    return lax.ppermute(x, "row", [(i, to(i) % n) for i in range(n)])


def tables(a_cols, p_cols, c_cols, b):
    j = a_cols[:, 0, :]
    odd = b % 2
    rel = j // F - b
    near = 1 - 2 * odd
    slot = jnp.where(rel == -2, 0, jnp.where(rel == 0, 1, jnp.where(rel == 2, 2, jnp.where(rel == near, 3, 4))))
    pidx = slot * F + j % F
    wcol = p_cols[j].reshape(F, S * KP) - (b - 3) * C
    m = jnp.arange(S * KP, dtype=jnp.int32)
    same = wcol[:, :, None] == wcol[:, None, :]
    first = 1 - jnp.any(same & (m[None, None, :] < m[None, :, None]), axis=2).astype(jnp.int32)
    own = lax.dynamic_slice_in_dim(p_cols, b * F, F, 0)
    lrow = own - (b - 1) * C
    want = c_cols[own] - (b - 3) * C
    filled = jnp.any(want[..., None] == wcol[:, None, None, :], axis=-1)
    sidx = jnp.where(filled, want, NW).reshape(F * KP, KC)
    return pidx, wcol, first, lrow, sidx, jnp.full((1,), odd, jnp.int32)


def products(part, tabs, arrays):
    smem = pl.BlockSpec(memory_space=pltpu.SMEM)
    anyspace = pl.BlockSpec(memory_space=pl.ANY)
    vmem = pl.BlockSpec(memory_space=pltpu.VMEM)
    if part == "outer":
        out_shape = [jax.ShapeDtypeStruct((G, PACK, T), jnp.int16)] * 2
        nc = C
    else:
        out_shape = [
            jax.ShapeDtypeStruct((2, G, PACK, T), jnp.int16),
            jax.ShapeDtypeStruct((C, KC, T, T), jnp.float32),
        ]
        nc = 2 * C
    return pl.pallas_call(
        functools.partial(products_kernel, part),
        out_shape=out_shape,
        in_specs=[smem] * 6 + [anyspace] * 7,
        out_specs=[vmem] * 2,
        scratch_shapes=[
            pltpu.VMEM((F, S, T, T), jnp.bfloat16),
            pltpu.VMEM((5, F, KP, T, T), jnp.bfloat16),
            pltpu.VMEM((F, KP, T, T), jnp.bfloat16),
            pltpu.VMEM((NW, T, T), jnp.float32),
            pltpu.VMEM((NW + 1, 2 * T, T), jnp.bfloat16),
            pltpu.VMEM((nc, KC, T, T), jnp.float32),
            pltpu.VMEM((SCALES, T), jnp.float32),
            pltpu.SemaphoreType.DMA((7,)),
        ],
        compiler_params=pltpu.CompilerParams(vmem_limit_bytes=48 * 1024 * 1024),
        cost_estimate=pl.CostEstimate(flops=3 * 10**9, bytes_accessed=10**7, transcendentals=0),
    )(*tabs, *arrays)


def summed(h, own, inner, outer):
    return pl.pallas_call(
        sum_kernel,
        name="summed",
        out_shape=jax.ShapeDtypeStruct((G, PACK, T), jnp.int16),
        grid=(G,),
        in_specs=[
            pl.BlockSpec((HC, KG, T, T), lambda g: (h, g, 0, 0)),
            pl.BlockSpec((1, 1, PACK, T), lambda g: (h, g, 0, 0)),
            pl.BlockSpec((1, PACK, T), lambda g: (g, 0, 0)),
        ],
        out_specs=pl.BlockSpec((1, PACK, T), lambda g: (g, 0, 0)),
        scratch_shapes=[pltpu.VMEM((SCALES, T), jnp.float32)] * 3,
        cost_estimate=pl.CostEstimate(flops=10**8, bytes_accessed=5 * 10**6, transcendentals=0),
    )(own, inner, outer)


def finished(r0, r1):
    return pl.pallas_call(
        final_kernel,
        name="finished",
        out_shape=jax.ShapeDtypeStruct((C, KG, T, T), jnp.float32),
        scratch_shapes=[pltpu.VMEM((G, SCALES, T), jnp.float32)],
        cost_estimate=pl.CostEstimate(flops=10**8, bytes_accessed=4 * 10**6, transcendentals=0),
    )(r0, r1)


def body(a_tiles, a_cols, p_tiles, p_cols, c_cols):
    b = lax.axis_index("row")
    a = a_tiles[:, 0]
    right = permuted(p_tiles, lambda i: i - 2)
    left = permuted(p_tiles, lambda i: i + 2)
    near = permuted(p_tiles, lambda i: i ^ 1)
    tabs = tables(a_cols, p_cols, c_cols, b)
    pt = jnp.swapaxes(p_tiles, 2, 3)
    left, right, tabs, pt = lax.optimization_barrier((left, right, tabs, pt))
    far = permuted(jnp.where(b % 2 == 0, right, left), lambda i: i ^ 1)
    arrays = (a, left, p_tiles, right, near, far, pt)
    out0, out1 = products("outer", tabs, arrays)
    out0, out1, tabs = lax.optimization_barrier((out0, out1, tabs))
    away = lambda i: i - 1 if i % 2 == 0 else i + 1
    got0 = permuted(out0, away)
    got1 = permuted(out1, away)
    inner, own = products("rest", tabs, arrays)
    got = permuted(inner, lambda i: i ^ 1)
    results = []
    for h, outer in enumerate((got0, got1)):
        x = summed(h, own, got, outer)
        results.append(lax.all_to_all(x, "grp", 0, 0, tiled=True))
    return finished(*results)


def solution(mesh):
    return jax.shard_map(
        body,
        mesh=mesh,
        in_specs=(
            P("row", "grp", None, None, None),
            P("row", "grp", None),
            P("row", None, None, None),
            P(),
            P(),
        ),
        out_specs=P("row", "grp", None, None),
        check_vma=False,
    )
```

time: 435 us -> 150 us (0.34)
  local copies, waits for them, and re-layouts: 116 us -> 8.31 us
  matrix products: 92.8 us -> 0 us
  other arithmetic: 79.4 us -> 2.93 us
  Pallas kernels: 0 us -> 45.8 us
  blocking collectives: 49.2 us -> 17.5 us
  waiting for transfers between devices: 71.7 us -> 41.7 us
  starting transfers between devices: 23.6 us -> 31.7 us
    dot_general x32 -> x0, matrix products: 92.8 us -> none  [the longest x8 40.7 us: fine_row(): jnp.einsum('qyx,qkyz->qkxz', own_tiles.astype(jnp.float32), chosen, preci...]
    scatter-add x8 -> x0, other arithmetic: 71.9 us -> none  [fine_row(): return (total.at[local_index].add(row_terms), None)]
    transpose x17 -> x0, local copies, waits for them, and re-layouts: 59.1 us -> none  [the longest x8 42.9 us: fine_row(): jnp.einsum('qyx,qkyz->qkxz', own_tiles.astype(jnp.float32), chosen, preci...]
    pallas_call x0 -> x5, Pallas kernels: none -> 45.8 us  [the longest x2 34 us: products(): pl.pallas_call(functools.partial(products_kernel, part), out_shape=out_sh...]
    ppermute x6 -> x7, waiting for transfers between devices: 71.7 us -> 32.4 us  [permuted(): return lax.ppermute(x, 'row', [(i, to(i) % n) for i in range(n)])]
    gather x24 -> x2, local copies, waits for them, and re-layouts: 34.6 us -> 2.21 us  [the longest x1 1.63 us: tables(): wcol = p_cols[j].reshape(F, S * KP) - (b - 3) * C]
    all_to_all x1, blocking collectives: 49.2 us -> 17.5 us  [body(): results.append(lax.all_to_all(x, 'grp', 0, 0, tiled=True))]
    all_to_all x0 -> x1, waiting for transfers between devices: none -> 9.28 us  [body(): results.append(lax.all_to_all(x, 'grp', 0, 0, tiled=True))]
  transfers between devices with their start and end apart: 6 -> 8, of which waited for: 4 -> 6; matrix products, arithmetic and copies ran while one was open for 2% -> 6% of each run, Pallas kernels for 0% -> 6%
where the time goes in v1:
time: 150 us; the launch traced here: 148 us
  Pallas kernels  45.8 us (31%)
  waiting for transfers between devices  41.7 us (28%)
  starting transfers between devices  31.7 us (21%)
  blocking collectives  17.5 us (12%)
  local copies, waits for them, and re-layouts  8.31 us (6%)
  other arithmetic  2.93 us (2%)
    pallas_call x2, Pallas kernels, products(): pl.pallas_call(functools.partial(products_kernel, part), out_shape=out_sh...  34 us
    ppermute x7, waiting for transfers between devices, permuted(): return lax.ppermute(x, 'row', [(i, to(i) % n) for i in range(n)])  32.4 us
    ppermute x7, starting transfers between devices, permuted(): return lax.ppermute(x, 'row', [(i, to(i) % n) for i in range(n)])  27.2 us
    all_to_all x1, blocking collectives, body(): results.append(lax.all_to_all(x, 'grp', 0, 0, tiled=True))  17.5 us
    all_to_all x1, waiting for transfers between devices, body(): results.append(lax.all_to_all(x, 'grp', 0, 0, tiled=True))  9.28 us
    pallas_call x2, Pallas kernels, summed(): pl.pallas_call(sum_kernel, name='summed', out_shape=jax.ShapeDtypeStruct(...  8.69 us
    unnamed x18, local copies, waits for them, and re-layouts  5.6 us
    all_to_all x1, starting transfers between devices, body(): results.append(lax.all_to_all(x, 'grp', 0, 0, tiled=True))  4.47 us
  transfers between devices with their start and end apart: 8, of which 6 were waited for; matrix products, arithmetic and copies ran while one was open for 6% of the time, Pallas kernels for 6%

profile of v1, /device:TPU:6, one launch (start us, length us, event | category | flops | bytes accessed | tf_op | source)
XLA Modules:
  0.0 148.1 jit_solution(11649041246920709596)
XLA Ops:
  0.0 2.0 %collective-permute-start.2 = (bf16[8,4,128,128]{3,2,1,0:T(8,128)(2,1)}, bf16[8,4,128,128]{3,2,1,0:T(8,128)(2,1)}, u32[]{:S(2)}, u32[]{:S(2)}) collective-permute-start(bf16[8,4,128,128]{3,2,1,0:T(8,128)(2,1)} %o_hbm.3), channel_id=1, source_target_pairs={{0,1},{1,0},{2,3},{3,2},{4,5},{5,4},{6,7},{7,6},{8,9},{9,8},{10,11... | collective-permute-start | bytes 3145736 | tf_op jit(solution)/shard_map/ppermute | solution.py:161
  2.1 11.7 %collective-permute-start.1 = (bf16[8,4,128,128]{3,2,1,0:T(8,128)(2,1)}, bf16[8,4,128,128]{3,2,1,0:T(8,128)(2,1)S(1)}, u32[]{:S(2)}, u32[]{:S(2)}) collective-permute-start(bf16[8,4,128,128]{3,2,1,0:T(8,128)(2,1)} %o_hbm.3), channel_id=1, source_target_pairs={{0,126},{1,127},{2,0},{3,1},{4,2},{5,3},{6,4},{7,5},{8,6},{9,7},{1... | collective-permute-start | bytes 3145736 | tf_op jit(solution)/shard_map/ppermute | solution.py:161
  13.7 1.9 %collective-permute-start = (bf16[8,4,128,128]{3,2,1,0:T(8,128)(2,1)}, bf16[8,4,128,128]{3,2,1,0:T(8,128)(2,1)S(1)}, u32[]{:S(2)}, u32[]{:S(2)}) collective-permute-start(bf16[8,4,128,128]{3,2,1,0:T(8,128)(2,1)} %o_hbm.3), channel_id=1, source_target_pairs={{0,2},{1,3},{2,4},{3,5},{4,6},{5,7},{6,8},{7,9},{8,10},{9,11},{10,... | collective-permute-start | bytes 3145736 | tf_op jit(solution)/shard_map/ppermute | solution.py:161
  15.7 0.7 compare_select_fusion
  16.4 0.1 copy.19
  16.5 0.1 reshape.73
  16.6 1.7 %copy.20 = s32[1024,4]{1,0:T(8,128)} copy(s32[1024,4]{0,1:T(4,128)} %param.8) | data formatting | bytes 32768 | tf_op args[3]
  18.3 1.6 %gather_fusion = s32[56,4]{1,0:T(8,128)S(1)} fusion(s32[1024,4]{1,0:T(8,128)} %copy.20, s32[1024]{0:T(1024)S(1)} %pad_clamp_fusion.1), kind=kCustom, calls=%fused_computation | custom fusion | bytes 2016 | tf_op jit(solution)/shard_map/gather | solution.py:171
  19.9 0.1 sub.74.wcol
  20.0 0.7 compare_select_fusion.1
  20.7 0.1 reshape.81
  20.8 0.1 copy.21
  20.9 0.6 and_reduce_fusion
  21.5 0.0 copy-start.4
  21.5 0.0 copy-done.5
  21.5 0.1 copy.18
  21.6 0.0 copy-done
  21.6 1.3 copy.25
  22.9 0.0 copy-done.4
  22.9 0.1 copy.24
  23.1 0.1 copy.22
  23.2 0.6 gather_fusion.1
  23.7 0.7 compare_reduce_fusion
  24.5 12.6 %collective-permute-done.1.r_hbm = bf16[8,4,128,128]{3,2,1,0:T(8,128)(2,1)S(1)} collective-permute-done((bf16[8,4,128,128]{3,2,1,0:T(8,128)(2,1)}, bf16[8,4,128,128]{3,2,1,0:T(8,128)(2,1)S(1)}, u32[]{:S(2)}, u32[]{:S(2)}) %collective-permute-start.1) | collective-permute-done | bytes 1048608 | tf_op jit(solution)/shard_map/ppermute | solution.py:161
  37.1 6.1 %collective-permute-done.l_hbm = bf16[8,4,128,128]{3,2,1,0:T(8,128)(2,1)S(1)} collective-permute-done((bf16[8,4,128,128]{3,2,1,0:T(8,128)(2,1)}, bf16[8,4,128,128]{3,2,1,0:T(8,128)(2,1)S(1)}, u32[]{:S(2)}, u32[]{:S(2)}) %collective-permute-start) | collective-permute-done | bytes 1048608 | tf_op jit(solution)/shard_map/ppermute | solution.py:161
  43.2 0.1 broadcast_select_fusion
  43.3 1.9 %collective-permute-start.3 = (bf16[8,4,128,128]{3,2,1,0:T(8,128)(2,1)S(1)}, bf16[8,4,128,128]{3,2,1,0:T(8,128)(2,1)S(1)}, u32[]{:S(2)}, u32[]{:S(2)}) collective-permute-start(bf16[8,4,128,128]{3,2,1,0:T(8,128)(2,1)S(1)} %broadcast_select_fusion), channel_id=1, source_target_pairs={{0,1},{1,0},{2,3},{3,2},{4,5},{5,4},{6,7},{7,6},{8,9},{9,8},{10,11... | collective-permute-start | bytes 3145736 | tf_op jit(solution)/shard_map/ppermute | solution.py:161
  45.3 0.0 collective-permute-done.2.x_hbm
  45.3 2.6 %collective-permute-done.3.y_hbm = bf16[8,4,128,128]{3,2,1,0:T(8,128)(2,1)S(1)} collective-permute-done((bf16[8,4,128,128]{3,2,1,0:T(8,128)(2,1)S(1)}, bf16[8,4,128,128]{3,2,1,0:T(8,128)(2,1)S(1)}, u32[]{:S(2)}, u32[]{:S(2)}) %collective-permute-start.3) | collective-permute-done | bytes 1048608 | tf_op jit(solution)/shard_map/ppermute | solution.py:161
  47.9 15.0 %shard_map.55 = (s16[4,1040,128]{2,1,0:T(8,128)(2,1)}, s16[4,1040,128]{2,1,0:T(8,128)(2,1)}) custom-call(s32[8,7]{1,0:T(8,128)S(1)} %fusion.1.pidx, s32[8,28]{1,0:T(8,128)S(1)} %sub.74.wcol, s32[8,28]{1,0:T(8,128)S(1)} %convert_subtract_fusion.first, s32[8,4]{1,0:T(8,128)S(1)} %get-tuple-element.40.lrow, s32[32,16]{1,0:T(8,128)S(1)} %bitcast.27, ...), custom_call_target="tpu_custom_call" | custom-call | flops 3000000000 | bytes 10000000 | tf_op jit(solution)/shard_map/pallas_call | solution.py:196
  62.9 0.0 copy-start.6
  62.9 19.0 %shard_map.56 = (s16[2,4,1040,128]{3,2,1,0:T(8,128)(2,1)}, f32[4,16,128,128]{3,2,1,0:T(8,128)}) custom-call(s32[8,7]{1,0:T(8,128)S(1)} %fusion.1.pidx, s32[8,28]{1,0:T(8,128)S(1)} %sub.74.wcol, s32[8,28]{1,0:T(8,128)S(1)} %convert_subtract_fusion.first, s32[8,4]{1,0:T(8,128)S(1)} %get-tuple-element.40.lrow, s32[32,16]{1,0:T(8,128)S(1)} %bitcast.28, ...), custom_call_target="tpu_custom_call" | custom-call | flops 3000000000 | bytes 10000000 | tf_op jit(solution)/shard_map/pallas_call | solution.py:196
  81.9 2.0 %collective-permute-start.4 = (s16[2,4,1040,128]{3,2,1,0:T(8,128)(2,1)}, s16[2,4,1040,128]{3,2,1,0:T(8,128)(2,1)S(1)}, u32[]{:S(2)}, u32[]{:S(2)}) collective-permute-start(s16[2,4,1040,128]{3,2,1,0:T(8,128)(2,1)} %get-tuple-element.44), channel_id=1, source_target_pairs={{0,1},{1,0},{2,3},{3,2},{4,5},{5,4},{6,7},{7,6},{8,9},{9,8},{10,11... | collective-permute-start | bytes 6389768 | tf_op jit(solution)/shard_map/ppermute | solution.py:161
  84.0 0.0 copy-done.6
  84.0 1.9 %collective-permute-start.5 = (s16[4,1040,128]{2,1,0:T(8,128)(2,1)S(1)}, s16[4,1040,128]{2,1,0:T(8,128)(2,1)S(1)}, u32[]{:S(2)}, u32[]{:S(2)}) collective-permute-start(s16[4,1040,128]{2,1,0:T(8,128)(2,1)S(1)} %copy-done.6), channel_id=1, source_target_pairs={{0,127},{1,2},{2,1},{3,4},{4,3},{5,6},{6,5},{7,8},{8,7},{9,10},{10... | collective-permute-start | bytes 3194888 | tf_op jit(solution)/shard_map/ppermute | solution.py:161
  85.9 5.8 %collective-permute-start.6 = (s16[4,1040,128]{2,1,0:T(8,128)(2,1)}, s16[4,1040,128]{2,1,0:T(8,128)(2,1)}, u32[]{:S(2)}, u32[]{:S(2)}) collective-permute-start(s16[4,1040,128]{2,1,0:T(8,128)(2,1)} %get-tuple-element.46), channel_id=1, source_target_pairs={{0,127},{1,2},{2,1},{3,4},{4,3},{5,6},{6,5},{7,8},{8,7},{9,10},{10... | collective-permute-start | bytes 3194888 | tf_op jit(solution)/shard_map/ppermute | solution.py:161
  91.7 10.7 %collective-permute-done.5.outer = s16[4,1040,128]{2,1,0:T(8,128)(2,1)S(1)} collective-permute-done((s16[4,1040,128]{2,1,0:T(8,128)(2,1)S(1)}, s16[4,1040,128]{2,1,0:T(8,128)(2,1)S(1)}, u32[]{:S(2)}, u32[]{:S(2)}) %collective-permute-start.5) | collective-permute-done | bytes 1064992 | tf_op jit(solution)/shard_map/ppermute | solution.py:161
  102.4 0.0 collective-permute-done.4.inner
  102.4 1.0 copy-done.3
  103.4 1.3 copy-done.1
  104.7 4.3 %summed.2 = s16[4,1040,128]{2,1,0:T(8,128)(2,1)} custom-call(f32[4,16,128,128]{3,2,1,0:T(8,128)} %get-tuple-element.43.own, s16[2,4,1040,128]{3,2,1,0:T(8,128)(2,1)} %copy-done.1, s16[4,1040,128]{2,1,0:T(8,128)(2,1)} %copy-done.3), custom_call_target="tpu_custom_call" | custom-call | flops 100000000 | bytes 5000000 | tf_op jit(solution)/shard_map/summed/pallas_call | solution.py:217
  109.1 4.5 %all-to-all-start = ((s16[4,1040,128]{2,1,0:T(8,128)(2,1)}), s16[4,1040,128]{2,1,0:T(8,128)(2,1)S(1)}, u32[]{:S(2)}, u32[]{:S(2)}) async-start(s16[4,1040,128]{2,1,0:T(8,128)(2,1)} %summed.2), calls=%async_computation | async-start | bytes 2129920 | tf_op jit(solution)/shard_map/all_to_all | solution.py:264
  113.5 0.4 collective-permute-done.6.outer
  113.9 4.3 %summed.3 = s16[4,1040,128]{2,1,0:T(8,128)(2,1)} custom-call(f32[4,16,128,128]{3,2,1,0:T(8,128)} %get-tuple-element.43.own, s16[2,4,1040,128]{3,2,1,0:T(8,128)(2,1)} %copy-done.1, s16[4,1040,128]{2,1,0:T(8,128)(2,1)} %collective-permute-done.6.outer), custom_call_target="tpu_custom_call" | custom-call | flops 100000000 | bytes 5000000 | tf_op jit(solution)/shard_map/summed/pallas_call | solution.py:217
  118.3 9.3 %all-to-all-done.r0 = s16[4,1040,128]{2,1,0:T(8,128)(2,1)S(1)} async-done(((s16[4,1040,128]{2,1,0:T(8,128)(2,1)}), s16[4,1040,128]{2,1,0:T(8,128)(2,1)S(1)}, u32[]{:S(2)}, u32[]{:S(2)}) %all-to-all-start) | async-done | bytes 1064992 | tf_op jit(solution)/shard_map/all_to_all | solution.py:264
  127.5 17.5 %all_to_all.10.r1 = s16[4,1040,128]{2,1,0:T(8,128)(2,1)} all-to-all(s16[4,1040,128]{2,1,0:T(8,128)(2,1)} %summed.3), channel_id=1, replica_groups=mesh['grp'=4,'row'=128] {'grp'}, dimensions={0} | all-to-all | bytes 2129920 | tf_op jit(solution)/shard_map/all_to_all | solution.py:264
  145.0 0.0 copy-done.2
  145.0 3.0 %finished.1 = f32[4,4,128,128]{3,2,1,0:T(8,128)} custom-call(s16[4,1040,128]{2,1,0:T(8,128)(2,1)} %copy-done.2, s16[4,1040,128]{2,1,0:T(8,128)(2,1)} %all_to_all.10.r1), custom_call_target="tpu_custom_call" | custom-call | flops 100000000 | bytes 4000000 | tf_op jit(solution)/shard_map/finished/pallas_call | solution.py:234
  (13 shorter events, 0.1 us)
Async XLA Ops:
  0.0 21.6 %copy-start = (bf16[8,4,128,128]{3,2,1,0:T(8,128)(2,1)S(1)}, bf16[8,4,128,128]{3,2,1,0:T(8,128)(2,1)}, u32[]{:S(2)}) copy-start(bf16[8,4,128,128]{3,2,1,0:T(8,128)(2,1)} %o_hbm.3) | copy-start | bytes 3145732
  0.0 21.5 %copy-start.5 = (s32[8,1,7]{0,1,2:T(1,128)S(1)}, s32[8,1,7]{0,1,2:T(1,128)}, u32[]{:S(2)}) copy-start(s32[8,1,7]{0,1,2:T(1,128)} %param.6) | copy-start | bytes 676
  0.0 45.3 %collective-permute-start.2 = (bf16[8,4,128,128]{3,2,1,0:T(8,128)(2,1)}, bf16[8,4,128,128]{3,2,1,0:T(8,128)(2,1)}, u32[]{:S(2)}, u32[]{:S(2)}) collective-permute-start(bf16[8,4,128,128]{3,2,1,0:T(8,128)(2,1)} %o_hbm.3), channel_id=1, source_target_pairs={{0,1},{1,0},{2,3},{3,2},{4,5},{5,4},{6,7},{7,6},{8,9},{9,8},{10,11... | collective-permute-start | bytes 3145736 | tf_op jit(solution)/shard_map/ppermute | solution.py:161
  2.1 35.0 %collective-permute-start.1 = (bf16[8,4,128,128]{3,2,1,0:T(8,128)(2,1)}, bf16[8,4,128,128]{3,2,1,0:T(8,128)(2,1)S(1)}, u32[]{:S(2)}, u32[]{:S(2)}) collective-permute-start(bf16[8,4,128,128]{3,2,1,0:T(8,128)(2,1)} %o_hbm.3), channel_id=1, source_target_pairs={{0,126},{1,127},{2,0},{3,1},{4,2},{5,3},{6,4},{7,5},{8,6},{9,7},{1... | collective-permute-start | bytes 3145736 | tf_op jit(solution)/shard_map/ppermute | solution.py:161
  13.7 29.5 %collective-permute-start = (bf16[8,4,128,128]{3,2,1,0:T(8,128)(2,1)}, bf16[8,4,128,128]{3,2,1,0:T(8,128)(2,1)S(1)}, u32[]{:S(2)}, u32[]{:S(2)}) collective-permute-start(bf16[8,4,128,128]{3,2,1,0:T(8,128)(2,1)} %o_hbm.3), channel_id=1, source_target_pairs={{0,2},{1,3},{2,4},{3,5},{4,6},{5,7},{6,8},{7,9},{8,10},{9,11},{10,... | collective-permute-start | bytes 3145736 | tf_op jit(solution)/shard_map/ppermute | solution.py:161
  21.5 1.4 copy-start.4
  43.3 4.6 %collective-permute-start.3 = (bf16[8,4,128,128]{3,2,1,0:T(8,128)(2,1)S(1)}, bf16[8,4,128,128]{3,2,1,0:T(8,128)(2,1)S(1)}, u32[]{:S(2)}, u32[]{:S(2)}) collective-permute-start(bf16[8,4,128,128]{3,2,1,0:T(8,128)(2,1)S(1)} %broadcast_select_fusion), channel_id=1, source_target_pairs={{0,1},{1,0},{2,3},{3,2},{4,5},{5,4},{6,7},{7,6},{8,9},{9,8},{10,11... | collective-permute-start | bytes 3145736 | tf_op jit(solution)/shard_map/ppermute | solution.py:161
  62.9 21.1 %copy-start.6 = (s16[4,1040,128]{2,1,0:T(8,128)(2,1)S(1)}, s16[4,1040,128]{2,1,0:T(8,128)(2,1)}, u32[]{:S(2)}) copy-start(s16[4,1040,128]{2,1,0:T(8,128)(2,1)} %get-tuple-element.45) | copy-start | bytes 3194884
  81.9 20.4 %collective-permute-start.4 = (s16[2,4,1040,128]{3,2,1,0:T(8,128)(2,1)}, s16[2,4,1040,128]{3,2,1,0:T(8,128)(2,1)S(1)}, u32[]{:S(2)}, u32[]{:S(2)}) collective-permute-start(s16[2,4,1040,128]{3,2,1,0:T(8,128)(2,1)} %get-tuple-element.44), channel_id=1, source_target_pairs={{0,1},{1,0},{2,3},{3,2},{4,5},{5,4},{6,7},{7,6},{8,9},{9,8},{10,11... | collective-permute-start | bytes 6389768 | tf_op jit(solution)/shard_map/ppermute | solution.py:161
  84.0 18.4 %collective-permute-start.5 = (s16[4,1040,128]{2,1,0:T(8,128)(2,1)S(1)}, s16[4,1040,128]{2,1,0:T(8,128)(2,1)S(1)}, u32[]{:S(2)}, u32[]{:S(2)}) collective-permute-start(s16[4,1040,128]{2,1,0:T(8,128)(2,1)S(1)} %copy-done.6), channel_id=1, source_target_pairs={{0,127},{1,2},{2,1},{3,4},{4,3},{5,6},{6,5},{7,8},{8,7},{9,10},{10... | collective-permute-start | bytes 3194888 | tf_op jit(solution)/shard_map/ppermute | solution.py:161
  85.9 28.0 %collective-permute-start.6 = (s16[4,1040,128]{2,1,0:T(8,128)(2,1)}, s16[4,1040,128]{2,1,0:T(8,128)(2,1)}, u32[]{:S(2)}, u32[]{:S(2)}) collective-permute-start(s16[4,1040,128]{2,1,0:T(8,128)(2,1)} %get-tuple-element.46), channel_id=1, source_target_pairs={{0,127},{1,2},{2,1},{3,4},{4,3},{5,6},{6,5},{7,8},{8,7},{9,10},{10... | collective-permute-start | bytes 3194888 | tf_op jit(solution)/shard_map/ppermute | solution.py:161
  102.4 1.0 copy-start.3
  103.4 1.4 copy-start.1
  109.1 18.5 %all-to-all-start = ((s16[4,1040,128]{2,1,0:T(8,128)(2,1)}), s16[4,1040,128]{2,1,0:T(8,128)(2,1)S(1)}, u32[]{:S(2)}, u32[]{:S(2)}) async-start(s16[4,1040,128]{2,1,0:T(8,128)(2,1)} %summed.2), calls=%async_computation | async-start | bytes 2129920 | tf_op jit(solution)/shard_map/all_to_all | solution.py:264
  127.5 17.5 %copy-start.2 = (s16[4,1040,128]{2,1,0:T(8,128)(2,1)}, s16[4,1040,128]{2,1,0:T(8,128)(2,1)S(1)}, u32[]{:S(2)}) copy-start(s16[4,1040,128]{2,1,0:T(8,128)(2,1)S(1)} %all-to-all-done.r0) | copy-start | bytes 3194884

commit v2 on v0

v2 whole, which is shorter than its diff:
```python
import functools

import jax
import jax.numpy as jnp
from jax import lax
from jax.experimental import pallas as pl
from jax.experimental.pallas import tpu as pltpu
from jax.sharding import PartitionSpec as P


T = 128
F = 8
C = 4
S = 7
KP = 4
KC = 16
G = 4
KG = KC // G
N = S * KP
U = 4
NE = 72
SPARE = F * N
ZERO = SPARE + 1
NS = ZERO + 1
HC = 2
TC = HC * KG
ROWS = TC * T
SCALES = 16
PACK = ROWS + SCALES
LEVELS = 32760.0
MB = 1 << 20

SMEM = pl.BlockSpec(memory_space=pltpu.SMEM)
VMEM = pl.BlockSpec(memory_space=pltpu.VMEM)


def near_memory(x):
    return pltpu.with_memory_space_constraint(x, pltpu.VMEM)


def code(x, scratch, row):
    top = jnp.maximum(jnp.max(jnp.abs(x), axis=0, keepdims=True), 1e-37)
    exponent = jnp.floor(jnp.log2(top)) + 1.0
    scratch[pl.ds(row, 1), :] = exponent
    return jnp.round(x * (jnp.exp2(-exponent) * LEVELS)).astype(jnp.int32).astype(jnp.int16)


def widen(x):
    return x.astype(jnp.int32).astype(jnp.float32)


def params(mib):
    return pltpu.CompilerParams(vmem_limit_bytes=mib * MB)


def cost(flops):
    return pl.CostEstimate(flops=flops, bytes_accessed=10**6, transcendentals=0)


def tables(a_cols, p_cols, c_cols, b):
    i32 = jnp.int32
    j = a_cols.reshape(F * S)
    odd = b % 2
    rel = j // F - b
    near = 1 - 2 * odd
    seg = jnp.where(rel == 0, 0, jnp.where(rel == near, 1, jnp.where(rel == -2, 2, jnp.where(rel == 2, 3, 4))))
    e = jnp.arange(F * S, dtype=i32)
    same = seg[:, None] == seg[None, :]
    before = jnp.sum((same & (e[None, :] < e[:, None])).astype(i32), axis=1)
    count = jnp.sum((seg[None, :] == jnp.arange(5, dtype=i32)[:, None]).astype(i32), axis=1)
    steps = (count + U - 1) // U
    five = jnp.arange(6, dtype=i32)
    start = jnp.sum(jnp.where(five[None, :5] < five[:, None], steps[None, :], 0), axis=1)
    pos = jnp.sum(jnp.where(seg[:, None] == five[None, :5], start[None, :5], 0), axis=1) * U + before
    band0 = jnp.clip((b - 2) * F, 0, p_cols.shape[0] - 5 * F)
    band = lax.dynamic_slice_in_dim(p_cols, band0, 5 * F, 0)
    hit = (j - band0)[:, None] == jnp.arange(5 * F, dtype=i32)[None, :]
    wcol = jnp.sum(jnp.where(hit[:, :, None], band[None], 0), axis=1) - (b - 3) * C
    w = wcol.reshape(F, N)
    key = (pos[:, None] * KP + jnp.arange(KP, dtype=i32)[None, :]).reshape(F, N)
    dup = (w[:, :, None] == w[:, None, :]) & (key[:, None, :] < key[:, :, None])
    first = 1 - jnp.any(dup, axis=2).astype(i32)
    rank = jnp.sum(jnp.where(w[:, None, :] < w[:, :, None], first[:, None, :], 0), axis=2)
    many = jnp.sum(first, axis=1)
    rows = jnp.arange(F, dtype=i32)
    base = jnp.sum(jnp.where(rows[None, :] < rows[:, None], many[None, :], 0), axis=1)
    slot = (base[:, None] + rank).reshape(F * S, KP)
    place = pos[None, :] == jnp.arange(NE, dtype=i32)[:, None]
    taken = jnp.any(place, axis=1)

    def listed(x, empty):
        return jnp.where(taken[:, None], jnp.sum(jnp.where(place[:, :, None], x[None], 0), axis=1), empty)

    head = listed(jnp.stack([e, j % F], axis=1), 0)
    slots = listed(slot, SPARE)
    firsts = listed(first.reshape(F * S, KP), 1)
    entries = jnp.concatenate([head, slots, firsts], axis=1)

    own = lax.dynamic_slice_in_dim(p_cols, b * F, F, 0)
    row0 = jnp.clip((b - 1) * C, 0, c_cols.shape[0] - 3 * C)
    crows = lax.dynamic_slice_in_dim(c_cols, row0, 3 * C, 0)
    chit = (own.reshape(F * KP) - row0)[:, None] == jnp.arange(3 * C, dtype=i32)[None, :]
    want = jnp.sum(jnp.where(chit[:, :, None], crows[None], 0), axis=1) - (b - 3) * C
    want = want.reshape(F, KP * KC)
    filled = jnp.any(want[:, :, None] == w[:, None, :], axis=2)
    below = jnp.sum(jnp.where(w[:, None, :] < want[:, :, None], first[:, None, :], 0), axis=2)
    sidx = jnp.where(filled, base[:, None] + below, ZERO).reshape(F * KP, KC)

    local = own.reshape(F * KP) - (b - 1) * C
    left_first = local // C
    kind = jnp.where(left_first == 1, 2, jnp.where((left_first == 0) == (odd == 0), 0, 1))
    crow = kind * C + local % C
    pr = jnp.arange(F * KP, dtype=i32)
    ahead = (crow[None, :] < crow[:, None]) | ((crow[None, :] == crow[:, None]) & (pr[None, :] < pr[:, None]))
    ppos = jnp.sum(ahead.astype(i32), axis=1)
    cs = jnp.arange(16, dtype=i32)
    cstart = jnp.sum((crow[None, :] < cs[:, None]).astype(i32), axis=1)
    plist = jnp.sum(jnp.where(ppos[None, :] == pr[:, None], pr[None, :], 0), axis=1)
    small = jnp.concatenate([start, jnp.sum(many)[None], odd.reshape(1).astype(i32), cstart, plist])
    return entries, small, sidx


CSTART, PLIST, TOTAL, ODD = 8, 24, 6, 7


def entry_loop(seg, small, entries, a, p, acc):
    def step(t, _):
        for u in range(U):
            r = t * U + u
            j = entries[r, 1]
            rhs = jnp.concatenate([p[j, k] for k in range(KP)], axis=1)
            prod = jnp.dot(a[entries[r, 0]], rhs, preferred_element_type=jnp.float32)
            for k in range(KP):
                slot = entries[r, 2 + k]
                old = jnp.where(entries[r, 2 + KP + k] == 1, 0.0, acc[slot])
                acc[slot] = old + prod[:, k * T : (k + 1) * T]
        return 0

    lax.fori_loop(small[seg], small[seg + 1], step, 0)


def early_kernel(segs, small, entries, a, p0, p1, *refs):
    acc = refs[-1]
    entry_loop(segs[0], small, entries, a, p0, acc)
    entry_loop(segs[1], small, entries, a, p1, acc)


def last_kernel(small, entries, a, p, acc_in, acc, sp):
    entry_loop(4, small, entries, a, p, acc)
    sp[ZERO] = jnp.zeros((2 * T, T), jnp.bfloat16)

    def split(t, _):
        for u in range(4):
            n = t * 4 + u
            x = acc[n]
            hi = x.astype(jnp.bfloat16)
            sp[n, 0:T, :] = hi
            sp[n, T : 2 * T, :] = (x - hi.astype(jnp.float32)).astype(jnp.bfloat16)
        return 0

    lax.fori_loop(0, (small[TOTAL] + 3) // 4, split, 0)


ACC = pltpu.VMEM((NS, T, T), jnp.float32)


def early(segs, tabs, a, p0, p1, acc=None):
    entries, small, _ = tabs
    args = [small, entries, near_memory(a), near_memory(p0), near_memory(p1)]
    alias = {}
    if acc is not None:
        args.append(near_memory(acc))
        alias = {5: 0}
    return pl.pallas_call(
        functools.partial(early_kernel, segs),
        out_shape=ACC,
        in_specs=[SMEM] * 2 + [VMEM] * (len(args) - 2),
        out_specs=VMEM,
        input_output_aliases=alias,
        compiler_params=params(4),
        cost_estimate=cost(2 * 10**7),
    )(*args)


def last(tabs, a, p, acc):
    entries, small, _ = tabs
    return pl.pallas_call(
        last_kernel,
        name="last",
        out_shape=[ACC, pltpu.VMEM((NS, 2 * T, T), jnp.bfloat16)],
        in_specs=[SMEM] * 2 + [VMEM] * 3,
        out_specs=[VMEM] * 2,
        input_output_aliases={4: 0},
        compiler_params=params(4),
        cost_estimate=cost(2 * 10**7),
    )(small, entries, near_memory(a), near_memory(p), near_memory(acc))[1]


def coarse_kernel(rows, small, sidx, sp, pt, *refs):
    outs, ex = refs[:-1], refs[-1]

    def body(*accs):
        for acc in accs:
            pltpu.matmul_pop(acc)
        for c, (kind, dest, at, *half) in rows:
            out = outs[dest].at[half[0]] if half else outs[dest]
            e0 = half[0] * G * SCALES if half else 0

            def pair(r, _):
                pr = small[PLIST + r]
                tile = pt[pr]
                lhs = jnp.concatenate([tile, tile], axis=1)
                for n in range(KC // 2):
                    rhs = jnp.concatenate([sp[sidx[pr, 2 * n]], sp[sidx[pr, 2 * n + 1]]], axis=1)
                    pltpu.matmul_push_rhs(rhs, staging_register=(n // 2) % 2, mxu_index=n % 2)
                    pltpu.matmul_acc_lhs(accs[n], lhs, load_staged_rhs=(n // 2) % 2)
                return 0

            lax.fori_loop(small[CSTART + c], small[CSTART + c + 1], pair, 0)
            for n in range(KC // 2):
                x = pltpu.matmul_pop(accs[n])
                for h in range(2):
                    k = 2 * n + h
                    y = x[:, h * T : (h + 1) * T]
                    if kind == "plain":
                        out[at, k] = y
                    else:
                        g, t = k // KG, at * KG + k % KG
                        out[g, t * T : (t + 1) * T, :] = code(y, ex, e0 + g * SCALES + t)
            if kind == "code" and at == HC - 1:
                for g in range(G):
                    r0 = e0 + g * SCALES
                    out[g, ROWS:PACK, :] = ex[r0 : r0 + SCALES, :].astype(jnp.int32).astype(jnp.int16)

    pl.run_scoped(body, *[pltpu.ACC(n % 2)((T, 2 * T), jnp.float32) for n in range(KC // 2)])


def coarse(rows, out_shape, tabs, sp, pt):
    _, small, sidx = tabs
    return pl.pallas_call(
        functools.partial(coarse_kernel, rows),
        out_shape=out_shape,
        in_specs=[SMEM] * 2 + [VMEM] * 2,
        out_specs=[VMEM] * len(out_shape),
        scratch_shapes=[pltpu.VMEM((2 * G * SCALES, T), jnp.float32)],
        compiler_params=params(4),
        cost_estimate=cost(2 * 10**7),
    )(small, sidx, near_memory(sp), near_memory(pt))


CHUNK = pltpu.VMEM((G, PACK, T), jnp.int16)


def outer_chunk(h, tabs, sp, pt):
    rows = [(HC * h + c, ("code", 0, c)) for c in range(HC)]
    return coarse(rows, [CHUNK], tabs, sp, pt)[0]


def inner_chunks(tabs, sp, pt):
    rows = [(C + HC * h + c, ("code", 0, c, h)) for h in range(2) for c in range(HC)]
    shape = pltpu.VMEM((2, G, PACK, T), jnp.int16)
    return coarse(rows, [shape], tabs, sp, pt)[0]


def own_rows(tabs, sp, pt):
    rows = [(2 * C + c, ("plain", 0, c)) for c in range(C)]
    return coarse(rows, [pltpu.VMEM((C, KC, T, T), jnp.float32)], tabs, sp, pt)[0]


def pick_kernel(small, left, right, out):
    @pl.when(small[ODD] == 0)
    def _():
        out[...] = right[...]

    @pl.when(small[ODD] == 1)
    def _():
        out[...] = left[...]


def picked(tabs, left, right):
    return pl.pallas_call(
        pick_kernel,
        name="picked",
        out_shape=pltpu.VMEM(left.shape, left.dtype),
        in_specs=[SMEM] + [VMEM] * 2,
        out_specs=VMEM,
        compiler_params=params(4),
        cost_estimate=cost(10**6),
    )(tabs[1], near_memory(left), near_memory(right))


def sum_kernel(h, group, own, inner, outer, mine, *refs):
    sends, (ex_i, ex_o, ex) = refs[:3], refs[3:]
    for step in range(G):
        g = lax.rem(group[0] + step, G)
        ex_i[...] = jnp.exp2(widen(inner[h, g, ROWS:PACK, :])) * (1.0 / LEVELS)
        ex_o[...] = jnp.exp2(widen(outer[g, ROWS:PACK, :])) * (1.0 / LEVELS)
        for c in range(HC):
            for k in range(KG):
                t = c * KG + k
                rows = slice(t * T, (t + 1) * T)
                x = own[h * HC + c, g * KG + k] + widen(inner[h, g, rows, :]) * ex_i[t : t + 1, :]
                x = x + widen(outer[g, rows, :]) * ex_o[t : t + 1, :]
                if step == 0:
                    mine[c, k] = x
                else:
                    sends[step - 1][rows, :] = code(x, ex, t)
        if step:
            sends[step - 1][ROWS:PACK, :] = ex[...].astype(jnp.int32).astype(jnp.int16)


def summed(h, group, own, inner, outer):
    piece = pltpu.VMEM((PACK, T), jnp.int16)
    return pl.pallas_call(
        functools.partial(sum_kernel, h),
        out_shape=[pltpu.VMEM((HC, KG, T, T), jnp.float32)] + [piece] * 3,
        in_specs=[SMEM] + [VMEM] * 3,
        out_specs=[VMEM] * 4,
        scratch_shapes=[pltpu.VMEM((SCALES, T), jnp.float32)] * 3,
        compiler_params=params(4),
        cost_estimate=cost(10**7),
    )(group, near_memory(own), near_memory(inner), near_memory(outer))


def final_kernel(*refs):
    out, ex = refs[-2:]
    for h in range(2):
        mine, *got = refs[4 * h : 4 * h + 4]
        for n, r in enumerate(got):
            ex[n] = jnp.exp2(widen(r[ROWS:PACK, :])) * (1.0 / LEVELS)
        for c in range(HC):
            for k in range(KG):
                t = c * KG + k
                rows = slice(t * T, (t + 1) * T)
                x = mine[c, k]
                for n, r in enumerate(got):
                    x = x + widen(r[rows, :]) * ex[n, t : t + 1, :]
                out[h * HC + c, k] = x


def finished(parts):
    return pl.pallas_call(
        final_kernel,
        name="finished",
        out_shape=jax.ShapeDtypeStruct((C, KG, T, T), jnp.float32),
        in_specs=[VMEM] * 8,
        out_specs=VMEM,
        scratch_shapes=[pltpu.VMEM((G, SCALES, T), jnp.float32)],
        compiler_params=params(8),
        cost_estimate=cost(10**7),
    )(*[near_memory(x) for x in parts])


def permuted(x, axis, to):
    n = lax.axis_size(axis)
    return lax.ppermute(x, axis, [(i, to(i) % n) for i in range(n)])


def other(i):
    return i ^ 1


def away(i):
    return i - 1 if i % 2 == 0 else i + 1


def body(a_tiles, a_cols, p_tiles, p_cols, c_cols):
    b = lax.axis_index("row")
    group = lax.axis_index("grp").astype(jnp.int32).reshape(1)
    a = a_tiles.reshape(F * S, T, T)
    left = permuted(p_tiles, "row", lambda i: i + 2)
    right = permuted(p_tiles, "row", lambda i: i - 2)
    near = permuted(p_tiles, "row", other)
    tabs = tables(a_cols, p_cols, c_cols, b)
    pt = jnp.swapaxes(p_tiles, 2, 3).reshape(F * KP, T, T)
    tabs, pt, near, group = lax.optimization_barrier((tabs, pt, near, group))
    acc = early((0, 1), tabs, a, p_tiles, near)
    left, right, acc = lax.optimization_barrier((left, right, acc))
    far = permuted(picked(tabs, left, right), "row", other)
    acc = early((2, 3), tabs, a, left, right, acc)
    sp = last(tabs, a, far, acc)
    out0 = outer_chunk(0, tabs, sp, pt)
    got0 = permuted(out0, "row", away)
    out1 = outer_chunk(1, tabs, sp, pt)
    got1 = permuted(out1, "row", away)
    ins = inner_chunks(tabs, sp, pt)
    inner = permuted(ins, "row", other)
    own = own_rows(tabs, sp, pt)
    parts = []
    for h, outer in enumerate((got0, got1)):
        mine, *sends = summed(h, group, own, inner, outer)
        parts.append(mine)
        for n, x in enumerate(sends):
            parts.append(permuted(x, "grp", lambda i, n=n: i + n + 1))
    return finished(parts)


def solution(mesh):
    return jax.shard_map(
        body,
        mesh=mesh,
        in_specs=(
            P("row", "grp", None, None, None),
            P("row", "grp", None),
            P("row", None, None, None),
            P(),
            P(),
        ),
        out_specs=P("row", "grp", None, None),
        check_vma=False,
    )
```

time: 435 us -> 111 us (0.26)
  local copies, waits for them, and re-layouts: 116 us -> 7.57 us
  matrix products: 92.8 us -> 0 us
  other arithmetic: 79.4 us -> 4.82 us
  waiting for transfers between devices: 71.7 us -> 19.7 us
  blocking collectives: 49.2 us -> 0 us
  Pallas kernels: 0 us -> 27.4 us
  starting transfers between devices: 23.6 us -> 49.8 us
    dot_general x32 -> x0, matrix products: 92.8 us -> none  [the longest x8 40.7 us: fine_row(): jnp.einsum('qyx,qkyz->qkxz', own_tiles.astype(jnp.float32), chosen, preci...]
    scatter-add x8 -> x0, other arithmetic: 71.9 us -> none  [fine_row(): return (total.at[local_index].add(row_terms), None)]
    transpose x17 -> x1, local copies, waits for them, and re-layouts: 59.1 us -> 1.64 us  [body(): pt = jnp.swapaxes(p_tiles, 2, 3).reshape(F * KP, T, T)]
    ppermute x6 -> x13, waiting for transfers between devices: 71.7 us -> 19.7 us  [permuted(): return lax.ppermute(x, axis, [(i, to(i) % n) for i in range(n)])]
    all_to_all x1 -> x0, blocking collectives: 49.2 us -> none  [summed_on_arrival(): lax.all_to_all(tiles, axis, split_axis=0, concat_axis=0, tiled=True)]
    gather x24 -> x0, local copies, waits for them, and re-layouts: 34.6 us -> none  [the longest x8 25.7 us: fine_row(): fetched = band_tiles[local_row]]
    pallas_call x0 -> x11, Pallas kernels: none -> 27.4 us  [the longest x4 12.1 us: coarse(): pl.pallas_call(functools.partial(coarse_kernel, rows), out_shape=out_shap...]
    ppermute x6 -> x13, starting transfers between devices: 23.6 us -> 49.8 us  [permuted(): return lax.ppermute(x, axis, [(i, to(i) % n) for i in range(n)])]
  transfers between devices with their start and end apart: 6 -> 13, of which waited for: 4 -> 6; matrix products, arithmetic and copies ran while one was open for 2% -> 10% of each run, Pallas kernels for 0% -> 15%
where the time goes in v2:
time: 111 us; the launch traced here: 110 us
  starting transfers between devices  49.8 us (45%)
  Pallas kernels  27.4 us (25%)
  waiting for transfers between devices  19.7 us (18%)
  local copies, waits for them, and re-layouts  7.57 us (7%)
  other arithmetic  4.82 us (4%)
    ppermute x13, starting transfers between devices, permuted(): return lax.ppermute(x, axis, [(i, to(i) % n) for i in range(n)])  49.8 us
    ppermute x13, waiting for transfers between devices, permuted(): return lax.ppermute(x, axis, [(i, to(i) % n) for i in range(n)])  19.7 us
    pallas_call x4, Pallas kernels, coarse(): pl.pallas_call(functools.partial(coarse_kernel, rows), out_shape=out_shap...  12.1 us
    pallas_call x2, Pallas kernels, early(): pl.pallas_call(functools.partial(early_kernel, segs), out_shape=ACC, in_s...  6.7 us
    pallas_call x1, Pallas kernels, last(): pl.pallas_call(last_kernel, name='last', out_shape=[ACC, pltpu.VMEM((NS,...  3.94 us
  transfers between devices with their start and end apart: 13, of which 6 were waited for; matrix products, arithmetic and copies ran while one was open for 10% of the time, Pallas kernels for 15%

profile of v2, /device:TPU:6, one launch (start us, length us, event | category | flops | bytes accessed | tf_op | source)
XLA Modules:
  0.0 109.6 jit_solution(10753260406415228086)
XLA Ops:
  0.0 3.9 %collective-permute-start.1 = (bf16[8,4,128,128]{3,2,1,0:T(8,128)(2,1)}, bf16[8,4,128,128]{3,2,1,0:T(8,128)(2,1)}, u32[]{:S(2)}, u32[]{:S(2)}) collective-permute-start(bf16[8,4,128,128]{3,2,1,0:T(8,128)(2,1)} %p0.1), channel_id=1, source_target_pairs={{0,2},{1,3},{2,4},{3,5},{4,6},{5,7},{6,8},{7,9},{8,10},{9,11},{10,... | collective-permute-start | bytes 3145736 | tf_op jit(solution)/shard_map/ppermute | solution.py:356
  4.0 1.9 %collective-permute-start = (bf16[8,4,128,128]{3,2,1,0:T(8,128)(2,1)}, bf16[8,4,128,128]{3,2,1,0:T(8,128)(2,1)}, u32[]{:S(2)}, u32[]{:S(2)}) collective-permute-start(bf16[8,4,128,128]{3,2,1,0:T(8,128)(2,1)} %p0.1), channel_id=1, source_target_pairs={{0,1},{1,0},{2,3},{3,2},{4,5},{5,4},{6,7},{7,6},{8,9},{9,8},{10,11... | collective-permute-start | bytes 3145736 | tf_op jit(solution)/shard_map/ppermute | solution.py:356
  5.9 9.8 %collective-permute-start.2 = (bf16[8,4,128,128]{3,2,1,0:T(8,128)(2,1)}, bf16[8,4,128,128]{3,2,1,0:T(8,128)(2,1)}, u32[]{:S(2)}, u32[]{:S(2)}) collective-permute-start(bf16[8,4,128,128]{3,2,1,0:T(8,128)(2,1)} %p0.1), channel_id=1, source_target_pairs={{0,126},{1,127},{2,0},{3,1},{4,2},{5,3},{6,4},{7,5},{8,6},{9,7},{1... | collective-permute-start | bytes 3145736 | tf_op jit(solution)/shard_map/ppermute | solution.py:356
  15.7 0.8 copy.41
  16.6 0.2 convert_reduce_fusion
  16.8 0.1 convert_reduce_fusion.3
  16.9 0.8 constant_dynamic-slice_fusion.1
  17.7 0.8 dynamic-slice_subtract_fusion
  18.6 0.2 convert_reduce_fusion.1
  18.8 0.1 convert_reduce_fusion.2
  19.1 0.1 select_reduce_fusion.10
  20.8 0.6 and_reduce_fusion
  21.4 0.7 fusion.3
  22.1 0.1 select_reduce_fusion
  22.3 0.1 select_reduce_fusion.7
  22.5 0.1 select_reduce_fusion.8
  22.6 0.6 select_reduce_fusion.3
  24.2 1.6 %copy.57 = bf16[8,4,128,128]{3,2,1,0:T(8,128)(2,1)S(1)} copy(bf16[8,4,128,128]{2,3,1,0:T(8,128)(2,1)} %bitcast.23) | data formatting | bytes 2097152 | tf_op jit(solution)/shard_map/transpose | solution.py:375
  25.8 0.7 concatenate.7.small
  26.6 0.1 select_reduce_fusion.2
  27.0 1.2 %copy-done.2 = bf16[8,4,128,128]{3,2,1,0:T(8,128)(2,1)S(1)} copy-done((bf16[8,4,128,128]{3,2,1,0:T(8,128)(2,1)S(1)}, bf16[8,4,128,128]{3,2,1,0:T(8,128)(2,1)}, u32[]{:S(2)}) %copy-start.2) | copy-done | bytes 1048600
  28.2 3.2 %shard_map.55.refs_0_ = f32[226,128,128]{2,1,0:T(8,128)S(1)} custom-call(s32[56]{0:T(128)S(1)} %concatenate.7.small, s32[72,10]{1,0:T(8,128)S(1)} %copy.60.entries, bf16[56,128,128]{2,1,0:T(8,128)(2,1)S(1)} %bitcast.20, bf16[8,4,128,128]{3,2,1,0:T(8,128)(2,1)S(1)} %copy-done.2, bf16[8,4,128,128]{3,2,1,0:T(8,128)(2,1)} %collective-permute-done.p1), custom_call_target="tpu_custom_call" | custom-call | flops 20000000 | bytes 1000000 | tf_op jit(solution)/shard_map/pallas_call | solution.py:174
  31.4 3.8 %collective-permute-done.1.left.p0 = bf16[8,4,128,128]{3,2,1,0:T(8,128)(2,1)} collective-permute-done((bf16[8,4,128,128]{3,2,1,0:T(8,128)(2,1)}, bf16[8,4,128,128]{3,2,1,0:T(8,128)(2,1)}, u32[]{:S(2)}, u32[]{:S(2)}) %collective-permute-start.1) | collective-permute-done | bytes 1048608 | tf_op jit(solution)/shard_map/ppermute | solution.py:356
  35.3 3.8 %collective-permute-done.2.right.p1 = bf16[8,4,128,128]{3,2,1,0:T(8,128)(2,1)} collective-permute-done((bf16[8,4,128,128]{3,2,1,0:T(8,128)(2,1)}, bf16[8,4,128,128]{3,2,1,0:T(8,128)(2,1)}, u32[]{:S(2)}, u32[]{:S(2)}) %collective-permute-start.2) | collective-permute-done | bytes 1048608 | tf_op jit(solution)/shard_map/ppermute | solution.py:356
  39.0 1.6 %picked.1 = bf16[8,4,128,128]{3,2,1,0:T(8,128)(2,1)S(1)} custom-call(s32[56]{0:T(128)S(1)} %concatenate.7.small, bf16[8,4,128,128]{3,2,1,0:T(8,128)(2,1)} %collective-permute-done.1.left.p0, bf16[8,4,128,128]{3,2,1,0:T(8,128)(2,1)} %collective-permute-done.2.right.p1), custom_call_target="tpu_custom_call" | custom-call | flops 1000000 | bytes 1000000 | tf_op jit(solution)/shard_map/picked/pallas_call | solution.py:281
  40.7 1.9 %collective-permute-start.3 = (bf16[8,4,128,128]{3,2,1,0:T(8,128)(2,1)S(1)}, bf16[8,4,128,128]{3,2,1,0:T(8,128)(2,1)S(1)}, u32[]{:S(2)}, u32[]{:S(2)}) collective-permute-start(bf16[8,4,128,128]{3,2,1,0:T(8,128)(2,1)S(1)} %picked.1), channel_id=1, source_target_pairs={{0,1},{1,0},{2,3},{3,2},{4,5},{5,4},{6,7},{7,6},{8,9},{9,8},{10,11... | collective-permute-start | bytes 3145736 | tf_op jit(solution)/shard_map/ppermute | solution.py:356
  42.6 3.5 %shard_map.56.acc_in = f32[226,128,128]{2,1,0:T(8,128)S(1)} custom-call(s32[56]{0:T(128)S(1)} %concatenate.7.small, s32[72,10]{1,0:T(8,128)S(1)} %copy.60.entries, bf16[56,128,128]{2,1,0:T(8,128)(2,1)S(1)} %bitcast.21, bf16[8,4,128,128]{3,2,1,0:T(8,128)(2,1)} %collective-permute-done.1.left.p0, ...), custom_call_target="tpu_custom_call", output_to_operand_aliasing={{}: (5, {})} | custom-call | flops 20000000 | bytes 1000000 | tf_op jit(solution)/shard_map/pallas_call | solution.py:174
  46.1 3.9 %last.1 = (f32[226,128,128]{2,1,0:T(8,128)S(1)}, bf16[226,256,128]{2,1,0:T(8,128)(2,1)S(1)}) custom-call(s32[56]{0:T(128)S(1)} %concatenate.7.small, s32[72,10]{1,0:T(8,128)S(1)} %copy.60.entries, bf16[56,128,128]{2,1,0:T(8,128)(2,1)S(1)} %bitcast.22, bf16[8,4,128,128]{3,2,1,0:T(8,128)(2,1)S(1)} %collective-permute-done.3.p, ...), custom_call_target="tpu_custom_call", output_to_operand_aliasing={{0}: (4, {})} | custom-call | flops 20000000 | bytes 1000000 | tf_op jit(solution)/shard_map/last/pallas_call | solution.py:187
  50.1 3.8 %shard_map.58 = s16[2,4,1040,128]{3,2,1,0:T(8,128)(2,1)S(1)} custom-call(s32[56]{0:T(128)S(1)} %concatenate.7.small, s32[32,16]{1,0:T(8,128)S(1)} %add_select_fusion.sidx, bf16[226,256,128]{2,1,0:T(8,128)(2,1)S(1)} %get-tuple-element.31.sp, bf16[32,128,128]{2,1,0:T(8,128)(2,1)S(1)} %bitcast.16), custom_call_target="tpu_custom_call" | custom-call | flops 20000000 | bytes 1000000 | tf_op jit(solution)/shard_map/pallas_call | solution.py:240
  53.8 1.9 %collective-permute-start.4 = (s16[2,4,1040,128]{3,2,1,0:T(8,128)(2,1)S(1)}, s16[2,4,1040,128]{3,2,1,0:T(8,128)(2,1)S(1)}, u32[]{:S(2)}, u32[]{:S(2)}) collective-permute-start(s16[2,4,1040,128]{3,2,1,0:T(8,128)(2,1)S(1)} %shard_map.58), channel_id=1, source_target_pairs={{0,1},{1,0},{2,3},{3,2},{4,5},{5,4},{6,7},{7,6},{8,9},{9,8},{10,11... | collective-permute-start | bytes 6389768 | tf_op jit(solution)/shard_map/ppermute | solution.py:356
  55.8 2.9 %shard_map.61 = s16[4,1040,128]{2,1,0:T(8,128)(2,1)S(1)} custom-call(s32[56]{0:T(128)S(1)} %concatenate.7.small, s32[32,16]{1,0:T(8,128)S(1)} %add_select_fusion.sidx, bf16[226,256,128]{2,1,0:T(8,128)(2,1)S(1)} %get-tuple-element.31.sp, bf16[32,128,128]{2,1,0:T(8,128)(2,1)S(1)} %bitcast.17), custom_call_target="tpu_custom_call" | custom-call | flops 20000000 | bytes 1000000 | tf_op jit(solution)/shard_map/pallas_call | solution.py:240
  58.7 6.4 %collective-permute-start.9 = (s16[4,1040,128]{2,1,0:T(8,128)(2,1)S(1)}, s16[4,1040,128]{2,1,0:T(8,128)(2,1)S(1)}, u32[]{:S(2)}, u32[]{:S(2)}) collective-permute-start(s16[4,1040,128]{2,1,0:T(8,128)(2,1)S(1)} %shard_map.61), channel_id=1, source_target_pairs={{0,127},{1,2},{2,1},{3,4},{4,3},{5,6},{6,5},{7,8},{8,7},{9,10},{10... | collective-permute-start | bytes 3194888 | tf_op jit(solution)/shard_map/ppermute | solution.py:356
  65.1 2.1 %shard_map.59 = s16[4,1040,128]{2,1,0:T(8,128)(2,1)S(1)} custom-call(s32[56]{0:T(128)S(1)} %concatenate.7.small, s32[32,16]{1,0:T(8,128)S(1)} %add_select_fusion.sidx, bf16[226,256,128]{2,1,0:T(8,128)(2,1)S(1)} %get-tuple-element.31.sp, bf16[32,128,128]{2,1,0:T(8,128)(2,1)S(1)} %bitcast.18), custom_call_target="tpu_custom_call" | custom-call | flops 20000000 | bytes 1000000 | tf_op jit(solution)/shard_map/pallas_call | solution.py:240
  67.2 2.1 %collective-permute-start.5 = (s16[4,1040,128]{2,1,0:T(8,128)(2,1)S(1)}, s16[4,1040,128]{2,1,0:T(8,128)(2,1)S(1)}, u32[]{:S(2)}, u32[]{:S(2)}) collective-permute-start(s16[4,1040,128]{2,1,0:T(8,128)(2,1)S(1)} %shard_map.59), channel_id=1, source_target_pairs={{0,127},{1,2},{2,1},{3,4},{4,3},{5,6},{6,5},{7,8},{8,7},{9,10},{10... | collective-permute-start | bytes 3194888 | tf_op jit(solution)/shard_map/ppermute | solution.py:356
  69.3 3.3 %shard_map.57.own = f32[4,16,128,128]{3,2,1,0:T(8,128)S(1)} custom-call(s32[56]{0:T(128)S(1)} %concatenate.7.small, s32[32,16]{1,0:T(8,128)S(1)} %add_select_fusion.sidx, bf16[226,256,128]{2,1,0:T(8,128)(2,1)S(1)} %get-tuple-element.31.sp, bf16[32,128,128]{2,1,0:T(8,128)(2,1)S(1)} %bitcast.19), custom_call_target="tpu_custom_call" | custom-call | flops 20000000 | bytes 1000000 | tf_op jit(solution)/shard_map/pallas_call | solution.py:240
  72.6 5.1 %collective-permute-done.9.outer = s16[4,1040,128]{2,1,0:T(8,128)(2,1)S(1)} collective-permute-done((s16[4,1040,128]{2,1,0:T(8,128)(2,1)S(1)}, s16[4,1040,128]{2,1,0:T(8,128)(2,1)S(1)}, u32[]{:S(2)}, u32[]{:S(2)}) %collective-permute-start.9) | collective-permute-done | bytes 1064992 | tf_op jit(solution)/shard_map/ppermute | solution.py:356
  77.7 0.8 shard_map.62
  78.5 3.2 %collective-permute-start.10 = (s16[1040,128]{1,0:T(8,128)(2,1)S(1)}, s16[1040,128]{1,0:T(8,128)(2,1)S(1)}, u32[]{:S(2)}, u32[]{:S(2)}) collective-permute-start(s16[1040,128]{1,0:T(8,128)(2,1)S(1)} %get-tuple-element.38), channel_id=1, source_target_pairs={{0,128},{128,256},{256,384},{384,0},{1,129},{129,257},{257,385},{3... | collective-permute-start | bytes 798728 | tf_op jit(solution)/shard_map/ppermute | solution.py:356
  81.7 5.1 %collective-permute-start.11 = (s16[1040,128]{1,0:T(8,128)(2,1)S(1)}, s16[1040,128]{1,0:T(8,128)(2,1)S(1)}, u32[]{:S(2)}, u32[]{:S(2)}) collective-permute-start(s16[1040,128]{1,0:T(8,128)(2,1)S(1)} %get-tuple-element.39), channel_id=1, source_target_pairs={{0,256},{128,384},{256,0},{384,128},{1,257},{129,385},{257,1},{385... | collective-permute-start | bytes 798728 | tf_op jit(solution)/shard_map/ppermute | solution.py:356
  86.8 3.0 %collective-permute-start.12 = (s16[1040,128]{1,0:T(8,128)(2,1)S(1)}, s16[1040,128]{1,0:T(8,128)(2,1)S(1)}, u32[]{:S(2)}, u32[]{:S(2)}) collective-permute-start(s16[1040,128]{1,0:T(8,128)(2,1)S(1)} %get-tuple-element.40), channel_id=1, source_target_pairs={{0,384},{128,0},{256,128},{384,256},{1,385},{129,1},{257,129},{385... | collective-permute-start | bytes 798728 | tf_op jit(solution)/shard_map/ppermute | solution.py:356
  89.8 0.8 shard_map.60
  90.7 2.8 %collective-permute-start.6 = (s16[1040,128]{1,0:T(8,128)(2,1)S(1)}, s16[1040,128]{1,0:T(8,128)(2,1)S(1)}, u32[]{:S(2)}, u32[]{:S(2)}) collective-permute-start(s16[1040,128]{1,0:T(8,128)(2,1)S(1)} %get-tuple-element.34), channel_id=1, source_target_pairs={{0,128},{128,256},{256,384},{384,0},{1,129},{129,257},{257,385},{3... | collective-permute-start | bytes 798728 | tf_op jit(solution)/shard_map/ppermute | solution.py:356
  93.5 4.7 %collective-permute-start.7 = (s16[1040,128]{1,0:T(8,128)(2,1)S(1)}, s16[1040,128]{1,0:T(8,128)(2,1)S(1)}, u32[]{:S(2)}, u32[]{:S(2)}) collective-permute-start(s16[1040,128]{1,0:T(8,128)(2,1)S(1)} %get-tuple-element.35), channel_id=1, source_target_pairs={{0,256},{128,384},{256,0},{384,128},{1,257},{129,385},{257,1},{385... | collective-permute-start | bytes 798728 | tf_op jit(solution)/shard_map/ppermute | solution.py:356
  98.2 3.0 %collective-permute-start.8 = (s16[1040,128]{1,0:T(8,128)(2,1)S(1)}, s16[1040,128]{1,0:T(8,128)(2,1)S(1)}, u32[]{:S(2)}, u32[]{:S(2)}) collective-permute-start(s16[1040,128]{1,0:T(8,128)(2,1)S(1)} %get-tuple-element.36), channel_id=1, source_target_pairs={{0,384},{128,0},{256,128},{384,256},{1,385},{129,1},{257,129},{385... | collective-permute-start | bytes 798728 | tf_op jit(solution)/shard_map/ppermute | solution.py:356
  101.3 1.6 %collective-permute-done.6.refs_1_ = s16[1040,128]{1,0:T(8,128)(2,1)S(1)} collective-permute-done((s16[1040,128]{1,0:T(8,128)(2,1)S(1)}, s16[1040,128]{1,0:T(8,128)(2,1)S(1)}, u32[]{:S(2)}, u32[]{:S(2)}) %collective-permute-start.6) | collective-permute-done | bytes 266272 | tf_op jit(solution)/shard_map/ppermute | solution.py:356
  102.9 2.9 %collective-permute-done.7.refs_2_ = s16[1040,128]{1,0:T(8,128)(2,1)S(1)} collective-permute-done((s16[1040,128]{1,0:T(8,128)(2,1)S(1)}, s16[1040,128]{1,0:T(8,128)(2,1)S(1)}, u32[]{:S(2)}, u32[]{:S(2)}) %collective-permute-start.7) | collective-permute-done | bytes 266272 | tf_op jit(solution)/shard_map/ppermute | solution.py:356
  105.7 2.5 %collective-permute-done.8.refs_3_ = s16[1040,128]{1,0:T(8,128)(2,1)S(1)} collective-permute-done((s16[1040,128]{1,0:T(8,128)(2,1)S(1)}, s16[1040,128]{1,0:T(8,128)(2,1)S(1)}, u32[]{:S(2)}, u32[]{:S(2)}) %collective-permute-start.8) | collective-permute-done | bytes 266272 | tf_op jit(solution)/shard_map/ppermute | solution.py:356
  108.2 1.4 %finished.1 = f32[4,4,128,128]{3,2,1,0:T(8,128)} custom-call(f32[2,4,128,128]{3,2,1,0:T(8,128)S(1)} %get-tuple-element.33.refs_0_, s16[1040,128]{1,0:T(8,128)(2,1)S(1)} %collective-permute-done.6.refs_1_, s16[1040,128]{1,0:T(8,128)(2,1)S(1)} %collective-permute-done.7.refs_2_, s16[1040,128]{1,0:T(8,128)(2,1)S(1)} %collective-permute-done.8.refs_3_, ...), custom_call_target="tpu_custom_call" | custom-call | flops 10000000 | bytes 1000000 | tf_op jit(solution)/shard_map/finished/pallas_call | solution.py:342
  (71 shorter events, 3.5 us)
Async XLA Ops:
  0.0 19.7 %copy-start = (s32[512,16]{0,1:T(8,128)S(1)}, s32[512,16]{0,1:T(8,128)}, u32[]{:S(2)}) copy-start(s32[512,16]{0,1:T(8,128)} %param.9) | copy-start | bytes 98308
  0.0 27.0 %copy-start.1 = (bf16[8,1,7,128,128]{4,3,2,1,0:T(8,128)(2,1)S(1)}, bf16[8,1,7,128,128]{4,3,2,1,0:T(8,128)(2,1)}, u32[]{:S(2)}) copy-start(bf16[8,1,7,128,128]{4,3,2,1,0:T(8,128)(2,1)} %param.5) | copy-start | bytes 5505028
  0.0 35.3 %collective-permute-start.1 = (bf16[8,4,128,128]{3,2,1,0:T(8,128)(2,1)}, bf16[8,4,128,128]{3,2,1,0:T(8,128)(2,1)}, u32[]{:S(2)}, u32[]{:S(2)}) collective-permute-start(bf16[8,4,128,128]{3,2,1,0:T(8,128)(2,1)} %p0.1), channel_id=1, source_target_pairs={{0,2},{1,3},{2,4},{3,5},{4,6},{5,7},{6,8},{7,9},{8,10},{9,11},{10,... | collective-permute-start | bytes 3145736 | tf_op jit(solution)/shard_map/ppermute | solution.py:356
  4.0 22.9 %collective-permute-start = (bf16[8,4,128,128]{3,2,1,0:T(8,128)(2,1)}, bf16[8,4,128,128]{3,2,1,0:T(8,128)(2,1)}, u32[]{:S(2)}, u32[]{:S(2)}) collective-permute-start(bf16[8,4,128,128]{3,2,1,0:T(8,128)(2,1)} %p0.1), channel_id=1, source_target_pairs={{0,1},{1,0},{2,3},{3,2},{4,5},{5,4},{6,7},{7,6},{8,9},{9,8},{10,11... | collective-permute-start | bytes 3145736 | tf_op jit(solution)/shard_map/ppermute | solution.py:356
  5.9 33.1 %collective-permute-start.2 = (bf16[8,4,128,128]{3,2,1,0:T(8,128)(2,1)}, bf16[8,4,128,128]{3,2,1,0:T(8,128)(2,1)}, u32[]{:S(2)}, u32[]{:S(2)}) collective-permute-start(bf16[8,4,128,128]{3,2,1,0:T(8,128)(2,1)} %p0.1), channel_id=1, source_target_pairs={{0,126},{1,127},{2,0},{3,1},{4,2},{5,3},{6,4},{7,5},{8,6},{9,7},{1... | collective-permute-start | bytes 3145736 | tf_op jit(solution)/shard_map/ppermute | solution.py:356
  27.0 1.2 %copy-start.2 = (bf16[8,4,128,128]{3,2,1,0:T(8,128)(2,1)S(1)}, bf16[8,4,128,128]{3,2,1,0:T(8,128)(2,1)}, u32[]{:S(2)}) copy-start(bf16[8,4,128,128]{3,2,1,0:T(8,128)(2,1)} %p0.1) | copy-start | bytes 3145732
  40.7 5.5 %collective-permute-start.3 = (bf16[8,4,128,128]{3,2,1,0:T(8,128)(2,1)S(1)}, bf16[8,4,128,128]{3,2,1,0:T(8,128)(2,1)S(1)}, u32[]{:S(2)}, u32[]{:S(2)}) collective-permute-start(bf16[8,4,128,128]{3,2,1,0:T(8,128)(2,1)S(1)} %picked.1), channel_id=1, source_target_pairs={{0,1},{1,0},{2,3},{3,2},{4,5},{5,4},{6,7},{7,6},{8,9},{9,8},{10,11... | collective-permute-start | bytes 3145736 | tf_op jit(solution)/shard_map/ppermute | solution.py:356
  53.8 23.9 %collective-permute-start.4 = (s16[2,4,1040,128]{3,2,1,0:T(8,128)(2,1)S(1)}, s16[2,4,1040,128]{3,2,1,0:T(8,128)(2,1)S(1)}, u32[]{:S(2)}, u32[]{:S(2)}) collective-permute-start(s16[2,4,1040,128]{3,2,1,0:T(8,128)(2,1)S(1)} %shard_map.58), channel_id=1, source_target_pairs={{0,1},{1,0},{2,3},{3,2},{4,5},{5,4},{6,7},{7,6},{8,9},{9,8},{10,11... | collective-permute-start | bytes 6389768 | tf_op jit(solution)/shard_map/ppermute | solution.py:356
  58.7 19.0 %collective-permute-start.9 = (s16[4,1040,128]{2,1,0:T(8,128)(2,1)S(1)}, s16[4,1040,128]{2,1,0:T(8,128)(2,1)S(1)}, u32[]{:S(2)}, u32[]{:S(2)}) collective-permute-start(s16[4,1040,128]{2,1,0:T(8,128)(2,1)S(1)} %shard_map.61), channel_id=1, source_target_pairs={{0,127},{1,2},{2,1},{3,4},{4,3},{5,6},{6,5},{7,8},{8,7},{9,10},{10... | collective-permute-start | bytes 3194888 | tf_op jit(solution)/shard_map/ppermute | solution.py:356
  67.2 22.7 %collective-permute-start.5 = (s16[4,1040,128]{2,1,0:T(8,128)(2,1)S(1)}, s16[4,1040,128]{2,1,0:T(8,128)(2,1)S(1)}, u32[]{:S(2)}, u32[]{:S(2)}) collective-permute-start(s16[4,1040,128]{2,1,0:T(8,128)(2,1)S(1)} %shard_map.59), channel_id=1, source_target_pairs={{0,127},{1,2},{2,1},{3,4},{4,3},{5,6},{6,5},{7,8},{8,7},{9,10},{10... | collective-permute-start | bytes 3194888 | tf_op jit(solution)/shard_map/ppermute | solution.py:356
  78.5 19.7 %collective-permute-start.10 = (s16[1040,128]{1,0:T(8,128)(2,1)S(1)}, s16[1040,128]{1,0:T(8,128)(2,1)S(1)}, u32[]{:S(2)}, u32[]{:S(2)}) collective-permute-start(s16[1040,128]{1,0:T(8,128)(2,1)S(1)} %get-tuple-element.38), channel_id=1, source_target_pairs={{0,128},{128,256},{256,384},{384,0},{1,129},{129,257},{257,385},{3... | collective-permute-start | bytes 798728 | tf_op jit(solution)/shard_map/ppermute | solution.py:356
  81.7 19.5 %collective-permute-start.11 = (s16[1040,128]{1,0:T(8,128)(2,1)S(1)}, s16[1040,128]{1,0:T(8,128)(2,1)S(1)}, u32[]{:S(2)}, u32[]{:S(2)}) collective-permute-start(s16[1040,128]{1,0:T(8,128)(2,1)S(1)} %get-tuple-element.39), channel_id=1, source_target_pairs={{0,256},{128,384},{256,0},{384,128},{1,257},{129,385},{257,1},{385... | collective-permute-start | bytes 798728 | tf_op jit(solution)/shard_map/ppermute | solution.py:356
  86.8 14.5 %collective-permute-start.12 = (s16[1040,128]{1,0:T(8,128)(2,1)S(1)}, s16[1040,128]{1,0:T(8,128)(2,1)S(1)}, u32[]{:S(2)}, u32[]{:S(2)}) collective-permute-start(s16[1040,128]{1,0:T(8,128)(2,1)S(1)} %get-tuple-element.40), channel_id=1, source_target_pairs={{0,384},{128,0},{256,128},{384,256},{1,385},{129,1},{257,129},{385... | collective-permute-start | bytes 798728 | tf_op jit(solution)/shard_map/ppermute | solution.py:356
  90.7 12.2 %collective-permute-start.6 = (s16[1040,128]{1,0:T(8,128)(2,1)S(1)}, s16[1040,128]{1,0:T(8,128)(2,1)S(1)}, u32[]{:S(2)}, u32[]{:S(2)}) collective-permute-start(s16[1040,128]{1,0:T(8,128)(2,1)S(1)} %get-tuple-element.34), channel_id=1, source_target_pairs={{0,128},{128,256},{256,384},{384,0},{1,129},{129,257},{257,385},{3... | collective-permute-start | bytes 798728 | tf_op jit(solution)/shard_map/ppermute | solution.py:356
  93.5 12.2 %collective-permute-start.7 = (s16[1040,128]{1,0:T(8,128)(2,1)S(1)}, s16[1040,128]{1,0:T(8,128)(2,1)S(1)}, u32[]{:S(2)}, u32[]{:S(2)}) collective-permute-start(s16[1040,128]{1,0:T(8,128)(2,1)S(1)} %get-tuple-element.35), channel_id=1, source_target_pairs={{0,256},{128,384},{256,0},{384,128},{1,257},{129,385},{257,1},{385... | collective-permute-start | bytes 798728 | tf_op jit(solution)/shard_map/ppermute | solution.py:356
  98.2 10.0 %collective-permute-start.8 = (s16[1040,128]{1,0:T(8,128)(2,1)S(1)}, s16[1040,128]{1,0:T(8,128)(2,1)S(1)}, u32[]{:S(2)}, u32[]{:S(2)}) collective-permute-start(s16[1040,128]{1,0:T(8,128)(2,1)S(1)} %get-tuple-element.36), channel_id=1, source_target_pairs={{0,384},{128,0},{256,128},{384,256},{1,385},{129,1},{257,129},{385... | collective-permute-start | bytes 798728 | tf_op jit(solution)/shard_map/ppermute | solution.py:356

commit v3 on v0

v3 whole, which is shorter than its diff:
```python
import functools

import jax
import jax.numpy as jnp
from jax import lax
from jax.experimental import pallas as pl
from jax.experimental.pallas import tpu as pltpu
from jax.sharding import PartitionSpec as P


T = 128
F = 8
C = 4
S = 7
KP = 4
KC = 16
G = 4
KG = KC // G
KD = 2 * KG
NA = F * S
HC = 2
TC = HC * KG
ROWS = TC * T
SCALES = 16
PACK = ROWS + SCALES
LEVELS = 32760.0
MB = 1 << 20

NW = 7 * C
SPARE = F * NW
ZERO = SPARE + 1
NS = ZERO + 1

LISTS = 5
U = 4
FRONT = U
CAP = FRONT + 2 * NA + 2 * U
WORDS = 1 + KP
PAIRS, PLIST = 0, 16
SMALL = PLIST + 3 * C * F * KP

SMEM = pl.BlockSpec(memory_space=pltpu.SMEM)
VMEM = pl.BlockSpec(memory_space=pltpu.VMEM)
HBM = pl.BlockSpec(memory_space=pltpu.HBM)


def call(kernel, args, outs, scratch=(), alias={}, mib=4):
    spec = {"smem": SMEM, "vmem": VMEM, "hbm": HBM}
    put = {
        "smem": lambda x: pltpu.with_memory_space_constraint(x, pltpu.SMEM),
        "vmem": lambda x: pltpu.with_memory_space_constraint(x, pltpu.VMEM),
        "hbm": lambda x: pltpu.with_memory_space_constraint(x, pltpu.HBM),
    }
    return pl.pallas_call(
        kernel,
        out_shape=[x for _, x in outs],
        in_specs=[spec[where] for where, _ in args],
        out_specs=[spec[where] for where, _ in outs],
        scratch_shapes=scratch,
        input_output_aliases=alias,
        compiler_params=pltpu.CompilerParams(vmem_limit_bytes=mib * MB),
        cost_estimate=pl.CostEstimate(flops=2 * 10**7, bytes_accessed=10**6, transcendentals=0),
    )(*(put[where](x) for where, x in args))


def ints(n):
    return ("smem", pltpu.SMEM((n,), jnp.int32))


def near(shape, dtype):
    return ("vmem", pltpu.VMEM(shape, dtype))


def code(x, scratch, row):
    top = jnp.maximum(jnp.max(jnp.abs(x), axis=0, keepdims=True), 1e-37)
    exponent = jnp.floor(jnp.log2(top)) + 1.0
    scratch[pl.ds(row, 1), :] = exponent
    return jnp.round(x * (jnp.exp2(-exponent) * LEVELS)).astype(jnp.int32).astype(jnp.int16)


def widen(x):
    return x.astype(jnp.int32).astype(jnp.float32)


def place_of(axis):
    return lax.axis_index(axis).astype(jnp.int32)


def started(sem, *pairs):
    copies = [pltpu.make_async_copy(src, dst, sem.at[n]) for n, (src, dst) in enumerate(pairs)]
    for c in copies:
        c.start()
    return copies


def plan_kernel(
    mine_hbm, their_vmem, pc_hbm, cc_hbm, tiles_hbm, p_hbm,
    entries, count, small, sidx, tiles, p, pt, acc,
    source, mine, their, pc, cc, sem,
):
    lanes = [pl.ds(n * T, T) for n in range(8)]
    copies = started(
        sem,
        (mine_hbm, mine),
        (their_vmem, their),
        (p_hbm, p.at[0]),
        *((pc_hbm.at[:, lanes[n]], pc.at[n]) for n in range(8)),
        *((cc_hbm.at[:, lanes[n]], cc.at[n]) for n in range(4)),
        (tiles_hbm, tiles.at[pl.ds(0, NA)]),
    )
    b, g = place_of("row"), place_of("grp")
    odd = lax.rem(b, 2)
    quarters = (g * KG, lax.rem(g + 2, G) * KG)
    for n in range(LISTS):
        count[n] = 0
        for u in range(FRONT):
            row = (n * CAP + u) * WORDS
            entries[row] = 0
            for k in range(KP):
                entries[row + 1 + k] = SPARE
    source[2] = 0
    source[1] = jnp.where(odd == 0, 3, 1)
    source[3] = jnp.where(odd == 0, 1, 3)
    source[0] = jnp.where(odd == 0, 4, 2)
    source[4] = jnp.where(odd == 0, 2, 4)
    for n in range(PLIST):
        small[n] = 0
    lowest = (b - 3) * C
    for c in copies[:-1]:
        c.wait()

    def rows(i, _):
        for w in range(NW):
            acc[i * NW + w] = jnp.zeros((T, T), jnp.float32)
        for which, cols in enumerate((mine, their)):
            for s in range(S):
                j = cols[s, 0, i]
                block = source[(j >> 3) - b + 2]
                if which == 0:
                    n = jnp.where(block == 0, 0, block - 1) + jnp.where(block > 2, 1, 0)
                else:
                    n = jnp.maximum(block, 2)
                at = count[n]
                count[n] = at + 1
                row = (n * CAP + FRONT + at) * WORDS
                entries[row] = (which * NA + i * S + s) | ((block * F + (j & (F - 1))) << 8)
                for k in range(KP):
                    entries[row + 1 + k] = pc[j >> 7, k, j & (T - 1)] + (i * NW - lowest)
        for q in range(KP):
            pr = i * KP + q
            pt[pr] = p[0, i, q].T
            f = b * F + i
            c = pc[f >> 7, q, f & (T - 1)]
            local = c - (b - 1) * C
            block = local >> 2
            kind = jnp.where(block == 1, 2, jnp.where((block == 0) == (odd == 0), 0, 1))
            crow = kind * C + (local & (C - 1))
            at = small[PAIRS + crow]
            small[PAIRS + crow] = at + 1
            small[PLIST + crow * (F * KP) + at] = pr
            for k in range(KD):
                w = cc[c >> 7, quarters[k // KG] + k % KG, c & (T - 1)] - lowest
                sidx[pr * KD + k] = jnp.where((w >= 0) & (w < NW), i * NW + w, ZERO)
        return 0

    lax.fori_loop(0, F, rows, 0)
    for n in range(LISTS):
        many = count[n]
        for u in range(2 * U - 1):
            row = (n * CAP + FRONT + many + u) * WORDS
            entries[row] = 0
            for k in range(KP):
                entries[row + 1 + k] = SPARE
        count[n] = (many + (2 * U - 1)) >> 3
    copies[-1].wait()


def planned(mine, their, p_cols, c_cols, a_tiles, p_tiles):
    mine, their = jnp.transpose(mine, (2, 1, 0)), jnp.transpose(their, (2, 1, 0))
    smem = lambda *shape: pltpu.SMEM(shape, jnp.int32)
    return call(
        plan_kernel,
        [("hbm", mine), ("vmem", their)] + [("hbm", x) for x in (p_cols.T, c_cols.T, a_tiles, p_tiles)],
        [
            ints(LISTS * CAP * WORDS),
            ints(8),
            ints(SMALL),
            ints(F * KP * KD),
            near((2 * NA, T, T), jnp.bfloat16),
            near((5, F, KP, T, T), jnp.bfloat16),
            near((F * KP, T, T), jnp.bfloat16),
            near((NS, T, T), jnp.float32),
        ],
        [
            smem(8),
            smem(*mine.shape),
            smem(*mine.shape),
            smem(8, KP, T),
            smem(4, KC, T),
            pltpu.SemaphoreType.DMA((16,)),
        ],
    )


def entry_loop(n, count, entries, a, p, acc, sets):
    zero = jnp.zeros((T, T), jnp.bfloat16)

    def issue(low, high, at, u):
        word = entries[at + u * WORDS]
        tile = a[word & 255]
        j = word >> 8
        block, r = j >> 3, j & (F - 1)
        rhs = jnp.concatenate(
            [jnp.concatenate([p[block, r, 2 * k], p[block, r, 2 * k + 1]], axis=1) for k in range(2)], axis=0
        )
        pltpu.matmul_push_rhs(rhs, staging_register=(u // 2) % 2, mxu_index=u % 2)
        pltpu.matmul_acc_lhs(low[u], jnp.concatenate([tile, zero], axis=1), load_staged_rhs=(u // 2) % 2)
        pltpu.matmul_acc_lhs(high[u], jnp.concatenate([zero, tile], axis=1))

    def drain(low, high, at, u):
        for k, ref in enumerate((low[u], high[u])):
            x = pltpu.matmul_pop(ref)
            for e in range(2):
                slot = entries[at + u * WORDS + 1 + 2 * k + e]
                acc[slot] += x[:, e * T : (e + 1) * T]

    def double(t, _):
        at = (n * CAP + FRONT + 2 * U * t) * WORDS
        for u in range(U):
            issue(*sets[0], at, u)
            drain(*sets[1], at - U * WORDS, u)
        for u in range(U):
            issue(*sets[1], at + U * WORDS, u)
            drain(*sets[0], at, u)
        return 0

    many = count[n]
    lax.fori_loop(0, many, double, 0)
    for u in range(U):
        drain(*sets[1], (n * CAP + 2 * U * many) * WORDS, u)


def with_sets(work):
    def body(*refs):
        refs = list(refs)
        sets = []
        for _ in range(2):
            sets.append(([refs.pop(0) for _ in range(U)], [refs.pop(0) for _ in range(U)]))
        for low, high in sets:
            for ref in (*low, *high):
                pltpu.matmul_pop(ref)
        work(sets)

    pl.run_scoped(body, *[pltpu.ACC(u % 2)((T, 2 * T), jnp.float32) for _ in range(4) for u in range(U)])


def part_kernel(lists, blocks, with_tiles, split, count, entries, *refs):
    refs = list(refs)
    tiles = refs.pop(0) if with_tiles else None
    new = [refs.pop(0) for _ in blocks]
    if split:
        a, p, acc, sp = refs[-4:]
    else:
        a, p, acc = refs[-3:]
    for block, ref in zip(blocks, new):
        p[block] = ref[...]
    if with_tiles:
        a[NA : 2 * NA] = tiles[...]

    def work(sets):
        for n in lists:
            entry_loop(n, count, entries, a, p, acc, sets)

    with_sets(work)
    if split:
        sp[ZERO] = jnp.zeros((2 * T, T), jnp.bfloat16)

        def halves(t, _):
            for u in range(4):
                n = t * 4 + u
                x = acc[n]
                hi = x.astype(jnp.bfloat16)
                sp[n, 0:T, :] = hi
                sp[n, T : 2 * T, :] = (x - hi.astype(jnp.float32)).astype(jnp.bfloat16)
            return 0

        lax.fori_loop(0, F * NW // 4, halves, 0)


def part(lists, tabs, state, blocks, tiles=None, split=False):
    args = [("smem", x) for x in tabs]
    if tiles is not None:
        args.append(("vmem", tiles))
    args += [("vmem", x) for x in blocks.values()]
    outs = [near((2 * NA, T, T), jnp.bfloat16), near((5, F, KP, T, T), jnp.bfloat16), near((NS, T, T), jnp.float32)]
    alias = {len(args) + n: n for n in range(len(state))}
    args += [("vmem", x) for x in state]
    if split:
        outs.append(near((NS, 2 * T, T), jnp.bfloat16))
    return call(functools.partial(part_kernel, lists, tuple(blocks), tiles is not None, split), args, outs, alias=alias)


def coarse_kernel(rows, small, sidx, sp, pt, *refs):
    outs, ex = refs[:-1], refs[-1]

    def body(*accs):
        for acc in accs:
            pltpu.matmul_pop(acc)
        for c, (kind, at, *half) in rows:
            out = outs[0].at[half[0]] if half else outs[0]
            e0 = half[0] * 2 * SCALES if half else 0

            def pair(r, _):
                pr = small[PLIST + c * (F * KP) + r]
                tile = pt[pr]
                lhs = jnp.concatenate([tile, tile], axis=1)
                for n in range(KD // 2):
                    rhs = jnp.concatenate([sp[sidx[pr * KD + 2 * n]], sp[sidx[pr * KD + 2 * n + 1]]], axis=1)
                    pltpu.matmul_push_rhs(rhs, staging_register=(n // 2) % 2, mxu_index=n % 2)
                    pltpu.matmul_acc_lhs(accs[n], lhs, load_staged_rhs=(n // 2) % 2)
                return 0

            lax.fori_loop(0, small[PAIRS + c], pair, 0)
            for n in range(KD // 2):
                x = pltpu.matmul_pop(accs[n])
                for e in range(2):
                    k = 2 * n + e
                    y = x[:, e * T : (e + 1) * T]
                    if kind == "plain":
                        out[at, k] = y
                    else:
                        d, t = k // KG, at * KG + k % KG
                        out[d, t * T : (t + 1) * T, :] = code(y, ex, e0 + d * SCALES + t)
            if kind == "code" and at == HC - 1:
                for d in range(2):
                    r0 = e0 + d * SCALES
                    out[d, ROWS:PACK, :] = ex[r0 : r0 + SCALES, :].astype(jnp.int32).astype(jnp.int16)

    pl.run_scoped(body, *[pltpu.ACC(n % 2)((T, 2 * T), jnp.float32) for n in range(KD // 2)])


def coarse(rows, out, tabs, sp, pt):
    return call(
        functools.partial(coarse_kernel, rows),
        [("smem", tabs[0]), ("smem", tabs[1]), ("vmem", sp), ("vmem", pt)],
        [out],
        [pltpu.VMEM((4 * SCALES, T), jnp.float32)],
    )[0]


def outer_chunk(h, *args):
    rows = [(HC * h + c, ("code", c)) for c in range(HC)]
    return coarse(rows, near((2, PACK, T), jnp.int16), *args)


def inner_chunks(*args):
    rows = [(C + HC * h + c, ("code", c, h)) for h in range(2) for c in range(HC)]
    return coarse(rows, near((2, 2, PACK, T), jnp.int16), *args)


def own_rows(h, *args):
    rows = [(2 * C + HC * h + c, ("plain", c)) for c in range(HC)]
    return coarse(rows, near((HC, KD, T, T), jnp.float32), *args)


def tiles():
    return [(c * KG + k, c, k, slice((c * KG + k) * T, (c * KG + k + 1) * T)) for c in range(HC) for k in range(KG)]


def sum_kernel(h, own, inner, outer, mine, send, ex_i, ex_o, ex):
    for d in (1, 0):
        ex_i[...] = jnp.exp2(widen(inner[h, d, ROWS:PACK, :])) * (1.0 / LEVELS)
        ex_o[...] = jnp.exp2(widen(outer[d, ROWS:PACK, :])) * (1.0 / LEVELS)
        for t, c, k, rows in tiles():
            x = own[c, d * KG + k] + widen(inner[h, d, rows, :]) * ex_i[t : t + 1, :]
            x = x + widen(outer[d, rows, :]) * ex_o[t : t + 1, :]
            if d:
                send[rows, :] = code(x, ex, t)
            else:
                mine[c, k] = x
        if d:
            send[ROWS:PACK, :] = ex[...].astype(jnp.int32).astype(jnp.int16)


def summed(h, own, inner, outer):
    return call(
        functools.partial(sum_kernel, h),
        [("vmem", x) for x in (own, inner, outer)],
        [near((HC, KG, T, T), jnp.float32), near((PACK, T), jnp.int16)],
        [pltpu.VMEM((SCALES, T), jnp.float32)] * 3,
    )


def final_kernel(*refs):
    out, ex = refs[-2:]
    for h in range(2):
        mine, got = refs[2 * h : 2 * h + 2]
        ex[...] = jnp.exp2(widen(got[ROWS:PACK, :])) * (1.0 / LEVELS)
        for t, c, k, rows in tiles():
            out[h * HC + c, k] = mine[c, k] + widen(got[rows, :]) * ex[t : t + 1, :]


def finished(parts):
    return call(
        final_kernel,
        [("vmem", x) for x in parts],
        [("vmem", jax.ShapeDtypeStruct((C, KG, T, T), jnp.float32))],
        [pltpu.VMEM((SCALES, T), jnp.float32)],
    )[0]


def along(x, to):
    n = lax.axis_size("row")
    return lax.ppermute(x, "row", [(i, to(i) % n) for i in range(n)])


def across(x, to):
    rows, n = lax.axis_size("row"), lax.axis_size("grp")
    return lax.ppermute(
        x, ("grp", "row"), [(g * rows + r, to(g, r % 2) * rows + r) for r in range(rows) for g in range(n)]
    )


def partner(g, core):
    return g ^ (3 if core else 1)


def opposite(g, core):
    return g ^ 2


def other(i):
    return i ^ 1


def away(i):
    return i - 1 if i % 2 == 0 else i + 1


def body(a_tiles, a_cols, p_tiles, p_cols, c_cols):
    tiles = a_tiles.reshape(NA, T, T)
    their_cols = across(a_cols, partner)
    turn = along(p_tiles, lambda i: i - 2 if i % 2 == 0 else i + 2)
    their_tiles = across(tiles, partner)
    beside = along(p_tiles, other)
    keep = along(p_tiles, lambda i: i + 2 if i % 2 == 0 else i - 2)
    entries, count, small, sidx, a, p, pt, acc = planned(a_cols, their_cols, p_cols, c_cols, tiles, p_tiles)
    lists, tabs, state = (count, entries), (small, sidx), (a, p, acc)
    state = part((0,), lists, state, {1: beside})
    far = along(turn, other)
    state = part((1,), lists, state, {2: turn})
    state = part((2, 3), lists, state, {3: far}, their_tiles)
    sp = part((4,), lists, state, {4: keep}, split=True)[3]
    out0 = outer_chunk(0, tabs, sp, pt)
    got0 = along(out0, away)
    ins = inner_chunks(tabs, sp, pt)
    out1 = outer_chunk(1, tabs, sp, pt)
    inner = along(ins, other)
    got1 = along(out1, away)
    parts = []
    for h, outer in enumerate((got0, got1)):
        own = own_rows(h, tabs, sp, pt)
        mine, send = summed(h, own, inner, outer)
        parts += [mine, across(send, opposite)]
    return finished(parts)


def solution(mesh):
    return jax.shard_map(
        body,
        mesh=mesh,
        in_specs=(
            P("row", "grp", None, None, None),
            P("row", "grp", None),
            P("row", None, None, None),
            P(),
            P(),
        ),
        out_specs=P("row", "grp", None, None),
        check_vma=False,
    )
```

time: 435 us -> 93.6 us (0.22)
  the two profiles are of different devices: /device:TPU:6 before, /device:TPU:24 now
where the time goes in v3:
time: 93.6 us; the launch traced here: 93.2 us
  starting transfers between devices  41.9 us (45%)
  waiting for transfers between devices  27.4 us (29%)
  Pallas kernels  23.7 us (25%)
    ppermute x7, starting transfers between devices, along(): return lax.ppermute(x, 'row', [(i, to(i) % n) for i in range(n)])  32.6 us
    pallas_call x13, Pallas kernels, call(): pl.pallas_call(kernel, out_shape=[x for _, x in outs], in_specs=[spec[whe...  23.7 us
    ppermute x4, waiting for transfers between devices, across(): lax.ppermute(x, ('grp', 'row'), [(g * rows + r, to(g, r % 2) * rows + r)...  14 us
    ppermute x7, waiting for transfers between devices, along(): return lax.ppermute(x, 'row', [(i, to(i) % n) for i in range(n)])  13.4 us
    ppermute x4, starting transfers between devices, across(): lax.ppermute(x, ('grp', 'row'), [(g * rows + r, to(g, r % 2) * rows + r)...  9.26 us
  transfers between devices with their start and end apart: 11, of which 6 were waited for; matrix products, arithmetic and copies ran while one was open for 0% of the time, Pallas kernels for 19%

profile of v3, /device:TPU:24, one launch (start us, length us, event | category | flops | bytes accessed | tf_op | source)
XLA Modules:
  0.0 93.2 jit_solution(10137781664485622310)
XLA Ops:
  0.0 13.6 %collective-permute-start.3 = (bf16[8,4,128,128]{3,2,1,0:T(8,128)(2,1)}, bf16[8,4,128,128]{3,2,1,0:T(8,128)(2,1)S(1)}, u32[]{:S(2)}, u32[]{:S(2)}) collective-permute-start(bf16[8,4,128,128]{3,2,1,0:T(8,128)(2,1)} %p_hbm.1), channel_id=1, source_target_pairs={{0,126},{1,3},{2,0},{3,5},{4,2},{5,7},{6,4},{7,9},{8,6},{9,11},{10... | collective-permute-start | bytes 3145736 | tf_op jit(solution)/shard_map/ppermute | solution.py:414
  13.6 2.7 %collective-permute-start.2 = (bf16[56,128,128]{2,1,0:T(8,128)(2,1)}, bf16[56,128,128]{2,1,0:T(8,128)(2,1)S(1)}, u32[]{:S(2)}, u32[]{:S(2)}) collective-permute-start(bf16[56,128,128]{2,1,0:T(8,128)(2,1)} %bitcast.6), channel_id=1, source_target_pairs={{0,128},{128,0},{256,384},{384,256},{1,385},{129,257},{257,129},{3... | collective-permute-start | bytes 5505032 | tf_op jit(solution)/shard_map/ppermute | solution.py:419
  16.3 1.9 %collective-permute-start.5 = (bf16[8,4,128,128]{3,2,1,0:T(8,128)(2,1)}, bf16[8,4,128,128]{3,2,1,0:T(8,128)(2,1)S(1)}, u32[]{:S(2)}, u32[]{:S(2)}) collective-permute-start(bf16[8,4,128,128]{3,2,1,0:T(8,128)(2,1)} %p_hbm.1), channel_id=1, source_target_pairs={{0,1},{1,0},{2,3},{3,2},{4,5},{5,4},{6,7},{7,6},{8,9},{9,8},{10,11... | collective-permute-start | bytes 3145736 | tf_op jit(solution)/shard_map/ppermute | solution.py:414
  18.2 8.0 %collective-permute-done.3.refs_0_ = bf16[8,4,128,128]{3,2,1,0:T(8,128)(2,1)S(1)} collective-permute-done((bf16[8,4,128,128]{3,2,1,0:T(8,128)(2,1)}, bf16[8,4,128,128]{3,2,1,0:T(8,128)(2,1)S(1)}, u32[]{:S(2)}, u32[]{:S(2)}) %collective-permute-start.3) | collective-permute-done | bytes 1048608 | tf_op jit(solution)/shard_map/ppermute | solution.py:414
  26.2 1.9 %collective-permute-start.4 = (bf16[8,4,128,128]{3,2,1,0:T(8,128)(2,1)S(1)}, bf16[8,4,128,128]{3,2,1,0:T(8,128)(2,1)S(1)}, u32[]{:S(2)}, u32[]{:S(2)}) collective-permute-start(bf16[8,4,128,128]{3,2,1,0:T(8,128)(2,1)S(1)} %collective-permute-done.3.refs_0_), channel_id=1, source_target_pairs={{0,1},{1,0},{2,3},{3,2},{4,5},{5,4},{6,7},{7,6},{8,9},{9,8},{10,11... | collective-permute-start | bytes 3145736 | tf_op jit(solution)/shard_map/ppermute | solution.py:414
  28.1 1.9 %collective-permute-start.1 = (bf16[8,4,128,128]{3,2,1,0:T(8,128)(2,1)}, bf16[8,4,128,128]{3,2,1,0:T(8,128)(2,1)S(1)}, u32[]{:S(2)}, u32[]{:S(2)}) collective-permute-start(bf16[8,4,128,128]{3,2,1,0:T(8,128)(2,1)} %p_hbm.1), channel_id=1, source_target_pairs={{0,2},{1,127},{2,4},{3,1},{4,6},{5,3},{6,8},{7,5},{8,10},{9,7},{10... | collective-permute-start | bytes 3145736 | tf_op jit(solution)/shard_map/ppermute | solution.py:414
  30.0 2.7 %collective-permute-start = (s32[8,1,7]{0,1,2:T(1,128)}, s32[8,1,7]{0,1,2:T(1,128)S(1)}, u32[]{:S(2)}, u32[]{:S(2)}) collective-permute-start(s32[8,1,7]{0,1,2:T(1,128)} %param.6), channel_id=1, source_target_pairs={{0,128},{128,0},{256,384},{384,256},{1,385},{129,257},{257,129},{3... | collective-permute-start | bytes 680 | tf_op jit(solution)/shard_map/ppermute | solution.py:419
  32.7 6.3 %collective-permute-done = s32[8,1,7]{0,1,2:T(1,128)S(1)} collective-permute-done((s32[8,1,7]{0,1,2:T(1,128)}, s32[8,1,7]{0,1,2:T(1,128)S(1)}, u32[]{:S(2)}, u32[]{:S(2)}) %collective-permute-start) | collective-permute-done | bytes 256 | tf_op jit(solution)/shard_map/ppermute | solution.py:419
  39.0 6.6 %shard_map.55 = (s32[3100]{0:T(1024)S(4)}, s32[8]{0:T(128)S(4)}, s32[400]{0:T(512)S(4)}, s32[256]{0:T(256)S(4)}, bf16[112,128,128]{2,1,0:T(8,128)(2,1)S(1)}, /*i...) custom-call(s32[7,1,8]{2,1,0:T(1,128)} %bitcast.10, ...), custom_call_target="tpu_custom_call" | custom-call | flops 20000000 | bytes 1000000 | tf_op jit(solution)/shard_map/pallas_call | solution.py:54
  45.6 0.0 collective-permute-done.5.refs_0_
  45.6 2.0 %shard_map.56 = (bf16[112,128,128]{2,1,0:T(8,128)(2,1)S(1)}, bf16[5,8,4,128,128]{4,3,2,1,0:T(8,128)(2,1)S(1)}, f32[226,128,128]{2,1,0:T(8,128)S(1)}) custom-call(s32[8]{0:T(128)S(4)} %get-tuple-element.29.count, s32[3100]{0:T(1024)S(4)} %get-tuple-element.30.entries, ...), custom_call_target="tpu_custom_call", output_to_operand_aliasing={{0}: (3, {}), {1}: (4, {}), {2}: (5, {})} | custom-call | flops 20000000 | bytes 1000000 | tf_op jit(solution)/shard_map/pallas_call | solution.py:54
  47.6 2.0 %shard_map.57 = (bf16[112,128,128]{2,1,0:T(8,128)(2,1)S(1)}, bf16[5,8,4,128,128]{4,3,2,1,0:T(8,128)(2,1)S(1)}, f32[226,128,128]{2,1,0:T(8,128)S(1)}) custom-call(s32[8]{0:T(128)S(4)} %get-tuple-element.29.count, s32[3100]{0:T(1024)S(4)} %get-tuple-element.30.entries, ...), custom_call_target="tpu_custom_call", output_to_operand_aliasing={{0}: (3, {}), {1}: (4, {}), {2}: (5, {})} | custom-call | flops 20000000 | bytes 1000000 | tf_op jit(solution)/shard_map/pallas_call | solution.py:54
  49.6 0.0 collective-permute-done.2.refs_0_
  49.6 0.0 collective-permute-done.4.refs_1_
  49.6 3.4 %shard_map.58 = (bf16[112,128,128]{2,1,0:T(8,128)(2,1)S(1)}, bf16[5,8,4,128,128]{4,3,2,1,0:T(8,128)(2,1)S(1)}, f32[226,128,128]{2,1,0:T(8,128)S(1)}) custom-call(s32[8]{0:T(128)S(4)} %get-tuple-element.29.count, s32[3100]{0:T(1024)S(4)} %get-tuple-element.30.entries, ...), custom_call_target="tpu_custom_call", output_to_operand_aliasing={{0}: (4, {}), {1}: (5, {}), {2}: (6, {})} | custom-call | flops 20000000 | bytes 1000000 | tf_op jit(solution)/shard_map/pallas_call | solution.py:54
  53.0 0.0 collective-permute-done.1.refs_0_
  53.0 2.0 %shard_map.59 = (bf16[112,128,128]{2,1,0:T(8,128)(2,1)S(1)}, bf16[5,8,4,128,128]{4,3,2,1,0:T(8,128)(2,1)S(1)}, f32[226,128,128]{2,1,0:T(8,128)S(1)}, bf16[226,256,128]{2,1,0:T(8,128)(2,1)S(1)}) custom-call(s32[8]{0:T(128)S(4)} %get-tuple-element.29.count, ...), custom_call_target="tpu_custom_call", output_to_operand_aliasing={{0}: (3, {}), {1}: (4, {}), {2}: (5, {})} | custom-call | flops 20000000 | bytes 1000000 | tf_op jit(solution)/shard_map/pallas_call | solution.py:54
  55.0 2.5 %shard_map.61 = s16[2,2,1040,128]{3,2,1,0:T(8,128)(2,1)S(1)} custom-call(s32[400]{0:T(512)S(4)} %get-tuple-element.27.small, s32[256]{0:T(256)S(4)} %get-tuple-element.28.sidx, bf16[226,256,128]{2,1,0:T(8,128)(2,1)S(1)} %get-tuple-element.43.sp, bf16[32,128,128]{2,1,0:T(8,128)(2,1)S(1)} %get-tuple-element.44.pt), custom_call_target="tpu_custom_call" | custom-call | flops 20000000 | bytes 1000000 | tf_op jit(solution)/shard_map/pallas_call | solution.py:54
  57.5 4.4 %collective-permute-start.6 = (s16[2,2,1040,128]{3,2,1,0:T(8,128)(2,1)S(1)}, s16[2,2,1040,128]{3,2,1,0:T(8,128)(2,1)S(1)}, u32[]{:S(2)}, u32[]{:S(2)}) collective-permute-start(s16[2,2,1040,128]{3,2,1,0:T(8,128)(2,1)S(1)} %shard_map.61), channel_id=1, source_target_pairs={{0,1},{1,0},{2,3},{3,2},{4,5},{5,4},{6,7},{7,6},{8,9},{9,8},{10,11... | collective-permute-start | bytes 3194888 | tf_op jit(solution)/shard_map/ppermute | solution.py:414
  61.9 0.3 shard_map.65
  62.2 2.0 %collective-permute-start.9 = (s16[2,1040,128]{2,1,0:T(8,128)(2,1)S(1)}, s16[2,1040,128]{2,1,0:T(8,128)(2,1)S(1)}, u32[]{:S(2)}, u32[]{:S(2)}) collective-permute-start(s16[2,1040,128]{2,1,0:T(8,128)(2,1)S(1)} %shard_map.65), channel_id=1, source_target_pairs={{0,127},{1,2},{2,1},{3,4},{4,3},{5,6},{6,5},{7,8},{8,7},{9,10},{10... | collective-permute-start | bytes 1597448 | tf_op jit(solution)/shard_map/ppermute | solution.py:414
  64.2 0.3 shard_map.62
  64.6 6.9 %collective-permute-start.7 = (s16[2,1040,128]{2,1,0:T(8,128)(2,1)S(1)}, s16[2,1040,128]{2,1,0:T(8,128)(2,1)S(1)}, u32[]{:S(2)}, u32[]{:S(2)}) collective-permute-start(s16[2,1040,128]{2,1,0:T(8,128)(2,1)S(1)} %shard_map.62), channel_id=1, source_target_pairs={{0,127},{1,2},{2,1},{3,4},{4,3},{5,6},{6,5},{7,8},{8,7},{9,10},{10... | collective-permute-start | bytes 1597448 | tf_op jit(solution)/shard_map/ppermute | solution.py:414
  71.4 1.1 %shard_map.64.own = f32[2,8,128,128]{3,2,1,0:T(8,128)S(1)} custom-call(s32[400]{0:T(512)S(4)} %get-tuple-element.27.small, s32[256]{0:T(256)S(4)} %get-tuple-element.28.sidx, bf16[226,256,128]{2,1,0:T(8,128)(2,1)S(1)} %get-tuple-element.43.sp, bf16[32,128,128]{2,1,0:T(8,128)(2,1)S(1)} %get-tuple-element.44.pt), custom_call_target="tpu_custom_call" | custom-call | flops 20000000 | bytes 1000000 | tf_op jit(solution)/shard_map/pallas_call | solution.py:54
  72.6 1.6 %shard_map.60.own = f32[2,8,128,128]{3,2,1,0:T(8,128)S(1)} custom-call(s32[400]{0:T(512)S(4)} %get-tuple-element.27.small, s32[256]{0:T(256)S(4)} %get-tuple-element.28.sidx, bf16[226,256,128]{2,1,0:T(8,128)(2,1)S(1)} %get-tuple-element.43.sp, bf16[32,128,128]{2,1,0:T(8,128)(2,1)S(1)} %get-tuple-element.44.pt), custom_call_target="tpu_custom_call" | custom-call | flops 20000000 | bytes 1000000 | tf_op jit(solution)/shard_map/pallas_call | solution.py:54
  74.2 2.0 %collective-permute-done.9.outer = s16[2,1040,128]{2,1,0:T(8,128)(2,1)S(1)} collective-permute-done((s16[2,1040,128]{2,1,0:T(8,128)(2,1)S(1)}, s16[2,1040,128]{2,1,0:T(8,128)(2,1)S(1)}, u32[]{:S(2)}, u32[]{:S(2)}) %collective-permute-start.9) | collective-permute-done | bytes 532512 | tf_op jit(solution)/shard_map/ppermute | solution.py:414
  76.1 0.0 collective-permute-done.6.inner
  76.1 0.4 shard_map.66
  76.5 1.9 %collective-permute-start.10 = (s16[1040,128]{1,0:T(8,128)(2,1)S(1)}, s16[1040,128]{1,0:T(8,128)(2,1)S(1)}, u32[]{:S(2)}, u32[]{:S(2)}) collective-permute-start(s16[1040,128]{1,0:T(8,128)(2,1)S(1)} %get-tuple-element.48), channel_id=1, source_target_pairs={{0,256},{128,384},{256,0},{384,128},{1,257},{129,385},{257,1},{385... | collective-permute-start | bytes 798728 | tf_op jit(solution)/shard_map/ppermute | solution.py:419
  78.4 3.4 %collective-permute-done.7.outer = s16[2,1040,128]{2,1,0:T(8,128)(2,1)S(1)} collective-permute-done((s16[2,1040,128]{2,1,0:T(8,128)(2,1)S(1)}, s16[2,1040,128]{2,1,0:T(8,128)(2,1)S(1)}, u32[]{:S(2)}, u32[]{:S(2)}) %collective-permute-start.7) | collective-permute-done | bytes 532512 | tf_op jit(solution)/shard_map/ppermute | solution.py:414
  81.8 0.4 shard_map.63
  82.2 2.0 %collective-permute-start.8 = (s16[1040,128]{1,0:T(8,128)(2,1)S(1)}, s16[1040,128]{1,0:T(8,128)(2,1)S(1)}, u32[]{:S(2)}, u32[]{:S(2)}) collective-permute-start(s16[1040,128]{1,0:T(8,128)(2,1)S(1)} %get-tuple-element.46), channel_id=1, source_target_pairs={{0,256},{128,384},{256,0},{384,128},{1,257},{129,385},{257,1},{385... | collective-permute-start | bytes 798728 | tf_op jit(solution)/shard_map/ppermute | solution.py:419
  84.3 2.2 %collective-permute-done.10.refs_3_ = s16[1040,128]{1,0:T(8,128)(2,1)S(1)} collective-permute-done((s16[1040,128]{1,0:T(8,128)(2,1)S(1)}, s16[1040,128]{1,0:T(8,128)(2,1)S(1)}, u32[]{:S(2)}, u32[]{:S(2)}) %collective-permute-start.10) | collective-permute-done | bytes 266272 | tf_op jit(solution)/shard_map/ppermute | solution.py:419
  86.5 5.5 %collective-permute-done.8.refs_1_ = s16[1040,128]{1,0:T(8,128)(2,1)S(1)} collective-permute-done((s16[1040,128]{1,0:T(8,128)(2,1)S(1)}, s16[1040,128]{1,0:T(8,128)(2,1)S(1)}, u32[]{:S(2)}, u32[]{:S(2)}) %collective-permute-start.8) | collective-permute-done | bytes 266272 | tf_op jit(solution)/shard_map/ppermute | solution.py:419
  92.0 1.1 %shard_map.67 = f32[4,4,128,128]{3,2,1,0:T(8,128)} custom-call(f32[2,4,128,128]{3,2,1,0:T(8,128)S(1)} %get-tuple-element.45.refs_0_, s16[1040,128]{1,0:T(8,128)(2,1)S(1)} %collective-permute-done.8.refs_1_, f32[2,4,128,128]{3,2,1,0:T(8,128)S(1)} %get-tuple-element.47.refs_2_, s16[1040,128]{1,0:T(8,128)(2,1)S(1)} %collective-permute-done.10.refs_3_), custom_call_target="tpu_custom_call" | custom-call | flops 20000000 | bytes 1000000 | tf_op jit(solution)/shard_map/pallas_call | solution.py:54
Async XLA Ops:
  0.0 26.2 %collective-permute-start.3 = (bf16[8,4,128,128]{3,2,1,0:T(8,128)(2,1)}, bf16[8,4,128,128]{3,2,1,0:T(8,128)(2,1)S(1)}, u32[]{:S(2)}, u32[]{:S(2)}) collective-permute-start(bf16[8,4,128,128]{3,2,1,0:T(8,128)(2,1)} %p_hbm.1), channel_id=1, source_target_pairs={{0,126},{1,3},{2,0},{3,5},{4,2},{5,7},{6,4},{7,9},{8,6},{9,11},{10... | collective-permute-start | bytes 3145736 | tf_op jit(solution)/shard_map/ppermute | solution.py:414
  13.6 36.0 %collective-permute-start.2 = (bf16[56,128,128]{2,1,0:T(8,128)(2,1)}, bf16[56,128,128]{2,1,0:T(8,128)(2,1)S(1)}, u32[]{:S(2)}, u32[]{:S(2)}) collective-permute-start(bf16[56,128,128]{2,1,0:T(8,128)(2,1)} %bitcast.6), channel_id=1, source_target_pairs={{0,128},{128,0},{256,384},{384,256},{1,385},{129,257},{257,129},{3... | collective-permute-start | bytes 5505032 | tf_op jit(solution)/shard_map/ppermute | solution.py:419
  16.3 29.3 %collective-permute-start.5 = (bf16[8,4,128,128]{3,2,1,0:T(8,128)(2,1)}, bf16[8,4,128,128]{3,2,1,0:T(8,128)(2,1)S(1)}, u32[]{:S(2)}, u32[]{:S(2)}) collective-permute-start(bf16[8,4,128,128]{3,2,1,0:T(8,128)(2,1)} %p_hbm.1), channel_id=1, source_target_pairs={{0,1},{1,0},{2,3},{3,2},{4,5},{5,4},{6,7},{7,6},{8,9},{9,8},{10,11... | collective-permute-start | bytes 3145736 | tf_op jit(solution)/shard_map/ppermute | solution.py:414
  26.2 23.4 %collective-permute-start.4 = (bf16[8,4,128,128]{3,2,1,0:T(8,128)(2,1)S(1)}, bf16[8,4,128,128]{3,2,1,0:T(8,128)(2,1)S(1)}, u32[]{:S(2)}, u32[]{:S(2)}) collective-permute-start(bf16[8,4,128,128]{3,2,1,0:T(8,128)(2,1)S(1)} %collective-permute-done.3.refs_0_), channel_id=1, source_target_pairs={{0,1},{1,0},{2,3},{3,2},{4,5},{5,4},{6,7},{7,6},{8,9},{9,8},{10,11... | collective-permute-start | bytes 3145736 | tf_op jit(solution)/shard_map/ppermute | solution.py:414
  28.1 24.9 %collective-permute-start.1 = (bf16[8,4,128,128]{3,2,1,0:T(8,128)(2,1)}, bf16[8,4,128,128]{3,2,1,0:T(8,128)(2,1)S(1)}, u32[]{:S(2)}, u32[]{:S(2)}) collective-permute-start(bf16[8,4,128,128]{3,2,1,0:T(8,128)(2,1)} %p_hbm.1), channel_id=1, source_target_pairs={{0,2},{1,127},{2,4},{3,1},{4,6},{5,3},{6,8},{7,5},{8,10},{9,7},{10... | collective-permute-start | bytes 3145736 | tf_op jit(solution)/shard_map/ppermute | solution.py:414
  30.0 8.9 %collective-permute-start = (s32[8,1,7]{0,1,2:T(1,128)}, s32[8,1,7]{0,1,2:T(1,128)S(1)}, u32[]{:S(2)}, u32[]{:S(2)}) collective-permute-start(s32[8,1,7]{0,1,2:T(1,128)} %param.6), channel_id=1, source_target_pairs={{0,128},{128,0},{256,384},{384,256},{1,385},{129,257},{257,129},{3... | collective-permute-start | bytes 680 | tf_op jit(solution)/shard_map/ppermute | solution.py:419
  57.5 18.7 %collective-permute-start.6 = (s16[2,2,1040,128]{3,2,1,0:T(8,128)(2,1)S(1)}, s16[2,2,1040,128]{3,2,1,0:T(8,128)(2,1)S(1)}, u32[]{:S(2)}, u32[]{:S(2)}) collective-permute-start(s16[2,2,1040,128]{3,2,1,0:T(8,128)(2,1)S(1)} %shard_map.61), channel_id=1, source_target_pairs={{0,1},{1,0},{2,3},{3,2},{4,5},{5,4},{6,7},{7,6},{8,9},{9,8},{10,11... | collective-permute-start | bytes 3194888 | tf_op jit(solution)/shard_map/ppermute | solution.py:414
  62.2 13.9 %collective-permute-start.9 = (s16[2,1040,128]{2,1,0:T(8,128)(2,1)S(1)}, s16[2,1040,128]{2,1,0:T(8,128)(2,1)S(1)}, u32[]{:S(2)}, u32[]{:S(2)}) collective-permute-start(s16[2,1040,128]{2,1,0:T(8,128)(2,1)S(1)} %shard_map.65), channel_id=1, source_target_pairs={{0,127},{1,2},{2,1},{3,4},{4,3},{5,6},{6,5},{7,8},{8,7},{9,10},{10... | collective-permute-start | bytes 1597448 | tf_op jit(solution)/shard_map/ppermute | solution.py:414
  64.6 17.3 %collective-permute-start.7 = (s16[2,1040,128]{2,1,0:T(8,128)(2,1)S(1)}, s16[2,1040,128]{2,1,0:T(8,128)(2,1)S(1)}, u32[]{:S(2)}, u32[]{:S(2)}) collective-permute-start(s16[2,1040,128]{2,1,0:T(8,128)(2,1)S(1)} %shard_map.62), channel_id=1, source_target_pairs={{0,127},{1,2},{2,1},{3,4},{4,3},{5,6},{6,5},{7,8},{8,7},{9,10},{10... | collective-permute-start | bytes 1597448 | tf_op jit(solution)/shard_map/ppermute | solution.py:414
  76.5 10.0 %collective-permute-start.10 = (s16[1040,128]{1,0:T(8,128)(2,1)S(1)}, s16[1040,128]{1,0:T(8,128)(2,1)S(1)}, u32[]{:S(2)}, u32[]{:S(2)}) collective-permute-start(s16[1040,128]{1,0:T(8,128)(2,1)S(1)} %get-tuple-element.48), channel_id=1, source_target_pairs={{0,256},{128,384},{256,0},{384,128},{1,257},{129,385},{257,1},{385... | collective-permute-start | bytes 798728 | tf_op jit(solution)/shard_map/ppermute | solution.py:419
  82.2 9.8 %collective-permute-start.8 = (s16[1040,128]{1,0:T(8,128)(2,1)S(1)}, s16[1040,128]{1,0:T(8,128)(2,1)S(1)}, u32[]{:S(2)}, u32[]{:S(2)}) collective-permute-start(s16[1040,128]{1,0:T(8,128)(2,1)S(1)} %get-tuple-element.46), channel_id=1, source_target_pairs={{0,256},{128,384},{256,0},{384,128},{1,257},{129,385},{257,1},{385... | collective-permute-start | bytes 798728 | tf_op jit(solution)/shard_map/ppermute | solution.py:419

commit v4 on v3

v4 whole, which is shorter than its diff:
```python
import functools

import jax
import jax.numpy as jnp
from jax import lax
from jax.experimental import pallas as pl
from jax.experimental.pallas import tpu as pltpu
from jax.sharding import PartitionSpec as P


T = 128
F = 8
C = 4
S = 7
KP = 4
KC = 16
G = 4
KG = KC // G
KD = 2 * KG
NA = F * S
SCALES = C * KG
ROWS = SCALES * T
PACK = ROWS + SCALES
LEVELS = 32760.0
MB = 1 << 20

NW = 7 * C
SPARE = F * NW
ZERO = SPARE + 1
NS = ZERO + 1

LISTS = 4
U = 4
FRONT = U
CAP = FRONT + 2 * NA + 2 * U
WORDS = 1 + KP
PAIRS, PLIST = 0, 16
SMALL = PLIST + 3 * C * F * KP

SMEM = pl.BlockSpec(memory_space=pltpu.SMEM)
VMEM = pl.BlockSpec(memory_space=pltpu.VMEM)
HBM = pl.BlockSpec(memory_space=pltpu.HBM)


def call(kernel, args, outs, scratch=(), alias={}, mib=4):
    spec = {"smem": SMEM, "vmem": VMEM, "hbm": HBM}
    put = {
        "smem": lambda x: pltpu.with_memory_space_constraint(x, pltpu.SMEM),
        "vmem": lambda x: pltpu.with_memory_space_constraint(x, pltpu.VMEM),
        "hbm": lambda x: pltpu.with_memory_space_constraint(x, pltpu.HBM),
    }
    return pl.pallas_call(
        kernel,
        out_shape=[x for _, x in outs],
        in_specs=[spec[where] for where, _ in args],
        out_specs=[spec[where] for where, _ in outs],
        scratch_shapes=scratch,
        input_output_aliases=alias,
        compiler_params=pltpu.CompilerParams(vmem_limit_bytes=mib * MB),
        cost_estimate=pl.CostEstimate(flops=2 * 10**7, bytes_accessed=10**6, transcendentals=0),
    )(*(put[where](x) for where, x in args))


def ints(n):
    return ("smem", pltpu.SMEM((n,), jnp.int32))


def near(shape, dtype):
    return ("vmem", pltpu.VMEM(shape, dtype))


def code(x, scratch, row):
    top = jnp.maximum(jnp.max(jnp.abs(x), axis=0, keepdims=True), 1e-37)
    exponent = jnp.floor(jnp.log2(top)) + 1.0
    scratch[pl.ds(row, 1), :] = exponent
    return jnp.round(x * (jnp.exp2(-exponent) * LEVELS)).astype(jnp.int32).astype(jnp.int16)


def widen(x):
    return x.astype(jnp.int32).astype(jnp.float32)


def place_of(axis):
    return lax.axis_index(axis).astype(jnp.int32)


def started(sem, *pairs):
    copies = [pltpu.make_async_copy(src, dst, sem.at[n]) for n, (src, dst) in enumerate(pairs)]
    for c in copies:
        c.start()
    return copies


def plan_kernel(
    mine_hbm, their_vmem, pc_hbm, cc_hbm, tiles_hbm, p_hbm,
    entries, count, small, sidx, tiles, p, pt, acc, sp,
    source, mine, their, pc, cc, sem,
):
    b, g = place_of("row"), place_of("grp")
    odd = lax.rem(b, 2)
    quarters = (jnp.where(odd == 0, 3 - g, g + 1 - 2 * (g & 1)) * KG, g * KG)
    np, nc = pc_hbm.shape[1], cc_hbm.shape[1]
    copies = started(
        sem,
        (mine_hbm, mine),
        (their_vmem, their),
        (p_hbm, p.at[0]),
        *((pc_hbm.at[k], pc.at[pl.ds(k * np, np)]) for k in range(KP)),
        *((cc_hbm.at[quarters[k // KG] + k % KG], cc.at[pl.ds(k * nc, nc)]) for k in range(KD)),
        (tiles_hbm, tiles.at[pl.ds(0, NA)]),
    )
    for n in range(LISTS):
        count[n] = 0
        for u in range(FRONT):
            row = (n * CAP + u) * WORDS
            entries[row] = 0
            for k in range(KP):
                entries[row + 1 + k] = SPARE
    source[2] = 0
    source[1] = jnp.where(odd == 0, 3, 1)
    source[3] = jnp.where(odd == 0, 1, 3)
    source[0] = jnp.where(odd == 0, 4, 2)
    source[4] = jnp.where(odd == 0, 2, 4)
    for n in range(PLIST):
        small[n] = 0
    lowest = (b - 3) * C

    def clear(n, _):
        for w in range(4):
            acc[n * 4 + w] = jnp.zeros((T, T), jnp.float32)
        return 0

    lax.fori_loop(0, F * NW // 4, clear, 0)
    sp[ZERO] = jnp.zeros((2 * T, T), jnp.bfloat16)
    for c in copies[:-1]:
        c.wait()

    for which, cols in enumerate((mine, their)):

        def enter(i, _):
            for s in range(S):
                j = cols[s, 0, i]
                block = source[(j >> 3) - b + 2]
                n = jnp.where(block < 2, which, 2 + (block >> 2))
                at = count[n]
                count[n] = at + 1
                row = (n * CAP + FRONT + at) * WORDS
                entries[row] = (which * NA + i * S + s) | ((block * F + (j & (F - 1))) << 8)
                for k in range(KP):
                    entries[row + 1 + k] = pc[k * np + j] + (i * NW - lowest)
            return 0

        lax.fori_loop(0, F, enter, 0)

    def pairs(i, _):
        for q in range(KP):
            pr = i * KP + q
            pt[pr] = p[0, i, q].T
            c = pc[q * np + b * F + i]
            local = c - (b - 1) * C
            block = local >> 2
            kind = jnp.where(block == 1, 2, jnp.where((block == 0) == (odd == 0), 0, 1))
            crow = kind * C + (local & (C - 1))
            at = small[PAIRS + crow]
            small[PAIRS + crow] = at + 1
            small[PLIST + crow * (F * KP) + at] = pr
            for k in range(KD):
                w = cc[k * nc + c] - lowest
                sidx[pr * KD + k] = jnp.where((w >= 0) & (w < NW), i * NW + w, ZERO)
        return 0

    lax.fori_loop(0, F, pairs, 0)
    for n in range(LISTS):
        many = count[n]
        for u in range(2 * U - 1):
            row = (n * CAP + FRONT + many + u) * WORDS
            entries[row] = 0
            for k in range(KP):
                entries[row + 1 + k] = SPARE
        count[n] = (many + (2 * U - 1)) >> 3
    copies[-1].wait()


def planned(mine, their, p_cols, c_cols, a_tiles, p_tiles):
    mine, their = jnp.transpose(mine, (2, 1, 0)), jnp.transpose(their, (2, 1, 0))
    smem = lambda *shape: pltpu.SMEM(shape, jnp.int32)
    return call(
        plan_kernel,
        [("hbm", mine), ("vmem", their)] + [("hbm", x) for x in (p_cols.T, c_cols.T, a_tiles, p_tiles)],
        [
            ints(LISTS * CAP * WORDS),
            ints(8),
            ints(SMALL),
            ints(F * KP * KD),
            near((2 * NA, T, T), jnp.bfloat16),
            near((5, F, KP, T, T), jnp.bfloat16),
            near((F * KP, T, T), jnp.bfloat16),
            near((NS, T, T), jnp.float32),
            near((NS, 2 * T, T), jnp.bfloat16),
        ],
        [
            smem(8),
            smem(*mine.shape),
            smem(*mine.shape),
            smem(p_cols.size),
            smem(c_cols.size // 2),
            pltpu.SemaphoreType.DMA((16,)),
        ],
    )


def entry_loop(n, count, entries, a, p, acc, sets):
    zero = jnp.zeros((T, T), jnp.bfloat16)

    def issue(low, high, at, u):
        word = entries[at + u * WORDS]
        tile = a[word & 255]
        j = word >> 8
        block, r = j >> 3, j & (F - 1)
        rhs = jnp.concatenate(
            [jnp.concatenate([p[block, r, 2 * k], p[block, r, 2 * k + 1]], axis=1) for k in range(2)], axis=0
        )
        pltpu.matmul_push_rhs(rhs, staging_register=(u // 2) % 2, mxu_index=u % 2)
        pltpu.matmul_acc_lhs(low[u], jnp.concatenate([tile, zero], axis=1), load_staged_rhs=(u // 2) % 2)
        pltpu.matmul_acc_lhs(high[u], jnp.concatenate([zero, tile], axis=1))

    def drain(low, high, at, u):
        for k, ref in enumerate((low[u], high[u])):
            x = pltpu.matmul_pop(ref)
            for e in range(2):
                slot = entries[at + u * WORDS + 1 + 2 * k + e]
                acc[slot] += x[:, e * T : (e + 1) * T]

    def double(t, _):
        at = (n * CAP + FRONT + 2 * U * t) * WORDS
        for u in range(U):
            issue(*sets[0], at, u)
            drain(*sets[1], at - U * WORDS, u)
        for u in range(U):
            issue(*sets[1], at + U * WORDS, u)
            drain(*sets[0], at, u)
        return 0

    many = count[n]
    lax.fori_loop(0, many, double, 0)
    for u in range(U):
        drain(*sets[1], (n * CAP + 2 * U * many) * WORDS, u)


def with_sets(work):
    def body(*refs):
        refs = list(refs)
        sets = []
        for _ in range(2):
            sets.append(([refs.pop(0) for _ in range(U)], [refs.pop(0) for _ in range(U)]))
        for low, high in sets:
            for ref in (*low, *high):
                pltpu.matmul_pop(ref)
        work(sets)

    pl.run_scoped(body, *[pltpu.ACC(u % 2)((T, 2 * T), jnp.float32) for _ in range(4) for u in range(U)])


def part_kernel(lists, blocks, with_tiles, halve, count, entries, *refs):
    refs = list(refs)
    their = refs.pop(0) if with_tiles else None
    new = [refs.pop(0) for _ in blocks]
    a, p, acc, sp = refs[-4:]
    for block, ref in zip(blocks, new):
        p[block] = ref[...]
    if with_tiles:
        a[NA : 2 * NA] = their[...]

    def work(sets):
        for n in lists:
            entry_loop(n, count, entries, a, p, acc, sets)

    with_sets(work)
    if halve:
        odd = lax.rem(place_of("row"), 2)
        if halve == "most":
            start, width = (1 - odd) * 3 * C, 4 * C
        else:
            start, width = odd * 4 * C, 3 * C

        def halves(t, _):
            first = (t >> 2) * NW + start + (t & 3) * (width // 4)
            for u in range(width // 4):
                x = acc[first + u]
                hi = x.astype(jnp.bfloat16)
                sp[first + u, 0:T, :] = hi
                sp[first + u, T : 2 * T, :] = (x - hi.astype(jnp.float32)).astype(jnp.bfloat16)
            return 0

        lax.fori_loop(0, 4 * F, halves, 0)


def part(lists, tabs, state, blocks, tiles=None, halve=None):
    args = [("smem", x) for x in tabs]
    if tiles is not None:
        args.append(("vmem", tiles))
    args += [("vmem", x) for x in blocks.values()]
    outs = [near(x.shape, x.dtype) for x in state]
    alias = {len(args) + n: n for n in range(len(state))}
    args += [("vmem", x) for x in state]
    return call(functools.partial(part_kernel, lists, tuple(blocks), tiles is not None, halve), args, outs, alias=alias)


def coarse_kernel(first, quarters, coded, small, sidx, sp, pt, out, *refs):
    def body(*accs):
        for acc in accs:
            pltpu.matmul_pop(acc)
        for c in range(C):

            def pair(r, _):
                pr = small[PLIST + (first + c) * (F * KP) + r]
                tile = pt[pr]
                lhs = jnp.concatenate([tile, tile], axis=1)
                for n, acc in enumerate(accs):
                    k = pr * KD + quarters[0] * KG + 2 * n
                    rhs = jnp.concatenate([sp[sidx[k]], sp[sidx[k + 1]]], axis=1)
                    pltpu.matmul_push_rhs(rhs, staging_register=(n // 2) % 2, mxu_index=n % 2)
                    pltpu.matmul_acc_lhs(acc, lhs, load_staged_rhs=(n // 2) % 2)
                return 0

            lax.fori_loop(0, small[PAIRS + first + c], pair, 0)
            for n, acc in enumerate(accs):
                x = pltpu.matmul_pop(acc)
                for e in range(2):
                    q, k = divmod(2 * n + e, KG)
                    y = x[:, e * T : (e + 1) * T]
                    if coded:
                        t = c * KG + k
                        out[q, t * T : (t + 1) * T, :] = code(y, refs[0].at[q], t)
                    else:
                        out[c, k] = y
        if coded:
            for q in range(len(quarters)):
                out[q, ROWS:PACK, :] = refs[0][q].astype(jnp.int32).astype(jnp.int16)

    pl.run_scoped(body, *[pltpu.ACC(n % 2)((T, 2 * T), jnp.float32) for n in range(len(quarters) * KG // 2)])


OUTER, INNER, OWN = 0, C, 2 * C


def coarse(first, quarters, coded, tabs, sp, pt):
    n = len(quarters)
    out = near((n, PACK, T), jnp.int16) if coded else near((C, KG, T, T), jnp.float32)
    return call(
        functools.partial(coarse_kernel, first, quarters, coded),
        [("smem", tabs[0]), ("smem", tabs[1]), ("vmem", sp), ("vmem", pt)],
        [out],
        [pltpu.VMEM((n, SCALES, T), jnp.float32)] if coded else [],
    )[0]


def tiles():
    return [(c * KG + k, c, k, slice((c * KG + k) * T, (c * KG + k + 1) * T)) for c in range(C) for k in range(KG)]


def scale(ref, rows):
    ref[...] = jnp.exp2(widen(rows)) * (1.0 / LEVELS)


def cross_kernel(inner, outer, out, ex_i, ex_o, ex):
    scale(ex_i, inner[0, ROWS:PACK, :])
    scale(ex_o, outer[0, ROWS:PACK, :])
    for t, c, k, rows in tiles():
        x = widen(inner[0, rows, :]) * ex_i[t : t + 1, :] + widen(outer[0, rows, :]) * ex_o[t : t + 1, :]
        out[0, rows, :] = code(x, ex, t)
    out[0, ROWS:PACK, :] = ex[...].astype(jnp.int32).astype(jnp.int16)


def crossed(inner, outer):
    return call(
        cross_kernel,
        [("vmem", inner), ("vmem", outer)],
        [near((1, PACK, T), jnp.int16)],
        [pltpu.VMEM((SCALES, T), jnp.float32)] * 3,
    )[0]


def add_kernel(own, *refs):
    *coded, out, ex = refs
    coded = [x.at[x.shape[0] - 1] for x in coded]
    for n, x in enumerate(coded):
        scale(ex.at[n], x[ROWS:PACK, :])
    for t, c, k, rows in tiles():
        y = own[c, k]
        for n, x in enumerate(coded):
            y = y + widen(x[rows, :]) * ex[n, t : t + 1, :]
        out[c, k] = y


def added(own, coded, out):
    return call(
        add_kernel,
        [("vmem", x) for x in (own, *coded)],
        [("vmem", out)],
        [pltpu.VMEM((len(coded), SCALES, T), jnp.float32)],
    )[0]


def along(x, to):
    n = lax.axis_size("row")
    return lax.ppermute(x, "row", [(i, to(i) % n) for i in range(n)])


def across(x, to):
    rows, n = lax.axis_size("row"), lax.axis_size("grp")
    return lax.ppermute(
        x, ("grp", "row"), [(g * rows + r, to(g, r % 2) * rows + r) for r in range(rows) for g in range(n)]
    )


def partner(g, core):
    return g ^ (3 if core else 1)


def second(g, core):
    return partner(g, 1 - core)


def other(i):
    return i ^ 1


def away(i):
    return i - 1 if i % 2 == 0 else i + 1


def body(a_tiles, a_cols, p_tiles, p_cols, c_cols):
    tiles = a_tiles.reshape(NA, T, T)
    their_cols = across(a_cols, partner)
    their_tiles = across(tiles, partner)
    turn = along(p_tiles, lambda i: i - 2 if i % 2 == 0 else i + 2)
    beside = along(p_tiles, other)
    keep = along(p_tiles, lambda i: i + 2 if i % 2 == 0 else i - 2)
    entries, count, small, sidx, a, p, pt, acc, sp = planned(
        a_cols, their_cols, p_cols, c_cols, tiles, p_tiles
    )
    lists, state = (count, entries), (a, p, acc, sp)
    state = part((0,), lists, state, {1: beside})
    far = along(turn, other)
    state = part((1,), lists, state, {}, their_tiles)
    state = part((2,), lists, state, {2: turn, 3: far}, halve="most")
    sp = part((3,), lists, state, {4: keep}, halve="rest")[3]
    rows = ((small, sidx), sp, pt)
    x = coarse(OUTER, (0,), True, *rows)
    outer = along(x, away)
    x = coarse(INNER, (0, 1), True, *rows)
    inner = along(x, other)
    x = coarse(OWN, (0,), True, *rows)
    from_second = across(x, second)
    x = crossed(inner, outer)
    from_partner = across(x, partner)
    x = coarse(OUTER, (1,), True, *rows)
    outer = along(x, away)
    own = coarse(OWN, (1,), False, *rows)
    shape = (C, KG, T, T)
    mine = added(own, (inner, outer), pltpu.VMEM(shape, jnp.float32))
    return added(mine, (from_second, from_partner), jax.ShapeDtypeStruct(shape, jnp.float32))


def solution(mesh):
    return jax.shard_map(
        body,
        mesh=mesh,
        in_specs=(
            P("row", "grp", None, None, None),
            P("row", "grp", None),
            P("row", None, None, None),
            P(),
            P(),
        ),
        out_specs=P("row", "grp", None, None),
        check_vma=False,
    )
```

time: 93.6 us -> 89.4 us (0.955)
  the two profiles are of different devices: /device:TPU:24 before, /device:TPU:1 now
where the time goes in v4:
time: 89.4 us; the launch traced here: 89 us
  starting transfers between devices  49.8 us (56%)
  Pallas kernels  23.9 us (27%)
  waiting for transfers between devices  15.1 us (17%)
    ppermute x7, starting transfers between devices, along(): return lax.ppermute(x, 'row', [(i, to(i) % n) for i in range(n)])  36.6 us
    pallas_call x13, Pallas kernels, call(): pl.pallas_call(kernel, out_shape=[x for _, x in outs], in_specs=[spec[whe...  23.9 us
    ppermute x4, starting transfers between devices, across(): lax.ppermute(x, ('grp', 'row'), [(g * rows + r, to(g, r % 2) * rows + r)...  13.1 us
    ppermute x7, waiting for transfers between devices, along(): return lax.ppermute(x, 'row', [(i, to(i) % n) for i in range(n)])  9.44 us
    ppermute x4, waiting for transfers between devices, across(): lax.ppermute(x, ('grp', 'row'), [(g * rows + r, to(g, r % 2) * rows + r)...  5.65 us
  transfers between devices with their start and end apart: 11, of which 4 were waited for; matrix products, arithmetic and copies ran while one was open for 0% of the time, Pallas kernels for 21%

profile of v4, /device:TPU:1, one launch (start us, length us, event | category | flops | bytes accessed | tf_op | source)
XLA Modules:
  0.0 89.0 jit_solution(9632113236916685528)
XLA Ops:
  0.0 4.4 %collective-permute-start.2 = (bf16[8,4,128,128]{3,2,1,0:T(8,128)(2,1)}, bf16[8,4,128,128]{3,2,1,0:T(8,128)(2,1)S(1)}, u32[]{:S(2)}, u32[]{:S(2)}) collective-permute-start(bf16[8,4,128,128]{3,2,1,0:T(8,128)(2,1)} %p_hbm.1), channel_id=1, source_target_pairs={{0,126},{1,3},{2,0},{3,5},{4,2},{5,7},{6,4},{7,9},{8,6},{9,11},{10... | collective-permute-start | bytes 3145736 | tf_op jit(solution)/shard_map/ppermute | solution.py:407
  4.4 4.6 %collective-permute-start.4 = (bf16[56,128,128]{2,1,0:T(8,128)(2,1)}, bf16[56,128,128]{2,1,0:T(8,128)(2,1)S(1)}, u32[]{:S(2)}, u32[]{:S(2)}) collective-permute-start(bf16[56,128,128]{2,1,0:T(8,128)(2,1)} %bitcast.6), channel_id=1, source_target_pairs={{0,128},{128,0},{256,384},{384,256},{1,385},{129,257},{257,129},{3... | collective-permute-start | bytes 5505032 | tf_op jit(solution)/shard_map/ppermute | solution.py:412
  9.0 11.5 %collective-permute-start.5 = (bf16[8,4,128,128]{3,2,1,0:T(8,128)(2,1)}, bf16[8,4,128,128]{3,2,1,0:T(8,128)(2,1)S(1)}, u32[]{:S(2)}, u32[]{:S(2)}) collective-permute-start(bf16[8,4,128,128]{3,2,1,0:T(8,128)(2,1)} %p_hbm.1), channel_id=1, source_target_pairs={{0,1},{1,0},{2,3},{3,2},{4,5},{5,4},{6,7},{7,6},{8,9},{9,8},{10,11... | collective-permute-start | bytes 3145736 | tf_op jit(solution)/shard_map/ppermute | solution.py:407
  20.5 6.0 %collective-permute-done.2.refs_0_ = bf16[8,4,128,128]{3,2,1,0:T(8,128)(2,1)S(1)} collective-permute-done((bf16[8,4,128,128]{3,2,1,0:T(8,128)(2,1)}, bf16[8,4,128,128]{3,2,1,0:T(8,128)(2,1)S(1)}, u32[]{:S(2)}, u32[]{:S(2)}) %collective-permute-start.2) | collective-permute-done | bytes 1048608 | tf_op jit(solution)/shard_map/ppermute | solution.py:407
  26.5 3.1 %collective-permute-start.3 = (bf16[8,4,128,128]{3,2,1,0:T(8,128)(2,1)S(1)}, bf16[8,4,128,128]{3,2,1,0:T(8,128)(2,1)S(1)}, u32[]{:S(2)}, u32[]{:S(2)}) collective-permute-start(bf16[8,4,128,128]{3,2,1,0:T(8,128)(2,1)S(1)} %collective-permute-done.2.refs_0_), channel_id=1, source_target_pairs={{0,1},{1,0},{2,3},{3,2},{4,5},{5,4},{6,7},{7,6},{8,9},{9,8},{10,11... | collective-permute-start | bytes 3145736 | tf_op jit(solution)/shard_map/ppermute | solution.py:407
  29.6 7.3 %collective-permute-start.1 = (bf16[8,4,128,128]{3,2,1,0:T(8,128)(2,1)}, bf16[8,4,128,128]{3,2,1,0:T(8,128)(2,1)S(1)}, u32[]{:S(2)}, u32[]{:S(2)}) collective-permute-start(bf16[8,4,128,128]{3,2,1,0:T(8,128)(2,1)} %p_hbm.1), channel_id=1, source_target_pairs={{0,2},{1,127},{2,4},{3,1},{4,6},{5,3},{6,8},{7,5},{8,10},{9,7},{10... | collective-permute-start | bytes 3145736 | tf_op jit(solution)/shard_map/ppermute | solution.py:407
  36.9 4.6 %collective-permute-start = (s32[8,1,7]{0,1,2:T(1,128)}, s32[8,1,7]{0,1,2:T(1,128)S(1)}, u32[]{:S(2)}, u32[]{:S(2)}) collective-permute-start(s32[8,1,7]{0,1,2:T(1,128)} %param.6), channel_id=1, source_target_pairs={{0,128},{128,0},{256,384},{384,256},{1,385},{129,257},{257,129},{3... | collective-permute-start | bytes 680 | tf_op jit(solution)/shard_map/ppermute | solution.py:412
  41.6 1.5 %collective-permute-done = s32[8,1,7]{0,1,2:T(1,128)S(1)} collective-permute-done((s32[8,1,7]{0,1,2:T(1,128)}, s32[8,1,7]{0,1,2:T(1,128)S(1)}, u32[]{:S(2)}, u32[]{:S(2)}) %collective-permute-start) | collective-permute-done | bytes 256 | tf_op jit(solution)/shard_map/ppermute | solution.py:412
  43.1 4.3 %shard_map.55 = (s32[2480]{0:T(1024)S(4)}, s32[8]{0:T(128)S(4)}, s32[400]{0:T(512)S(4)}, s32[256]{0:T(256)S(4)}, bf16[112,128,128]{2,1,0:T(8,128)(2,1)S(1)}, /*i...) custom-call(s32[7,1,8]{2,1,0:T(1,128)} %bitcast.10, ...), custom_call_target="tpu_custom_call" | custom-call | flops 20000000 | bytes 1000000 | tf_op jit(solution)/shard_map/pallas_call | solution.py:52
  47.4 0.0 collective-permute-done.5.refs_0_
  47.4 2.4 %shard_map.56 = (bf16[112,128,128]{2,1,0:T(8,128)(2,1)S(1)}, bf16[5,8,4,128,128]{4,3,2,1,0:T(8,128)(2,1)S(1)}, f32[226,128,128]{2,1,0:T(8,128)S(1)}, bf16[226,256,128]{2,1,0:T(8,128)(2,1)S(1)}) custom-call(s32[8]{0:T(128)S(4)} %get-tuple-element.29.count, ...), custom_call_target="tpu_custom_call", output_to_operand_aliasing={{0}: (3, {}), {1}: (4, {}), {2}: (5, {}), {3}: (6, {})} | custom-call | flops 20000000 | bytes 1000000 | tf_op jit(solution)/shard_map/pallas_call | solution.py:52
  49.8 0.0 collective-permute-done.4.refs_0_
  49.8 2.0 %shard_map.57 = (bf16[112,128,128]{2,1,0:T(8,128)(2,1)S(1)}, bf16[5,8,4,128,128]{4,3,2,1,0:T(8,128)(2,1)S(1)}, f32[226,128,128]{2,1,0:T(8,128)S(1)}, bf16[226,256,128]{2,1,0:T(8,128)(2,1)S(1)}) custom-call(s32[8]{0:T(128)S(4)} %get-tuple-element.29.count, ...), custom_call_target="tpu_custom_call", output_to_operand_aliasing={{0}: (3, {}), {1}: (4, {}), {2}: (5, {}), {3}: (6, {})} | custom-call | flops 20000000 | bytes 1000000 | tf_op jit(solution)/shard_map/pallas_call | solution.py:52
  51.8 0.0 collective-permute-done.3.refs_1_
  51.8 2.6 %shard_map.58 = (bf16[112,128,128]{2,1,0:T(8,128)(2,1)S(1)}, bf16[5,8,4,128,128]{4,3,2,1,0:T(8,128)(2,1)S(1)}, f32[226,128,128]{2,1,0:T(8,128)S(1)}, bf16[226,256,128]{2,1,0:T(8,128)(2,1)S(1)}) custom-call(s32[8]{0:T(128)S(4)} %get-tuple-element.29.count, ...), custom_call_target="tpu_custom_call", output_to_operand_aliasing={{0}: (4, {}), {1}: (5, {}), {2}: (6, {}), {3}: (7, {})} | custom-call | flops 20000000 | bytes 1000000 | tf_op jit(solution)/shard_map/pallas_call | solution.py:52
  54.4 0.0 collective-permute-done.1.refs_0_
  54.4 2.4 %shard_map.59 = (bf16[112,128,128]{2,1,0:T(8,128)(2,1)S(1)}, bf16[5,8,4,128,128]{4,3,2,1,0:T(8,128)(2,1)S(1)}, f32[226,128,128]{2,1,0:T(8,128)S(1)}, bf16[226,256,128]{2,1,0:T(8,128)(2,1)S(1)}) custom-call(s32[8]{0:T(128)S(4)} %get-tuple-element.29.count, ...), custom_call_target="tpu_custom_call", output_to_operand_aliasing={{0}: (3, {}), {1}: (4, {}), {2}: (5, {}), {3}: (6, {})} | custom-call | flops 20000000 | bytes 1000000 | tf_op jit(solution)/shard_map/pallas_call | solution.py:52
  56.8 1.9 %shard_map.61 = s16[2,2064,128]{2,1,0:T(8,128)(2,1)S(1)} custom-call(s32[400]{0:T(512)S(4)} %get-tuple-element.27.small, s32[256]{0:T(256)S(4)} %get-tuple-element.28.sidx, bf16[226,256,128]{2,1,0:T(8,128)(2,1)S(1)} %get-tuple-element.47.sp, bf16[32,128,128]{2,1,0:T(8,128)(2,1)S(1)} %get-tuple-element.48.pt), custom_call_target="tpu_custom_call" | custom-call | flops 20000000 | bytes 1000000 | tf_op jit(solution)/shard_map/pallas_call | solution.py:52
  58.7 1.9 %collective-permute-start.6 = (s16[2,2064,128]{2,1,0:T(8,128)(2,1)S(1)}, s16[2,2064,128]{2,1,0:T(8,128)(2,1)S(1)}, u32[]{:S(2)}, u32[]{:S(2)}) collective-permute-start(s16[2,2064,128]{2,1,0:T(8,128)(2,1)S(1)} %shard_map.61), channel_id=1, source_target_pairs={{0,1},{1,0},{2,3},{3,2},{4,5},{5,4},{6,7},{7,6},{8,9},{9,8},{10,11... | collective-permute-start | bytes 3170312 | tf_op jit(solution)/shard_map/ppermute | solution.py:407
  60.6 1.7 %shard_map.65 = s16[1,2064,128]{2,1,0:T(8,128)(2,1)S(1)} custom-call(s32[400]{0:T(512)S(4)} %get-tuple-element.27.small, s32[256]{0:T(256)S(4)} %get-tuple-element.28.sidx, bf16[226,256,128]{2,1,0:T(8,128)(2,1)S(1)} %get-tuple-element.47.sp, bf16[32,128,128]{2,1,0:T(8,128)(2,1)S(1)} %get-tuple-element.48.pt), custom_call_target="tpu_custom_call" | custom-call | flops 20000000 | bytes 1000000 | tf_op jit(solution)/shard_map/pallas_call | solution.py:52
  62.3 1.9 %collective-permute-start.9 = (s16[1,2064,128]{2,1,0:T(8,128)(2,1)S(1)}, s16[1,2064,128]{2,1,0:T(8,128)(2,1)S(1)}, u32[]{:S(2)}, u32[]{:S(2)}) collective-permute-start(s16[1,2064,128]{2,1,0:T(8,128)(2,1)S(1)} %shard_map.65), channel_id=1, source_target_pairs={{0,127},{1,2},{2,1},{3,4},{4,3},{5,6},{6,5},{7,8},{8,7},{9,10},{10... | collective-permute-start | bytes 1585160 | tf_op jit(solution)/shard_map/ppermute | solution.py:407
  64.3 1.6 %shard_map.64 = s16[1,2064,128]{2,1,0:T(8,128)(2,1)S(1)} custom-call(s32[400]{0:T(512)S(4)} %get-tuple-element.27.small, s32[256]{0:T(256)S(4)} %get-tuple-element.28.sidx, bf16[226,256,128]{2,1,0:T(8,128)(2,1)S(1)} %get-tuple-element.47.sp, bf16[32,128,128]{2,1,0:T(8,128)(2,1)S(1)} %get-tuple-element.48.pt), custom_call_target="tpu_custom_call" | custom-call | flops 20000000 | bytes 1000000 | tf_op jit(solution)/shard_map/pallas_call | solution.py:52
  65.9 1.9 %collective-permute-start.8 = (s16[1,2064,128]{2,1,0:T(8,128)(2,1)S(1)}, s16[1,2064,128]{2,1,0:T(8,128)(2,1)S(1)}, u32[]{:S(2)}, u32[]{:S(2)}) collective-permute-start(s16[1,2064,128]{2,1,0:T(8,128)(2,1)S(1)} %shard_map.64), channel_id=1, source_target_pairs={{0,384},{128,256},{256,128},{384,0},{1,129},{129,1},{257,385},{385... | collective-permute-start | bytes 1585160 | tf_op jit(solution)/shard_map/ppermute | solution.py:412
  67.8 1.7 %shard_map.62 = s16[1,2064,128]{2,1,0:T(8,128)(2,1)S(1)} custom-call(s32[400]{0:T(512)S(4)} %get-tuple-element.27.small, s32[256]{0:T(256)S(4)} %get-tuple-element.28.sidx, bf16[226,256,128]{2,1,0:T(8,128)(2,1)S(1)} %get-tuple-element.47.sp, bf16[32,128,128]{2,1,0:T(8,128)(2,1)S(1)} %get-tuple-element.48.pt), custom_call_target="tpu_custom_call" | custom-call | flops 20000000 | bytes 1000000 | tf_op jit(solution)/shard_map/pallas_call | solution.py:52
  69.5 6.6 %collective-permute-start.7 = (s16[1,2064,128]{2,1,0:T(8,128)(2,1)S(1)}, s16[1,2064,128]{2,1,0:T(8,128)(2,1)S(1)}, u32[]{:S(2)}, u32[]{:S(2)}) collective-permute-start(s16[1,2064,128]{2,1,0:T(8,128)(2,1)S(1)} %shard_map.62), channel_id=1, source_target_pairs={{0,127},{1,2},{2,1},{3,4},{4,3},{5,6},{6,5},{7,8},{8,7},{9,10},{10... | collective-permute-start | bytes 1585160 | tf_op jit(solution)/shard_map/ppermute | solution.py:407
  76.1 0.0 collective-permute-done.9.outer
  76.1 0.0 collective-permute-done.6.refs_0_.inner
  76.1 0.4 shard_map.66
  76.5 1.9 %collective-permute-start.10 = (s16[1,2064,128]{2,1,0:T(8,128)(2,1)S(1)}, s16[1,2064,128]{2,1,0:T(8,128)(2,1)S(1)}, u32[]{:S(2)}, u32[]{:S(2)}) collective-permute-start(s16[1,2064,128]{2,1,0:T(8,128)(2,1)S(1)} %shard_map.66), channel_id=1, source_target_pairs={{0,128},{128,0},{256,384},{384,256},{1,385},{129,257},{257,129},{3... | collective-permute-start | bytes 1585160 | tf_op jit(solution)/shard_map/ppermute | solution.py:412
  78.5 1.4 %shard_map.60.own = f32[4,4,128,128]{3,2,1,0:T(8,128)S(1)} custom-call(s32[400]{0:T(512)S(4)} %get-tuple-element.27.small, s32[256]{0:T(256)S(4)} %get-tuple-element.28.sidx, bf16[226,256,128]{2,1,0:T(8,128)(2,1)S(1)} %get-tuple-element.47.sp, bf16[32,128,128]{2,1,0:T(8,128)(2,1)S(1)} %get-tuple-element.48.pt), custom_call_target="tpu_custom_call" | custom-call | flops 20000000 | bytes 1000000 | tf_op jit(solution)/shard_map/pallas_call | solution.py:52
  79.8 3.4 %collective-permute-done.7.refs_1_ = s16[1,2064,128]{2,1,0:T(8,128)(2,1)S(1)} collective-permute-done((s16[1,2064,128]{2,1,0:T(8,128)(2,1)S(1)}, s16[1,2064,128]{2,1,0:T(8,128)(2,1)S(1)}, u32[]{:S(2)}, u32[]{:S(2)}) %collective-permute-start.7) | collective-permute-done | bytes 528416 | tf_op jit(solution)/shard_map/ppermute | solution.py:407
  83.3 0.3 shard_map.63.own
  83.5 0.0 collective-permute-done.8.refs_0_
  83.6 4.2 %collective-permute-done.10.refs_1_ = s16[1,2064,128]{2,1,0:T(8,128)(2,1)S(1)} collective-permute-done((s16[1,2064,128]{2,1,0:T(8,128)(2,1)S(1)}, s16[1,2064,128]{2,1,0:T(8,128)(2,1)S(1)}, u32[]{:S(2)}, u32[]{:S(2)}) %collective-permute-start.10) | collective-permute-done | bytes 528416 | tf_op jit(solution)/shard_map/ppermute | solution.py:412
  87.7 1.3 %shard_map.67 = f32[4,4,128,128]{3,2,1,0:T(8,128)} custom-call(f32[4,4,128,128]{3,2,1,0:T(8,128)S(1)} %shard_map.63.own, s16[1,2064,128]{2,1,0:T(8,128)(2,1)S(1)} %collective-permute-done.8.refs_0_, s16[1,2064,128]{2,1,0:T(8,128)(2,1)S(1)} %collective-permute-done.10.refs_1_), custom_call_target="tpu_custom_call" | custom-call | flops 20000000 | bytes 1000000 | tf_op jit(solution)/shard_map/pallas_call | solution.py:52
Async XLA Ops:
  0.0 26.5 %collective-permute-start.2 = (bf16[8,4,128,128]{3,2,1,0:T(8,128)(2,1)}, bf16[8,4,128,128]{3,2,1,0:T(8,128)(2,1)S(1)}, u32[]{:S(2)}, u32[]{:S(2)}) collective-permute-start(bf16[8,4,128,128]{3,2,1,0:T(8,128)(2,1)} %p_hbm.1), channel_id=1, source_target_pairs={{0,126},{1,3},{2,0},{3,5},{4,2},{5,7},{6,4},{7,9},{8,6},{9,11},{10... | collective-permute-start | bytes 3145736 | tf_op jit(solution)/shard_map/ppermute | solution.py:407
  4.4 45.4 %collective-permute-start.4 = (bf16[56,128,128]{2,1,0:T(8,128)(2,1)}, bf16[56,128,128]{2,1,0:T(8,128)(2,1)S(1)}, u32[]{:S(2)}, u32[]{:S(2)}) collective-permute-start(bf16[56,128,128]{2,1,0:T(8,128)(2,1)} %bitcast.6), channel_id=1, source_target_pairs={{0,128},{128,0},{256,384},{384,256},{1,385},{129,257},{257,129},{3... | collective-permute-start | bytes 5505032 | tf_op jit(solution)/shard_map/ppermute | solution.py:412
  9.0 38.4 %collective-permute-start.5 = (bf16[8,4,128,128]{3,2,1,0:T(8,128)(2,1)}, bf16[8,4,128,128]{3,2,1,0:T(8,128)(2,1)S(1)}, u32[]{:S(2)}, u32[]{:S(2)}) collective-permute-start(bf16[8,4,128,128]{3,2,1,0:T(8,128)(2,1)} %p_hbm.1), channel_id=1, source_target_pairs={{0,1},{1,0},{2,3},{3,2},{4,5},{5,4},{6,7},{7,6},{8,9},{9,8},{10,11... | collective-permute-start | bytes 3145736 | tf_op jit(solution)/shard_map/ppermute | solution.py:407
  26.5 25.3 %collective-permute-start.3 = (bf16[8,4,128,128]{3,2,1,0:T(8,128)(2,1)S(1)}, bf16[8,4,128,128]{3,2,1,0:T(8,128)(2,1)S(1)}, u32[]{:S(2)}, u32[]{:S(2)}) collective-permute-start(bf16[8,4,128,128]{3,2,1,0:T(8,128)(2,1)S(1)} %collective-permute-done.2.refs_0_), channel_id=1, source_target_pairs={{0,1},{1,0},{2,3},{3,2},{4,5},{5,4},{6,7},{7,6},{8,9},{9,8},{10,11... | collective-permute-start | bytes 3145736 | tf_op jit(solution)/shard_map/ppermute | solution.py:407
  29.6 24.8 %collective-permute-start.1 = (bf16[8,4,128,128]{3,2,1,0:T(8,128)(2,1)}, bf16[8,4,128,128]{3,2,1,0:T(8,128)(2,1)S(1)}, u32[]{:S(2)}, u32[]{:S(2)}) collective-permute-start(bf16[8,4,128,128]{3,2,1,0:T(8,128)(2,1)} %p_hbm.1), channel_id=1, source_target_pairs={{0,2},{1,127},{2,4},{3,1},{4,6},{5,3},{6,8},{7,5},{8,10},{9,7},{10... | collective-permute-start | bytes 3145736 | tf_op jit(solution)/shard_map/ppermute | solution.py:407
  36.9 6.1 %collective-permute-start = (s32[8,1,7]{0,1,2:T(1,128)}, s32[8,1,7]{0,1,2:T(1,128)S(1)}, u32[]{:S(2)}, u32[]{:S(2)}) collective-permute-start(s32[8,1,7]{0,1,2:T(1,128)} %param.6), channel_id=1, source_target_pairs={{0,128},{128,0},{256,384},{384,256},{1,385},{129,257},{257,129},{3... | collective-permute-start | bytes 680 | tf_op jit(solution)/shard_map/ppermute | solution.py:412
  58.7 17.4 %collective-permute-start.6 = (s16[2,2064,128]{2,1,0:T(8,128)(2,1)S(1)}, s16[2,2064,128]{2,1,0:T(8,128)(2,1)S(1)}, u32[]{:S(2)}, u32[]{:S(2)}) collective-permute-start(s16[2,2064,128]{2,1,0:T(8,128)(2,1)S(1)} %shard_map.61), channel_id=1, source_target_pairs={{0,1},{1,0},{2,3},{3,2},{4,5},{5,4},{6,7},{7,6},{8,9},{9,8},{10,11... | collective-permute-start | bytes 3170312 | tf_op jit(solution)/shard_map/ppermute | solution.py:407
  62.3 13.7 %collective-permute-start.9 = (s16[1,2064,128]{2,1,0:T(8,128)(2,1)S(1)}, s16[1,2064,128]{2,1,0:T(8,128)(2,1)S(1)}, u32[]{:S(2)}, u32[]{:S(2)}) collective-permute-start(s16[1,2064,128]{2,1,0:T(8,128)(2,1)S(1)} %shard_map.65), channel_id=1, source_target_pairs={{0,127},{1,2},{2,1},{3,4},{4,3},{5,6},{6,5},{7,8},{8,7},{9,10},{10... | collective-permute-start | bytes 1585160 | tf_op jit(solution)/shard_map/ppermute | solution.py:407
  65.9 17.7 %collective-permute-start.8 = (s16[1,2064,128]{2,1,0:T(8,128)(2,1)S(1)}, s16[1,2064,128]{2,1,0:T(8,128)(2,1)S(1)}, u32[]{:S(2)}, u32[]{:S(2)}) collective-permute-start(s16[1,2064,128]{2,1,0:T(8,128)(2,1)S(1)} %shard_map.64), channel_id=1, source_target_pairs={{0,384},{128,256},{256,128},{384,0},{1,129},{129,1},{257,385},{385... | collective-permute-start | bytes 1585160 | tf_op jit(solution)/shard_map/ppermute | solution.py:412
  69.5 13.8 %collective-permute-start.7 = (s16[1,2064,128]{2,1,0:T(8,128)(2,1)S(1)}, s16[1,2064,128]{2,1,0:T(8,128)(2,1)S(1)}, u32[]{:S(2)}, u32[]{:S(2)}) collective-permute-start(s16[1,2064,128]{2,1,0:T(8,128)(2,1)S(1)} %shard_map.62), channel_id=1, source_target_pairs={{0,127},{1,2},{2,1},{3,4},{4,3},{5,6},{6,5},{7,8},{8,7},{9,10},{10... | collective-permute-start | bytes 1585160 | tf_op jit(solution)/shard_map/ppermute | solution.py:407
  76.5 11.2 %collective-permute-start.10 = (s16[1,2064,128]{2,1,0:T(8,128)(2,1)S(1)}, s16[1,2064,128]{2,1,0:T(8,128)(2,1)S(1)}, u32[]{:S(2)}, u32[]{:S(2)}) collective-permute-start(s16[1,2064,128]{2,1,0:T(8,128)(2,1)S(1)} %shard_map.66), channel_id=1, source_target_pairs={{0,128},{128,0},{256,384},{384,256},{1,385},{129,257},{257,129},{3... | collective-permute-start | bytes 1585160 | tf_op jit(solution)/shard_map/ppermute | solution.py:412

commit v5 on v4

--- a/solution.py
+++ b/solution.py
@@ -32,7 +32,7 @@
 LISTS = 4
 U = 4
 FRONT = U
-CAP = FRONT + 2 * NA + 2 * U
+CAP = FRONT + NA + 2 * U
 WORDS = 1 + KP
 PAIRS, PLIST = 0, 16
 SMALL = PLIST + 3 * C * F * KP
@@ -107,7 +107,7 @@
         (p_hbm, p.at[0]),
         *((pc_hbm.at[k], pc.at[pl.ds(k * np, np)]) for k in range(KP)),
         *((cc_hbm.at[quarters[k // KG] + k % KG], cc.at[pl.ds(k * nc, nc)]) for k in range(KD)),
-        (tiles_hbm, tiles.at[pl.ds(0, NA)]),
+        (tiles_hbm, tiles),
     )
     for n in range(LISTS):
         count[n] = 0
@@ -141,11 +141,11 @@
             for s in range(S):
                 j = cols[s, 0, i]
                 block = source[(j >> 3) - b + 2]
-                n = jnp.where(block < 2, which, 2 + (block >> 2))
+                n = 3 if which else block >> 1
                 at = count[n]
                 count[n] = at + 1
                 row = (n * CAP + FRONT + at) * WORDS
-                entries[row] = (which * NA + i * S + s) | ((block * F + (j & (F - 1))) << 8)
+                entries[row] = (i * S + s) | ((block * F + (j & (F - 1))) << 8)
                 for k in range(KP):
                     entries[row + 1 + k] = pc[k * np + j] + (i * NW - lowest)
             return 0
@@ -192,7 +192,7 @@
             ints(8),
             ints(SMALL),
             ints(F * KP * KD),
-            near((2 * NA, T, T), jnp.bfloat16),
+            near((NA, T, T), jnp.bfloat16),
             near((5, F, KP, T, T), jnp.bfloat16),
             near((F * KP, T, T), jnp.bfloat16),
             near((NS, T, T), jnp.float32),
@@ -261,87 +261,97 @@
     pl.run_scoped(body, *[pltpu.ACC(u % 2)((T, 2 * T), jnp.float32) for _ in range(4) for u in range(U)])
 
 
-def part_kernel(lists, blocks, with_tiles, halve, count, entries, *refs):
-    refs = list(refs)
-    their = refs.pop(0) if with_tiles else None
-    new = [refs.pop(0) for _ in blocks]
-    a, p, acc, sp = refs[-4:]
+OUTER, INNER, OWN = 0, C, 2 * C
+
+
+def form_rows(first, quarters, coded, accs, small, sidx, sp, pt, out, *ex):
+    for c in range(C):
+
+        def pair(r, _):
+            pr = small[PLIST + (first + c) * (F * KP) + r]
+            tile = pt[pr]
+            lhs = jnp.concatenate([tile, tile], axis=1)
+            for n, acc in enumerate(accs):
+                k = pr * KD + quarters[0] * KG + 2 * n
+                rhs = jnp.concatenate([sp[sidx[k]], sp[sidx[k + 1]]], axis=1)
+                pltpu.matmul_push_rhs(rhs, staging_register=(n // 2) % 2, mxu_index=n % 2)
+                pltpu.matmul_acc_lhs(acc, lhs, load_staged_rhs=(n // 2) % 2)
+            return 0
+
+        lax.fori_loop(0, small[PAIRS + first + c], pair, 0)
+        for n, acc in enumerate(accs):
+            x = pltpu.matmul_pop(acc)
+            for e in range(2):
+                q, k = divmod(2 * n + e, KG)
+                y = x[:, e * T : (e + 1) * T]
+                if coded:
+                    t = c * KG + k
+                    out[q, t * T : (t + 1) * T, :] = code(y, ex[0].at[q], t)
+                else:
+                    out[c, k] = y
+    if coded:
+        for q in range(len(quarters)):
+            out[q, ROWS:PACK, :] = ex[0][q].astype(jnp.int32).astype(jnp.int16)
+
+
+def part_kernel(n, blocks, count, entries, *refs):
+    new = refs[: len(blocks)]
+    a, p, acc, _ = refs[-4:]
     for block, ref in zip(blocks, new):
         p[block] = ref[...]
-    if with_tiles:
-        a[NA : 2 * NA] = their[...]
+    with_sets(lambda sets: entry_loop(n, count, entries, a, p, acc, sets))
+
+
+def part(n, tabs, state, blocks):
+    args = [("smem", x) for x in tabs] + [("vmem", x) for x in (*blocks.values(), *state)]
+    first = len(args) - len(state)
+    return call(
+        functools.partial(part_kernel, n, tuple(blocks)),
+        args,
+        [near(x.shape, x.dtype) for x in state],
+        alias={first + n: n for n in range(len(state))},
+    )
+
+
+def last_kernel(count, entries, small, sidx, their, pt, *refs):
+    _, p, acc, sp, out, ex = refs[-6:]
+
+    def halves(t, _):
+        for u in range(4):
+            n = t * 4 + u
+            x = acc[n]
+            hi = x.astype(jnp.bfloat16)
+            sp[n, 0:T, :] = hi
+            sp[n, T : 2 * T, :] = (x - hi.astype(jnp.float32)).astype(jnp.bfloat16)
+        return 0
 
     def work(sets):
-        for n in lists:
-            entry_loop(n, count, entries, a, p, acc, sets)
+        entry_loop(LISTS - 1, count, entries, their, p, acc, sets)
+        lax.fori_loop(0, F * NW // 4, halves, 0)
+        form_rows(OUTER, (0,), True, sets[0][0][:2], small, sidx, sp, pt, out, ex)
 
     with_sets(work)
-    if halve:
-        odd = lax.rem(place_of("row"), 2)
-        if halve == "most":
-            start, width = (1 - odd) * 3 * C, 4 * C
-        else:
-            start, width = odd * 4 * C, 3 * C
-
-        def halves(t, _):
-            first = (t >> 2) * NW + start + (t & 3) * (width // 4)
-            for u in range(width // 4):
-                x = acc[first + u]
-                hi = x.astype(jnp.bfloat16)
-                sp[first + u, 0:T, :] = hi
-                sp[first + u, T : 2 * T, :] = (x - hi.astype(jnp.float32)).astype(jnp.bfloat16)
-            return 0
-
-        lax.fori_loop(0, 4 * F, halves, 0)
-
-
-def part(lists, tabs, state, blocks, tiles=None, halve=None):
-    args = [("smem", x) for x in tabs]
-    if tiles is not None:
-        args.append(("vmem", tiles))
-    args += [("vmem", x) for x in blocks.values()]
-    outs = [near(x.shape, x.dtype) for x in state]
-    alias = {len(args) + n: n for n in range(len(state))}
-    args += [("vmem", x) for x in state]
-    return call(functools.partial(part_kernel, lists, tuple(blocks), tiles is not None, halve), args, outs, alias=alias)
-
-
-def coarse_kernel(first, quarters, coded, small, sidx, sp, pt, out, *refs):
+
+
+def last(lists, tabs, state, their, pt):
+    args = [("smem", x) for x in (*lists, *tabs)] + [("vmem", x) for x in (their, pt, *state)]
+    first = len(args) - len(state)
+    return call(
+        last_kernel,
+        args,
+        [near(x.shape, x.dtype) for x in state] + [near((1, PACK, T), jnp.int16)],
+        [pltpu.VMEM((1, SCALES, T), jnp.float32)],
+        alias={first + n: n for n in range(len(state))},
+    )[3:]
+
+
+def coarse_kernel(first, quarters, coded, small, sidx, sp, pt, out, *ex):
     def body(*accs):
         for acc in accs:
             pltpu.matmul_pop(acc)
-        for c in range(C):
-
-            def pair(r, _):
-                pr = small[PLIST + (first + c) * (F * KP) + r]
-                tile = pt[pr]
-                lhs = jnp.concatenate([tile, tile], axis=1)
-                for n, acc in enumerate(accs):
-                    k = pr * KD + quarters[0] * KG + 2 * n
-                    rhs = jnp.concatenate([sp[sidx[k]], sp[sidx[k + 1]]], axis=1)
-                    pltpu.matmul_push_rhs(rhs, staging_register=(n // 2) % 2, mxu_index=n % 2)
-                    pltpu.matmul_acc_lhs(acc, lhs, load_staged_rhs=(n // 2) % 2)
-                return 0
-
-            lax.fori_loop(0, small[PAIRS + first + c], pair, 0)
-            for n, acc in enumerate(accs):
-                x = pltpu.matmul_pop(acc)
-                for e in range(2):
-                    q, k = divmod(2 * n + e, KG)
-                    y = x[:, e * T : (e + 1) * T]
-                    if coded:
-                        t = c * KG + k
-                        out[q, t * T : (t + 1) * T, :] = code(y, refs[0].at[q], t)
-                    else:
-                        out[c, k] = y
-        if coded:
-            for q in range(len(quarters)):
-                out[q, ROWS:PACK, :] = refs[0][q].astype(jnp.int32).astype(jnp.int16)
+        form_rows(first, quarters, coded, accs, small, sidx, sp, pt, out, *ex)
 
     pl.run_scoped(body, *[pltpu.ACC(n % 2)((T, 2 * T), jnp.float32) for n in range(len(quarters) * KG // 2)])
-
-
-OUTER, INNER, OWN = 0, C, 2 * C
 
 
 def coarse(first, quarters, coded, tabs, sp, pt):
@@ -393,12 +403,42 @@
         out[c, k] = y
 
 
-def added(own, coded, out):
+def added(own, coded):
     return call(
         add_kernel,
         [("vmem", x) for x in (own, *coded)],
-        [("vmem", out)],
+        [near(own.shape, own.dtype)],
         [pltpu.VMEM((len(coded), SCALES, T), jnp.float32)],
+    )[0]
+
+
+def finish_kernel(own, *refs):
+    *coded, out_hbm, out, ex, sem = refs
+    coded = [x.at[x.shape[0] - 1] for x in coded]
+    for n, x in enumerate(coded):
+        scale(ex.at[n], x[ROWS:PACK, :])
+    copies = [pltpu.make_async_copy(out.at[c], out_hbm.at[c], sem.at[c]) for c in range(C)]
+    for t, c, k, rows in tiles():
+        y = own[c, k]
+        for n, x in enumerate(coded):
+            y = y + widen(x[rows, :]) * ex[n, t : t + 1, :]
+        out[c, k] = y
+        if k == KG - 1:
+            copies[c].start()
+    for copy in copies:
+        copy.wait()
+
+
+def finished(own, coded):
+    return call(
+        finish_kernel,
+        [("vmem", x) for x in (own, *coded)],
+        [("hbm", jax.ShapeDtypeStruct(own.shape, own.dtype))],
+        [
+            pltpu.VMEM(own.shape, own.dtype),
+            pltpu.VMEM((len(coded), SCALES, T), jnp.float32),
+            pltpu.SemaphoreType.DMA((C,)),
+        ],
     )[0]
 
 
@@ -441,13 +481,12 @@
         a_cols, their_cols, p_cols, c_cols, tiles, p_tiles
     )
     lists, state = (count, entries), (a, p, acc, sp)
-    state = part((0,), lists, state, {1: beside})
+    state = part(0, lists, state, {1: beside})
     far = along(turn, other)
-    state = part((1,), lists, state, {}, their_tiles)
-    state = part((2,), lists, state, {2: turn, 3: far}, halve="most")
-    sp = part((3,), lists, state, {4: keep}, halve="rest")[3]
+    state = part(1, lists, state, {2: turn, 3: far})
+    state = part(2, lists, state, {4: keep})
+    sp, x = last(lists, (small, sidx), state, their_tiles, pt)
     rows = ((small, sidx), sp, pt)
-    x = coarse(OUTER, (0,), True, *rows)
     outer = along(x, away)
     x = coarse(INNER, (0, 1), True, *rows)
     inner = along(x, other)
@@ -458,9 +497,8 @@
     x = coarse(OUTER, (1,), True, *rows)
     outer = along(x, away)
     own = coarse(OWN, (1,), False, *rows)
-    shape = (C, KG, T, T)
-    mine = added(own, (inner, outer), pltpu.VMEM(shape, jnp.float32))
-    return added(mine, (from_second, from_partner), jax.ShapeDtypeStruct(shape, jnp.float32))
+    mine = added(own, (inner, outer))
+    return finished(mine, (from_second, from_partner))
 
 
 def solution(mesh):

time: 89.4 us -> 88.9 us (level)
    pallas_call x13 -> x12, Pallas kernels: 23.9 us -> 23.4 us  [call(): pl.pallas_call(kernel, out_shape=[x for _, x in outs], in_specs=[spec[whe...]
  transfers between devices with their start and end apart: 11 -> 11, of which waited for: 4 -> 4; matrix products, arithmetic and copies ran while one was open for 0% -> 0% of each run, Pallas kernels for 21% -> 16%
where the time goes in v5:
time: 88.9 us; the launch traced here: 88.5 us
  starting transfers between devices  49.8 us (56%)
  Pallas kernels  23.4 us (26%)
  waiting for transfers between devices  15.1 us (17%)
    ppermute x7, starting transfers between devices, along(): return lax.ppermute(x, 'row', [(i, to(i) % n) for i in range(n)])  36.7 us
    pallas_call x12, Pallas kernels, call(): pl.pallas_call(kernel, out_shape=[x for _, x in outs], in_specs=[spec[whe...  23.4 us
    ppermute x4, starting transfers between devices, across(): lax.ppermute(x, ('grp', 'row'), [(g * rows + r, to(g, r % 2) * rows + r)...  13.1 us
    ppermute x7, waiting for transfers between devices, along(): return lax.ppermute(x, 'row', [(i, to(i) % n) for i in range(n)])  9.45 us
    ppermute x4, waiting for transfers between devices, across(): lax.ppermute(x, ('grp', 'row'), [(g * rows + r, to(g, r % 2) * rows + r)...  5.64 us
  transfers between devices with their start and end apart: 11, of which 4 were waited for; matrix products, arithmetic and copies ran while one was open for 0% of the time, Pallas kernels for 16%

profile of v5, /device:TPU:1, one launch (start us, length us, event | category | flops | bytes accessed | tf_op | source)
XLA Modules:
  0.0 88.5 jit_solution(17775064948748050886)
XLA Ops:
  0.0 4.4 %collective-permute-start.3 = (bf16[8,4,128,128]{3,2,1,0:T(8,128)(2,1)}, bf16[8,4,128,128]{3,2,1,0:T(8,128)(2,1)S(1)}, u32[]{:S(2)}, u32[]{:S(2)}) collective-permute-start(bf16[8,4,128,128]{3,2,1,0:T(8,128)(2,1)} %p_hbm.1), channel_id=1, source_target_pairs={{0,126},{1,3},{2,0},{3,5},{4,2},{5,7},{6,4},{7,9},{8,6},{9,11},{10... | collective-permute-start | bytes 3145736 | tf_op jit(solution)/shard_map/ppermute | solution.py:447
  4.4 4.6 %collective-permute-start.1 = (bf16[56,128,128]{2,1,0:T(8,128)(2,1)}, bf16[56,128,128]{2,1,0:T(8,128)(2,1)S(1)}, u32[]{:S(2)}, u32[]{:S(2)}) collective-permute-start(bf16[56,128,128]{2,1,0:T(8,128)(2,1)} %bitcast.6), channel_id=1, source_target_pairs={{0,128},{128,0},{256,384},{384,256},{1,385},{129,257},{257,129},{3... | collective-permute-start | bytes 5505032 | tf_op jit(solution)/shard_map/ppermute | solution.py:452
  9.0 11.5 %collective-permute-start.5 = (bf16[8,4,128,128]{3,2,1,0:T(8,128)(2,1)}, bf16[8,4,128,128]{3,2,1,0:T(8,128)(2,1)S(1)}, u32[]{:S(2)}, u32[]{:S(2)}) collective-permute-start(bf16[8,4,128,128]{3,2,1,0:T(8,128)(2,1)} %p_hbm.1), channel_id=1, source_target_pairs={{0,1},{1,0},{2,3},{3,2},{4,5},{5,4},{6,7},{7,6},{8,9},{9,8},{10,11... | collective-permute-start | bytes 3145736 | tf_op jit(solution)/shard_map/ppermute | solution.py:447
  20.5 6.0 %collective-permute-done.3.refs_0_ = bf16[8,4,128,128]{3,2,1,0:T(8,128)(2,1)S(1)} collective-permute-done((bf16[8,4,128,128]{3,2,1,0:T(8,128)(2,1)}, bf16[8,4,128,128]{3,2,1,0:T(8,128)(2,1)S(1)}, u32[]{:S(2)}, u32[]{:S(2)}) %collective-permute-start.3) | collective-permute-done | bytes 1048608 | tf_op jit(solution)/shard_map/ppermute | solution.py:447
  26.5 3.1 %collective-permute-start.4 = (bf16[8,4,128,128]{3,2,1,0:T(8,128)(2,1)S(1)}, bf16[8,4,128,128]{3,2,1,0:T(8,128)(2,1)S(1)}, u32[]{:S(2)}, u32[]{:S(2)}) collective-permute-start(bf16[8,4,128,128]{3,2,1,0:T(8,128)(2,1)S(1)} %collective-permute-done.3.refs_0_), channel_id=1, source_target_pairs={{0,1},{1,0},{2,3},{3,2},{4,5},{5,4},{6,7},{7,6},{8,9},{9,8},{10,11... | collective-permute-start | bytes 3145736 | tf_op jit(solution)/shard_map/ppermute | solution.py:447
  29.6 7.3 %collective-permute-start.2 = (bf16[8,4,128,128]{3,2,1,0:T(8,128)(2,1)}, bf16[8,4,128,128]{3,2,1,0:T(8,128)(2,1)S(1)}, u32[]{:S(2)}, u32[]{:S(2)}) collective-permute-start(bf16[8,4,128,128]{3,2,1,0:T(8,128)(2,1)} %p_hbm.1), channel_id=1, source_target_pairs={{0,2},{1,127},{2,4},{3,1},{4,6},{5,3},{6,8},{7,5},{8,10},{9,7},{10... | collective-permute-start | bytes 3145736 | tf_op jit(solution)/shard_map/ppermute | solution.py:447
  36.9 4.6 %collective-permute-start = (s32[8,1,7]{0,1,2:T(1,128)}, s32[8,1,7]{0,1,2:T(1,128)S(1)}, u32[]{:S(2)}, u32[]{:S(2)}) collective-permute-start(s32[8,1,7]{0,1,2:T(1,128)} %param.6), channel_id=1, source_target_pairs={{0,128},{128,0},{256,384},{384,256},{1,385},{129,257},{257,129},{3... | collective-permute-start | bytes 680 | tf_op jit(solution)/shard_map/ppermute | solution.py:452
  41.6 1.5 %collective-permute-done = s32[8,1,7]{0,1,2:T(1,128)S(1)} collective-permute-done((s32[8,1,7]{0,1,2:T(1,128)}, s32[8,1,7]{0,1,2:T(1,128)S(1)}, u32[]{:S(2)}, u32[]{:S(2)}) %collective-permute-start) | collective-permute-done | bytes 256 | tf_op jit(solution)/shard_map/ppermute | solution.py:452
  43.1 4.1 %shard_map.55 = (s32[1360]{0:T(1024)S(4)}, s32[8]{0:T(128)S(4)}, s32[400]{0:T(512)S(4)}, s32[256]{0:T(256)S(4)}, bf16[56,128,128]{2,1,0:T(8,128)(2,1)S(1)}, /*in...) custom-call(s32[7,1,8]{2,1,0:T(1,128)} %bitcast.10, ...), custom_call_target="tpu_custom_call" | custom-call | flops 20000000 | bytes 1000000 | tf_op jit(solution)/shard_map/pallas_call | solution.py:52
  47.2 0.0 collective-permute-done.5.refs_0_
  47.2 2.4 %shard_map.56 = (bf16[56,128,128]{2,1,0:T(8,128)(2,1)S(1)}, bf16[5,8,4,128,128]{4,3,2,1,0:T(8,128)(2,1)S(1)}, f32[226,128,128]{2,1,0:T(8,128)S(1)}, bf16[226,256,128]{2,1,0:T(8,128)(2,1)S(1)}) custom-call(s32[8]{0:T(128)S(4)} %get-tuple-element.30.count, ...), custom_call_target="tpu_custom_call", output_to_operand_aliasing={{0}: (3, {}), {1}: (4, {}), {2}: (5, {}), {3}: (6, {})} | custom-call | flops 20000000 | bytes 1000000 | tf_op jit(solution)/shard_map/pallas_call | solution.py:52
  49.6 0.0 collective-permute-done.4.refs_1_
  49.6 1.2 %shard_map.57 = (bf16[56,128,128]{2,1,0:T(8,128)(2,1)S(1)}, bf16[5,8,4,128,128]{4,3,2,1,0:T(8,128)(2,1)S(1)}, f32[226,128,128]{2,1,0:T(8,128)S(1)}, bf16[226,256,128]{2,1,0:T(8,128)(2,1)S(1)}) custom-call(s32[8]{0:T(128)S(4)} %get-tuple-element.30.count, ...), custom_call_target="tpu_custom_call", output_to_operand_aliasing={{0}: (4, {}), {1}: (5, {}), {2}: (6, {}), {3}: (7, {})} | custom-call | flops 20000000 | bytes 1000000 | tf_op jit(solution)/shard_map/pallas_call | solution.py:52
  50.8 0.0 collective-permute-done.2.refs_0_
  50.8 0.7 shard_map.58
  51.5 0.0 collective-permute-done.1.their
  51.6 6.6 %shard_map.59 = (bf16[56,128,128]{2,1,0:T(8,128)(2,1)S(1)}, bf16[5,8,4,128,128]{4,3,2,1,0:T(8,128)(2,1)S(1)}, f32[226,128,128]{2,1,0:T(8,128)S(1)}, bf16[226,256...) custom-call(s32[8]{0:T(128)S(4)} %get-tuple-element.30.count, ...), custom_call_target="tpu_custom_call", output_to_operand_aliasing={{0}: (6, {}), {1}: (7, {}), {2}: (8, {}), {3}: (9, {})} | custom-call | flops 20000000 | bytes 1000000 | tf_op jit(solution)/shard_map/pallas_call | solution.py:52
  58.2 1.9 %shard_map.61 = s16[2,2064,128]{2,1,0:T(8,128)(2,1)S(1)} custom-call(s32[400]{0:T(512)S(4)} %get-tuple-element.28.small, s32[256]{0:T(256)S(4)} %get-tuple-element.29.sidx, bf16[226,256,128]{2,1,0:T(8,128)(2,1)S(1)} %get-tuple-element.49.sp, bf16[32,128,128]{2,1,0:T(8,128)(2,1)S(1)} %get-tuple-element.32.pt), custom_call_target="tpu_custom_call" | custom-call | flops 20000000 | bytes 1000000 | tf_op jit(solution)/shard_map/pallas_call | solution.py:52
  60.1 1.9 %collective-permute-start.6 = (s16[2,2064,128]{2,1,0:T(8,128)(2,1)S(1)}, s16[2,2064,128]{2,1,0:T(8,128)(2,1)S(1)}, u32[]{:S(2)}, u32[]{:S(2)}) collective-permute-start(s16[2,2064,128]{2,1,0:T(8,128)(2,1)S(1)} %shard_map.61), channel_id=1, source_target_pairs={{0,1},{1,0},{2,3},{3,2},{4,5},{5,4},{6,7},{7,6},{8,9},{9,8},{10,11... | collective-permute-start | bytes 3170312 | tf_op jit(solution)/shard_map/ppermute | solution.py:447
  62.0 1.9 %collective-permute-start.9 = (s16[1,2064,128]{2,1,0:T(8,128)(2,1)S(1)}, s16[1,2064,128]{2,1,0:T(8,128)(2,1)S(1)}, u32[]{:S(2)}, u32[]{:S(2)}) collective-permute-start(s16[1,2064,128]{2,1,0:T(8,128)(2,1)S(1)} %get-tuple-element.50), channel_id=1, source_target_pairs={{0,127},{1,2},{2,1},{3,4},{4,3},{5,6},{6,5},{7,8},{8,7},{9,10},{10... | collective-permute-start | bytes 1585160 | tf_op jit(solution)/shard_map/ppermute | solution.py:447
  63.9 1.6 %shard_map.64 = s16[1,2064,128]{2,1,0:T(8,128)(2,1)S(1)} custom-call(s32[400]{0:T(512)S(4)} %get-tuple-element.28.small, s32[256]{0:T(256)S(4)} %get-tuple-element.29.sidx, bf16[226,256,128]{2,1,0:T(8,128)(2,1)S(1)} %get-tuple-element.49.sp, bf16[32,128,128]{2,1,0:T(8,128)(2,1)S(1)} %get-tuple-element.32.pt), custom_call_target="tpu_custom_call" | custom-call | flops 20000000 | bytes 1000000 | tf_op jit(solution)/shard_map/pallas_call | solution.py:52
  65.5 1.9 %collective-permute-start.8 = (s16[1,2064,128]{2,1,0:T(8,128)(2,1)S(1)}, s16[1,2064,128]{2,1,0:T(8,128)(2,1)S(1)}, u32[]{:S(2)}, u32[]{:S(2)}) collective-permute-start(s16[1,2064,128]{2,1,0:T(8,128)(2,1)S(1)} %shard_map.64), channel_id=1, source_target_pairs={{0,384},{128,256},{256,128},{384,0},{1,129},{129,1},{257,385},{385... | collective-permute-start | bytes 1585160 | tf_op jit(solution)/shard_map/ppermute | solution.py:452
  67.5 1.7 %shard_map.62 = s16[1,2064,128]{2,1,0:T(8,128)(2,1)S(1)} custom-call(s32[400]{0:T(512)S(4)} %get-tuple-element.28.small, s32[256]{0:T(256)S(4)} %get-tuple-element.29.sidx, bf16[226,256,128]{2,1,0:T(8,128)(2,1)S(1)} %get-tuple-element.49.sp, bf16[32,128,128]{2,1,0:T(8,128)(2,1)S(1)} %get-tuple-element.32.pt), custom_call_target="tpu_custom_call" | custom-call | flops 20000000 | bytes 1000000 | tf_op jit(solution)/shard_map/pallas_call | solution.py:52
  69.1 6.6 %collective-permute-start.7 = (s16[1,2064,128]{2,1,0:T(8,128)(2,1)S(1)}, s16[1,2064,128]{2,1,0:T(8,128)(2,1)S(1)}, u32[]{:S(2)}, u32[]{:S(2)}) collective-permute-start(s16[1,2064,128]{2,1,0:T(8,128)(2,1)S(1)} %shard_map.62), channel_id=1, source_target_pairs={{0,127},{1,2},{2,1},{3,4},{4,3},{5,6},{6,5},{7,8},{8,7},{9,10},{10... | collective-permute-start | bytes 1585160 | tf_op jit(solution)/shard_map/ppermute | solution.py:447
  75.7 0.0 collective-permute-done.9.outer
  75.8 0.0 collective-permute-done.6.refs_0_.inner
  75.8 0.4 shard_map.65
  76.2 1.9 %collective-permute-start.10 = (s16[1,2064,128]{2,1,0:T(8,128)(2,1)S(1)}, s16[1,2064,128]{2,1,0:T(8,128)(2,1)S(1)}, u32[]{:S(2)}, u32[]{:S(2)}) collective-permute-start(s16[1,2064,128]{2,1,0:T(8,128)(2,1)S(1)} %shard_map.65), channel_id=1, source_target_pairs={{0,128},{128,0},{256,384},{384,256},{1,385},{129,257},{257,129},{3... | collective-permute-start | bytes 1585160 | tf_op jit(solution)/shard_map/ppermute | solution.py:452
  78.1 1.4 %shard_map.60.own = f32[4,4,128,128]{3,2,1,0:T(8,128)S(1)} custom-call(s32[400]{0:T(512)S(4)} %get-tuple-element.28.small, s32[256]{0:T(256)S(4)} %get-tuple-element.29.sidx, bf16[226,256,128]{2,1,0:T(8,128)(2,1)S(1)} %get-tuple-element.49.sp, bf16[32,128,128]{2,1,0:T(8,128)(2,1)S(1)} %get-tuple-element.32.pt), custom_call_target="tpu_custom_call" | custom-call | flops 20000000 | bytes 1000000 | tf_op jit(solution)/shard_map/pallas_call | solution.py:52
  79.5 3.4 %collective-permute-done.7.refs_1_ = s16[1,2064,128]{2,1,0:T(8,128)(2,1)S(1)} collective-permute-done((s16[1,2064,128]{2,1,0:T(8,128)(2,1)S(1)}, s16[1,2064,128]{2,1,0:T(8,128)(2,1)S(1)}, u32[]{:S(2)}, u32[]{:S(2)}) %collective-permute-start.7) | collective-permute-done | bytes 528416 | tf_op jit(solution)/shard_map/ppermute | solution.py:447
  82.9 0.3 shard_map.63.own
  83.2 0.0 collective-permute-done.8.refs_0_
  83.2 4.2 %collective-permute-done.10.refs_1_ = s16[1,2064,128]{2,1,0:T(8,128)(2,1)S(1)} collective-permute-done((s16[1,2064,128]{2,1,0:T(8,128)(2,1)S(1)}, s16[1,2064,128]{2,1,0:T(8,128)(2,1)S(1)}, u32[]{:S(2)}, u32[]{:S(2)}) %collective-permute-start.10) | collective-permute-done | bytes 528416 | tf_op jit(solution)/shard_map/ppermute | solution.py:452
  87.4 1.1 %shard_map.66 = f32[4,4,128,128]{3,2,1,0:T(8,128)} custom-call(f32[4,4,128,128]{3,2,1,0:T(8,128)S(1)} %shard_map.63.own, s16[1,2064,128]{2,1,0:T(8,128)(2,1)S(1)} %collective-permute-done.8.refs_0_, s16[1,2064,128]{2,1,0:T(8,128)(2,1)S(1)} %collective-permute-done.10.refs_1_), custom_call_target="tpu_custom_call" | custom-call | flops 20000000 | bytes 1000000 | tf_op jit(solution)/shard_map/pallas_call | solution.py:52
Async XLA Ops:
  0.0 26.5 %collective-permute-start.3 = (bf16[8,4,128,128]{3,2,1,0:T(8,128)(2,1)}, bf16[8,4,128,128]{3,2,1,0:T(8,128)(2,1)S(1)}, u32[]{:S(2)}, u32[]{:S(2)}) collective-permute-start(bf16[8,4,128,128]{3,2,1,0:T(8,128)(2,1)} %p_hbm.1), channel_id=1, source_target_pairs={{0,126},{1,3},{2,0},{3,5},{4,2},{5,7},{6,4},{7,9},{8,6},{9,11},{10... | collective-permute-start | bytes 3145736 | tf_op jit(solution)/shard_map/ppermute | solution.py:447
  4.4 47.2 %collective-permute-start.1 = (bf16[56,128,128]{2,1,0:T(8,128)(2,1)}, bf16[56,128,128]{2,1,0:T(8,128)(2,1)S(1)}, u32[]{:S(2)}, u32[]{:S(2)}) collective-permute-start(bf16[56,128,128]{2,1,0:T(8,128)(2,1)} %bitcast.6), channel_id=1, source_target_pairs={{0,128},{128,0},{256,384},{384,256},{1,385},{129,257},{257,129},{3... | collective-permute-start | bytes 5505032 | tf_op jit(solution)/shard_map/ppermute | solution.py:452
  9.0 38.2 %collective-permute-start.5 = (bf16[8,4,128,128]{3,2,1,0:T(8,128)(2,1)}, bf16[8,4,128,128]{3,2,1,0:T(8,128)(2,1)S(1)}, u32[]{:S(2)}, u32[]{:S(2)}) collective-permute-start(bf16[8,4,128,128]{3,2,1,0:T(8,128)(2,1)} %p_hbm.1), channel_id=1, source_target_pairs={{0,1},{1,0},{2,3},{3,2},{4,5},{5,4},{6,7},{7,6},{8,9},{9,8},{10,11... | collective-permute-start | bytes 3145736 | tf_op jit(solution)/shard_map/ppermute | solution.py:447
  26.5 23.1 %collective-permute-start.4 = (bf16[8,4,128,128]{3,2,1,0:T(8,128)(2,1)S(1)}, bf16[8,4,128,128]{3,2,1,0:T(8,128)(2,1)S(1)}, u32[]{:S(2)}, u32[]{:S(2)}) collective-permute-start(bf16[8,4,128,128]{3,2,1,0:T(8,128)(2,1)S(1)} %collective-permute-done.3.refs_0_), channel_id=1, source_target_pairs={{0,1},{1,0},{2,3},{3,2},{4,5},{5,4},{6,7},{7,6},{8,9},{9,8},{10,11... | collective-permute-start | bytes 3145736 | tf_op jit(solution)/shard_map/ppermute | solution.py:447
  29.6 21.2 %collective-permute-start.2 = (bf16[8,4,128,128]{3,2,1,0:T(8,128)(2,1)}, bf16[8,4,128,128]{3,2,1,0:T(8,128)(2,1)S(1)}, u32[]{:S(2)}, u32[]{:S(2)}) collective-permute-start(bf16[8,4,128,128]{3,2,1,0:T(8,128)(2,1)} %p_hbm.1), channel_id=1, source_target_pairs={{0,2},{1,127},{2,4},{3,1},{4,6},{5,3},{6,8},{7,5},{8,10},{9,7},{10... | collective-permute-start | bytes 3145736 | tf_op jit(solution)/shard_map/ppermute | solution.py:447
  36.9 6.1 %collective-permute-start = (s32[8,1,7]{0,1,2:T(1,128)}, s32[8,1,7]{0,1,2:T(1,128)S(1)}, u32[]{:S(2)}, u32[]{:S(2)}) collective-permute-start(s32[8,1,7]{0,1,2:T(1,128)} %param.6), channel_id=1, source_target_pairs={{0,128},{128,0},{256,384},{384,256},{1,385},{129,257},{257,129},{3... | collective-permute-start | bytes 680 | tf_op jit(solution)/shard_map/ppermute | solution.py:452
  60.1 15.7 %collective-permute-start.6 = (s16[2,2064,128]{2,1,0:T(8,128)(2,1)S(1)}, s16[2,2064,128]{2,1,0:T(8,128)(2,1)S(1)}, u32[]{:S(2)}, u32[]{:S(2)}) collective-permute-start(s16[2,2064,128]{2,1,0:T(8,128)(2,1)S(1)} %shard_map.61), channel_id=1, source_target_pairs={{0,1},{1,0},{2,3},{3,2},{4,5},{5,4},{6,7},{7,6},{8,9},{9,8},{10,11... | collective-permute-start | bytes 3170312 | tf_op jit(solution)/shard_map/ppermute | solution.py:447
  62.0 13.7 %collective-permute-start.9 = (s16[1,2064,128]{2,1,0:T(8,128)(2,1)S(1)}, s16[1,2064,128]{2,1,0:T(8,128)(2,1)S(1)}, u32[]{:S(2)}, u32[]{:S(2)}) collective-permute-start(s16[1,2064,128]{2,1,0:T(8,128)(2,1)S(1)} %get-tuple-element.50), channel_id=1, source_target_pairs={{0,127},{1,2},{2,1},{3,4},{4,3},{5,6},{6,5},{7,8},{8,7},{9,10},{10... | collective-permute-start | bytes 1585160 | tf_op jit(solution)/shard_map/ppermute | solution.py:447
  65.5 17.7 %collective-permute-start.8 = (s16[1,2064,128]{2,1,0:T(8,128)(2,1)S(1)}, s16[1,2064,128]{2,1,0:T(8,128)(2,1)S(1)}, u32[]{:S(2)}, u32[]{:S(2)}) collective-permute-start(s16[1,2064,128]{2,1,0:T(8,128)(2,1)S(1)} %shard_map.64), channel_id=1, source_target_pairs={{0,384},{128,256},{256,128},{384,0},{1,129},{129,1},{257,385},{385... | collective-permute-start | bytes 1585160 | tf_op jit(solution)/shard_map/ppermute | solution.py:452
  69.1 13.8 %collective-permute-start.7 = (s16[1,2064,128]{2,1,0:T(8,128)(2,1)S(1)}, s16[1,2064,128]{2,1,0:T(8,128)(2,1)S(1)}, u32[]{:S(2)}, u32[]{:S(2)}) collective-permute-start(s16[1,2064,128]{2,1,0:T(8,128)(2,1)S(1)} %shard_map.62), channel_id=1, source_target_pairs={{0,127},{1,2},{2,1},{3,4},{4,3},{5,6},{6,5},{7,8},{8,7},{9,10},{10... | collective-permute-start | bytes 1585160 | tf_op jit(solution)/shard_map/ppermute | solution.py:447
  76.2 11.2 %collective-permute-start.10 = (s16[1,2064,128]{2,1,0:T(8,128)(2,1)S(1)}, s16[1,2064,128]{2,1,0:T(8,128)(2,1)S(1)}, u32[]{:S(2)}, u32[]{:S(2)}) collective-permute-start(s16[1,2064,128]{2,1,0:T(8,128)(2,1)S(1)} %shard_map.65), channel_id=1, source_target_pairs={{0,128},{128,0},{256,384},{384,256},{1,385},{129,257},{257,129},{3... | collective-permute-start | bytes 1585160 | tf_op jit(solution)/shard_map/ppermute | solution.py:452

commit v6 on v5

--- a/solution.py
+++ b/solution.py
@@ -328,7 +328,7 @@
     def work(sets):
         entry_loop(LISTS - 1, count, entries, their, p, acc, sets)
         lax.fori_loop(0, F * NW // 4, halves, 0)
-        form_rows(OUTER, (0,), True, sets[0][0][:2], small, sidx, sp, pt, out, ex)
+        form_rows(OWN, (0,), True, sets[0][0][:2], small, sidx, sp, pt, out, ex)
 
     with_sets(work)
 
@@ -371,24 +371,6 @@
 
 def scale(ref, rows):
     ref[...] = jnp.exp2(widen(rows)) * (1.0 / LEVELS)
-
-
-def cross_kernel(inner, outer, out, ex_i, ex_o, ex):
-    scale(ex_i, inner[0, ROWS:PACK, :])
-    scale(ex_o, outer[0, ROWS:PACK, :])
-    for t, c, k, rows in tiles():
-        x = widen(inner[0, rows, :]) * ex_i[t : t + 1, :] + widen(outer[0, rows, :]) * ex_o[t : t + 1, :]
-        out[0, rows, :] = code(x, ex, t)
-    out[0, ROWS:PACK, :] = ex[...].astype(jnp.int32).astype(jnp.int16)
-
-
-def crossed(inner, outer):
-    return call(
-        cross_kernel,
-        [("vmem", inner), ("vmem", outer)],
-        [near((1, PACK, T), jnp.int16)],
-        [pltpu.VMEM((SCALES, T), jnp.float32)] * 3,
-    )[0]
 
 
 def add_kernel(own, *refs):
@@ -444,13 +426,20 @@
 
 def along(x, to):
     n = lax.axis_size("row")
-    return lax.ppermute(x, "row", [(i, to(i) % n) for i in range(n)])
-
-
-def across(x, to):
+    return lax.ppermute(x, "row", [(i, to(i)) for i in range(n) if 0 <= to(i) < n])
+
+
+def across(x, to, row=lambda r: r):
     rows, n = lax.axis_size("row"), lax.axis_size("grp")
     return lax.ppermute(
-        x, ("grp", "row"), [(g * rows + r, to(g, r % 2) * rows + r) for r in range(rows) for g in range(n)]
+        x,
+        ("grp", "row"),
+        [
+            (g * rows + r, to(g, r % 2) * rows + row(r))
+            for r in range(rows)
+            for g in range(n)
+            if 0 <= row(r) < rows
+        ],
     )
 
 
@@ -487,18 +476,18 @@
     state = part(2, lists, state, {4: keep})
     sp, x = last(lists, (small, sidx), state, their_tiles, pt)
     rows = ((small, sidx), sp, pt)
-    outer = along(x, away)
-    x = coarse(INNER, (0, 1), True, *rows)
-    inner = along(x, other)
-    x = coarse(OWN, (0,), True, *rows)
     from_second = across(x, second)
-    x = crossed(inner, outer)
-    from_partner = across(x, partner)
+    x = coarse(OUTER, (0,), True, *rows)
+    from_skew = across(x, second, away)
+    x = coarse(INNER, (0,), True, *rows)
+    from_side = across(x, second, other)
     x = coarse(OUTER, (1,), True, *rows)
     outer = along(x, away)
+    x = coarse(INNER, (1,), True, *rows)
+    inner = along(x, other)
     own = coarse(OWN, (1,), False, *rows)
-    mine = added(own, (inner, outer))
-    return finished(mine, (from_second, from_partner))
+    mine = added(own, (from_second, from_side))
+    return finished(mine, (from_skew, outer, inner))
 
 
 def solution(mesh):

time: 88.9 us -> 89.9 us (1.011)
  the two profiles are of different devices: /device:TPU:1 before, /device:TPU:6 now
where the time goes in v6:
time: 89.9 us; the launch traced here: 88.8 us
  starting transfers between devices  44.2 us (49%)
  Pallas kernels  24.1 us (27%)
  waiting for transfers between devices  20.3 us (23%)
    ppermute x6, starting transfers between devices, along(): lax.ppermute(x, 'row', [(i, to(i)) for i in range(n) if 0 <= to(i) < n])  24.6 us
    pallas_call x12, Pallas kernels, call(): pl.pallas_call(kernel, out_shape=[x for _, x in outs], in_specs=[spec[whe...  24.1 us
    ppermute x5, starting transfers between devices, across(): lax.ppermute(x, ('grp', 'row'), [(g * rows + r, to(g, r % 2) * rows + row...  19.6 us
    ppermute x5, waiting for transfers between devices, across(): lax.ppermute(x, ('grp', 'row'), [(g * rows + r, to(g, r % 2) * rows + row...  11.6 us
    ppermute x6, waiting for transfers between devices, along(): lax.ppermute(x, 'row', [(i, to(i)) for i in range(n) if 0 <= to(i) < n])  8.75 us
  transfers between devices with their start and end apart: 11, of which 5 were waited for; matrix products, arithmetic and copies ran while one was open for 0% of the time, Pallas kernels for 15%

profile of v6, /device:TPU:6, one launch (start us, length us, event | category | flops | bytes accessed | tf_op | source)
XLA Modules:
  0.0 88.8 jit_solution(16962333885369437518)
XLA Ops:
  0.0 11.7 %collective-permute-start.3 = (bf16[8,4,128,128]{3,2,1,0:T(8,128)(2,1)}, bf16[8,4,128,128]{3,2,1,0:T(8,128)(2,1)S(1)}, u32[]{:S(2)}, u32[]{:S(2)}) collective-permute-start(bf16[8,4,128,128]{3,2,1,0:T(8,128)(2,1)} %p_hbm.1), channel_id=1, source_target_pairs={{1,3},{2,0},{3,5},{4,2},{5,7},{6,4},{7,9},{8,6},{9,11},{10,8},{11,... | collective-permute-start | bytes 3145736 | tf_op jit(solution)/shard_map/ppermute | solution.py:429
  11.7 3.5 %collective-permute-start.1 = (bf16[56,128,128]{2,1,0:T(8,128)(2,1)}, bf16[56,128,128]{2,1,0:T(8,128)(2,1)S(1)}, u32[]{:S(2)}, u32[]{:S(2)}) collective-permute-start(bf16[56,128,128]{2,1,0:T(8,128)(2,1)} %bitcast.6), channel_id=1, source_target_pairs={{0,128},{128,0},{256,384},{384,256},{1,385},{129,257},{257,129},{3... | collective-permute-start | bytes 5505032 | tf_op jit(solution)/shard_map/ppermute | solution.py:434
  15.2 1.9 %collective-permute-start.5 = (bf16[8,4,128,128]{3,2,1,0:T(8,128)(2,1)}, bf16[8,4,128,128]{3,2,1,0:T(8,128)(2,1)S(1)}, u32[]{:S(2)}, u32[]{:S(2)}) collective-permute-start(bf16[8,4,128,128]{3,2,1,0:T(8,128)(2,1)} %p_hbm.1), channel_id=1, source_target_pairs={{0,1},{1,0},{2,3},{3,2},{4,5},{5,4},{6,7},{7,6},{8,9},{9,8},{10,11... | collective-permute-start | bytes 3145736 | tf_op jit(solution)/shard_map/ppermute | solution.py:429
  17.1 7.2 %collective-permute-done.3.refs_0_ = bf16[8,4,128,128]{3,2,1,0:T(8,128)(2,1)S(1)} collective-permute-done((bf16[8,4,128,128]{3,2,1,0:T(8,128)(2,1)}, bf16[8,4,128,128]{3,2,1,0:T(8,128)(2,1)S(1)}, u32[]{:S(2)}, u32[]{:S(2)}) %collective-permute-start.3) | collective-permute-done | bytes 1048608 | tf_op jit(solution)/shard_map/ppermute | solution.py:429
  24.3 1.9 %collective-permute-start.4 = (bf16[8,4,128,128]{3,2,1,0:T(8,128)(2,1)S(1)}, bf16[8,4,128,128]{3,2,1,0:T(8,128)(2,1)S(1)}, u32[]{:S(2)}, u32[]{:S(2)}) collective-permute-start(bf16[8,4,128,128]{3,2,1,0:T(8,128)(2,1)S(1)} %collective-permute-done.3.refs_0_), channel_id=1, source_target_pairs={{0,1},{1,0},{2,3},{3,2},{4,5},{5,4},{6,7},{7,6},{8,9},{9,8},{10,11... | collective-permute-start | bytes 3145736 | tf_op jit(solution)/shard_map/ppermute | solution.py:429
  26.2 1.9 %collective-permute-start.2 = (bf16[8,4,128,128]{3,2,1,0:T(8,128)(2,1)}, bf16[8,4,128,128]{3,2,1,0:T(8,128)(2,1)S(1)}, u32[]{:S(2)}, u32[]{:S(2)}) collective-permute-start(bf16[8,4,128,128]{3,2,1,0:T(8,128)(2,1)} %p_hbm.1), channel_id=1, source_target_pairs={{0,2},{2,4},{3,1},{4,6},{5,3},{6,8},{7,5},{8,10},{9,7},{10,12},{11... | collective-permute-start | bytes 3145736 | tf_op jit(solution)/shard_map/ppermute | solution.py:429
  28.1 3.5 %collective-permute-start = (s32[8,1,7]{0,1,2:T(1,128)}, s32[8,1,7]{0,1,2:T(1,128)S(1)}, u32[]{:S(2)}, u32[]{:S(2)}) collective-permute-start(s32[8,1,7]{0,1,2:T(1,128)} %param.6), channel_id=1, source_target_pairs={{0,128},{128,0},{256,384},{384,256},{1,385},{129,257},{257,129},{3... | collective-permute-start | bytes 680 | tf_op jit(solution)/shard_map/ppermute | solution.py:434
  31.6 5.4 %collective-permute-done = s32[8,1,7]{0,1,2:T(1,128)S(1)} collective-permute-done((s32[8,1,7]{0,1,2:T(1,128)}, s32[8,1,7]{0,1,2:T(1,128)S(1)}, u32[]{:S(2)}, u32[]{:S(2)}) %collective-permute-start) | collective-permute-done | bytes 256 | tf_op jit(solution)/shard_map/ppermute | solution.py:434
  37.0 4.1 %shard_map.55 = (s32[1360]{0:T(1024)S(4)}, s32[8]{0:T(128)S(4)}, s32[400]{0:T(512)S(4)}, s32[256]{0:T(256)S(4)}, bf16[56,128,128]{2,1,0:T(8,128)(2,1)S(1)}, /*in...) custom-call(s32[7,1,8]{2,1,0:T(1,128)} %bitcast.10, ...), custom_call_target="tpu_custom_call" | custom-call | flops 20000000 | bytes 1000000 | tf_op jit(solution)/shard_map/pallas_call | solution.py:52
  41.2 0.0 collective-permute-done.5.refs_0_
  41.2 1.6 %shard_map.56 = (bf16[56,128,128]{2,1,0:T(8,128)(2,1)S(1)}, bf16[5,8,4,128,128]{4,3,2,1,0:T(8,128)(2,1)S(1)}, f32[226,128,128]{2,1,0:T(8,128)S(1)}, bf16[226,256,128]{2,1,0:T(8,128)(2,1)S(1)}) custom-call(s32[8]{0:T(128)S(4)} %get-tuple-element.30.count, ...), custom_call_target="tpu_custom_call", output_to_operand_aliasing={{0}: (3, {}), {1}: (4, {}), {2}: (5, {}), {3}: (6, {})} | custom-call | flops 20000000 | bytes 1000000 | tf_op jit(solution)/shard_map/pallas_call | solution.py:52
  42.8 0.0 collective-permute-done.4.refs_1_
  42.8 2.0 %shard_map.57 = (bf16[56,128,128]{2,1,0:T(8,128)(2,1)S(1)}, bf16[5,8,4,128,128]{4,3,2,1,0:T(8,128)(2,1)S(1)}, f32[226,128,128]{2,1,0:T(8,128)S(1)}, bf16[226,256,128]{2,1,0:T(8,128)(2,1)S(1)}) custom-call(s32[8]{0:T(128)S(4)} %get-tuple-element.30.count, ...), custom_call_target="tpu_custom_call", output_to_operand_aliasing={{0}: (4, {}), {1}: (5, {}), {2}: (6, {}), {3}: (7, {})} | custom-call | flops 20000000 | bytes 1000000 | tf_op jit(solution)/shard_map/pallas_call | solution.py:52
  44.8 0.8 collective-permute-done.2.refs_0_
  45.6 1.1 %shard_map.58 = (bf16[56,128,128]{2,1,0:T(8,128)(2,1)S(1)}, bf16[5,8,4,128,128]{4,3,2,1,0:T(8,128)(2,1)S(1)}, f32[226,128,128]{2,1,0:T(8,128)S(1)}, bf16[226,256,128]{2,1,0:T(8,128)(2,1)S(1)}) custom-call(s32[8]{0:T(128)S(4)} %get-tuple-element.30.count, ...), custom_call_target="tpu_custom_call", output_to_operand_aliasing={{0}: (3, {}), {1}: (4, {}), {2}: (5, {}), {3}: (6, {})} | custom-call | flops 20000000 | bytes 1000000 | tf_op jit(solution)/shard_map/pallas_call | solution.py:52
  46.7 0.0 collective-permute-done.1.their
  46.7 6.4 %shard_map.59 = (bf16[56,128,128]{2,1,0:T(8,128)(2,1)S(1)}, bf16[5,8,4,128,128]{4,3,2,1,0:T(8,128)(2,1)S(1)}, f32[226,128,128]{2,1,0:T(8,128)S(1)}, bf16[226,256...) custom-call(s32[8]{0:T(128)S(4)} %get-tuple-element.30.count, ...), custom_call_target="tpu_custom_call", output_to_operand_aliasing={{0}: (6, {}), {1}: (7, {}), {2}: (8, {}), {3}: (9, {})} | custom-call | flops 20000000 | bytes 1000000 | tf_op jit(solution)/shard_map/pallas_call | solution.py:52
  53.1 1.5 %shard_map.65 = s16[1,2064,128]{2,1,0:T(8,128)(2,1)S(1)} custom-call(s32[400]{0:T(512)S(4)} %get-tuple-element.28.small, s32[256]{0:T(256)S(4)} %get-tuple-element.29.sidx, bf16[226,256,128]{2,1,0:T(8,128)(2,1)S(1)} %get-tuple-element.49.sp, bf16[32,128,128]{2,1,0:T(8,128)(2,1)S(1)} %get-tuple-element.32.pt), custom_call_target="tpu_custom_call" | custom-call | flops 20000000 | bytes 1000000 | tf_op jit(solution)/shard_map/pallas_call | solution.py:52
  54.6 1.5 %shard_map.61 = s16[1,2064,128]{2,1,0:T(8,128)(2,1)S(1)} custom-call(s32[400]{0:T(512)S(4)} %get-tuple-element.28.small, s32[256]{0:T(256)S(4)} %get-tuple-element.29.sidx, bf16[226,256,128]{2,1,0:T(8,128)(2,1)S(1)} %get-tuple-element.49.sp, bf16[32,128,128]{2,1,0:T(8,128)(2,1)S(1)} %get-tuple-element.32.pt), custom_call_target="tpu_custom_call" | custom-call | flops 20000000 | bytes 1000000 | tf_op jit(solution)/shard_map/pallas_call | solution.py:52
  56.1 5.6 %collective-permute-start.7 = (s16[1,2064,128]{2,1,0:T(8,128)(2,1)S(1)}, s16[1,2064,128]{2,1,0:T(8,128)(2,1)S(1)}, u32[]{:S(2)}, u32[]{:S(2)}) collective-permute-start(s16[1,2064,128]{2,1,0:T(8,128)(2,1)S(1)} %shard_map.61), channel_id=1, source_target_pairs={{0,385},{128,257},{256,129},{384,1},{1,128},{129,0},{257,384},{385... | collective-permute-start | bytes 1585160 | tf_op jit(solution)/shard_map/ppermute | solution.py:434
  61.7 1.9 %collective-permute-start.6 = (s16[1,2064,128]{2,1,0:T(8,128)(2,1)S(1)}, s16[1,2064,128]{2,1,0:T(8,128)(2,1)S(1)}, u32[]{:S(2)}, u32[]{:S(2)}) collective-permute-start(s16[1,2064,128]{2,1,0:T(8,128)(2,1)S(1)} %get-tuple-element.50), channel_id=1, source_target_pairs={{0,384},{128,256},{256,128},{384,0},{1,129},{129,1},{257,385},{385... | collective-permute-start | bytes 1585160 | tf_op jit(solution)/shard_map/ppermute | solution.py:434
  63.7 1.6 %shard_map.64 = s16[1,2064,128]{2,1,0:T(8,128)(2,1)S(1)} custom-call(s32[400]{0:T(512)S(4)} %get-tuple-element.28.small, s32[256]{0:T(256)S(4)} %get-tuple-element.29.sidx, bf16[226,256,128]{2,1,0:T(8,128)(2,1)S(1)} %get-tuple-element.49.sp, bf16[32,128,128]{2,1,0:T(8,128)(2,1)S(1)} %get-tuple-element.32.pt), custom_call_target="tpu_custom_call" | custom-call | flops 20000000 | bytes 1000000 | tf_op jit(solution)/shard_map/pallas_call | solution.py:52
  65.3 1.6 %shard_map.63 = s16[1,2064,128]{2,1,0:T(8,128)(2,1)S(1)} custom-call(s32[400]{0:T(512)S(4)} %get-tuple-element.28.small, s32[256]{0:T(256)S(4)} %get-tuple-element.29.sidx, bf16[226,256,128]{2,1,0:T(8,128)(2,1)S(1)} %get-tuple-element.49.sp, bf16[32,128,128]{2,1,0:T(8,128)(2,1)S(1)} %get-tuple-element.32.pt), custom_call_target="tpu_custom_call" | custom-call | flops 20000000 | bytes 1000000 | tf_op jit(solution)/shard_map/pallas_call | solution.py:52
  66.9 1.9 %collective-permute-start.10 = (s16[1,2064,128]{2,1,0:T(8,128)(2,1)S(1)}, s16[1,2064,128]{2,1,0:T(8,128)(2,1)S(1)}, u32[]{:S(2)}, u32[]{:S(2)}) collective-permute-start(s16[1,2064,128]{2,1,0:T(8,128)(2,1)S(1)} %shard_map.65), channel_id=1, source_target_pairs={{0,1},{1,0},{2,3},{3,2},{4,5},{5,4},{6,7},{7,6},{8,9},{9,8},{10,11... | collective-permute-start | bytes 1585160 | tf_op jit(solution)/shard_map/ppermute | solution.py:429
  68.8 5.2 %collective-permute-start.9 = (s16[1,2064,128]{2,1,0:T(8,128)(2,1)S(1)}, s16[1,2064,128]{2,1,0:T(8,128)(2,1)S(1)}, u32[]{:S(2)}, u32[]{:S(2)}) collective-permute-start(s16[1,2064,128]{2,1,0:T(8,128)(2,1)S(1)} %shard_map.64), channel_id=1, source_target_pairs={{1,2},{2,1},{3,4},{4,3},{5,6},{6,5},{7,8},{8,7},{9,10},{10,9},{11,... | collective-permute-start | bytes 1585160 | tf_op jit(solution)/shard_map/ppermute | solution.py:429
  74.0 5.1 %collective-permute-start.8 = (s16[1,2064,128]{2,1,0:T(8,128)(2,1)S(1)}, s16[1,2064,128]{2,1,0:T(8,128)(2,1)S(1)}, u32[]{:S(2)}, u32[]{:S(2)}) collective-permute-start(s16[1,2064,128]{2,1,0:T(8,128)(2,1)S(1)} %shard_map.63), channel_id=1, source_target_pairs={{1,130},{129,2},{257,386},{385,258},{2,385},{130,257},{258,129},{3... | collective-permute-start | bytes 1585160 | tf_op jit(solution)/shard_map/ppermute | solution.py:434
  79.2 1.2 %shard_map.60.own = f32[4,4,128,128]{3,2,1,0:T(8,128)S(1)} custom-call(s32[400]{0:T(512)S(4)} %get-tuple-element.28.small, s32[256]{0:T(256)S(4)} %get-tuple-element.29.sidx, bf16[226,256,128]{2,1,0:T(8,128)(2,1)S(1)} %get-tuple-element.49.sp, bf16[32,128,128]{2,1,0:T(8,128)(2,1)S(1)} %get-tuple-element.32.pt), custom_call_target="tpu_custom_call" | custom-call | flops 20000000 | bytes 1000000 | tf_op jit(solution)/shard_map/pallas_call | solution.py:52
  80.4 0.0 collective-permute-done.7.refs_1_
  80.4 0.0 collective-permute-done.6.refs_0_
  80.4 0.3 shard_map.62.own
  80.7 0.0 collective-permute-done.10.refs_2_
  80.7 0.8 collective-permute-done.9.refs_1_
  81.5 6.1 %collective-permute-done.8.refs_0_ = s16[1,2064,128]{2,1,0:T(8,128)(2,1)S(1)} collective-permute-done((s16[1,2064,128]{2,1,0:T(8,128)(2,1)S(1)}, s16[1,2064,128]{2,1,0:T(8,128)(2,1)S(1)}, u32[]{:S(2)}, u32[]{:S(2)}) %collective-permute-start.8) | collective-permute-done | bytes 528416 | tf_op jit(solution)/shard_map/ppermute | solution.py:434
  87.6 1.2 %shard_map.66 = f32[4,4,128,128]{3,2,1,0:T(8,128)} custom-call(f32[4,4,128,128]{3,2,1,0:T(8,128)S(1)} %shard_map.62.own, s16[1,2064,128]{2,1,0:T(8,128)(2,1)S(1)} %collective-permute-done.8.refs_0_, s16[1,2064,128]{2,1,0:T(8,128)(2,1)S(1)} %collective-permute-done.9.refs_1_, s16[1,2064,128]{2,1,0:T(8,128)(2,1)S(1)} %collective-permute-done.10.refs_2_), custom_call_target="tpu_custom_call" | custom-call | flops 20000000 | bytes 1000000 | tf_op jit(solution)/shard_map/pallas_call | solution.py:52
Async XLA Ops:
  0.0 24.3 %collective-permute-start.3 = (bf16[8,4,128,128]{3,2,1,0:T(8,128)(2,1)}, bf16[8,4,128,128]{3,2,1,0:T(8,128)(2,1)S(1)}, u32[]{:S(2)}, u32[]{:S(2)}) collective-permute-start(bf16[8,4,128,128]{3,2,1,0:T(8,128)(2,1)} %p_hbm.1), channel_id=1, source_target_pairs={{1,3},{2,0},{3,5},{4,2},{5,7},{6,4},{7,9},{8,6},{9,11},{10,8},{11,... | collective-permute-start | bytes 3145736 | tf_op jit(solution)/shard_map/ppermute | solution.py:429
  11.7 35.1 %collective-permute-start.1 = (bf16[56,128,128]{2,1,0:T(8,128)(2,1)}, bf16[56,128,128]{2,1,0:T(8,128)(2,1)S(1)}, u32[]{:S(2)}, u32[]{:S(2)}) collective-permute-start(bf16[56,128,128]{2,1,0:T(8,128)(2,1)} %bitcast.6), channel_id=1, source_target_pairs={{0,128},{128,0},{256,384},{384,256},{1,385},{129,257},{257,129},{3... | collective-permute-start | bytes 5505032 | tf_op jit(solution)/shard_map/ppermute | solution.py:434
  15.2 26.0 %collective-permute-start.5 = (bf16[8,4,128,128]{3,2,1,0:T(8,128)(2,1)}, bf16[8,4,128,128]{3,2,1,0:T(8,128)(2,1)S(1)}, u32[]{:S(2)}, u32[]{:S(2)}) collective-permute-start(bf16[8,4,128,128]{3,2,1,0:T(8,128)(2,1)} %p_hbm.1), channel_id=1, source_target_pairs={{0,1},{1,0},{2,3},{3,2},{4,5},{5,4},{6,7},{7,6},{8,9},{9,8},{10,11... | collective-permute-start | bytes 3145736 | tf_op jit(solution)/shard_map/ppermute | solution.py:429
  24.3 18.5 %collective-permute-start.4 = (bf16[8,4,128,128]{3,2,1,0:T(8,128)(2,1)S(1)}, bf16[8,4,128,128]{3,2,1,0:T(8,128)(2,1)S(1)}, u32[]{:S(2)}, u32[]{:S(2)}) collective-permute-start(bf16[8,4,128,128]{3,2,1,0:T(8,128)(2,1)S(1)} %collective-permute-done.3.refs_0_), channel_id=1, source_target_pairs={{0,1},{1,0},{2,3},{3,2},{4,5},{5,4},{6,7},{7,6},{8,9},{9,8},{10,11... | collective-permute-start | bytes 3145736 | tf_op jit(solution)/shard_map/ppermute | solution.py:429
  26.2 19.4 %collective-permute-start.2 = (bf16[8,4,128,128]{3,2,1,0:T(8,128)(2,1)}, bf16[8,4,128,128]{3,2,1,0:T(8,128)(2,1)S(1)}, u32[]{:S(2)}, u32[]{:S(2)}) collective-permute-start(bf16[8,4,128,128]{3,2,1,0:T(8,128)(2,1)} %p_hbm.1), channel_id=1, source_target_pairs={{0,2},{2,4},{3,1},{4,6},{5,3},{6,8},{7,5},{8,10},{9,7},{10,12},{11... | collective-permute-start | bytes 3145736 | tf_op jit(solution)/shard_map/ppermute | solution.py:429
  28.1 8.9 %collective-permute-start = (s32[8,1,7]{0,1,2:T(1,128)}, s32[8,1,7]{0,1,2:T(1,128)S(1)}, u32[]{:S(2)}, u32[]{:S(2)}) collective-permute-start(s32[8,1,7]{0,1,2:T(1,128)} %param.6), channel_id=1, source_target_pairs={{0,128},{128,0},{256,384},{384,256},{1,385},{129,257},{257,129},{3... | collective-permute-start | bytes 680 | tf_op jit(solution)/shard_map/ppermute | solution.py:434
  56.1 24.3 %collective-permute-start.7 = (s16[1,2064,128]{2,1,0:T(8,128)(2,1)S(1)}, s16[1,2064,128]{2,1,0:T(8,128)(2,1)S(1)}, u32[]{:S(2)}, u32[]{:S(2)}) collective-permute-start(s16[1,2064,128]{2,1,0:T(8,128)(2,1)S(1)} %shard_map.61), channel_id=1, source_target_pairs={{0,385},{128,257},{256,129},{384,1},{1,128},{129,0},{257,384},{385... | collective-permute-start | bytes 1585160 | tf_op jit(solution)/shard_map/ppermute | solution.py:434
  61.7 18.7 %collective-permute-start.6 = (s16[1,2064,128]{2,1,0:T(8,128)(2,1)S(1)}, s16[1,2064,128]{2,1,0:T(8,128)(2,1)S(1)}, u32[]{:S(2)}, u32[]{:S(2)}) collective-permute-start(s16[1,2064,128]{2,1,0:T(8,128)(2,1)S(1)} %get-tuple-element.50), channel_id=1, source_target_pairs={{0,384},{128,256},{256,128},{384,0},{1,129},{129,1},{257,385},{385... | collective-permute-start | bytes 1585160 | tf_op jit(solution)/shard_map/ppermute | solution.py:434
  66.9 13.8 %collective-permute-start.10 = (s16[1,2064,128]{2,1,0:T(8,128)(2,1)S(1)}, s16[1,2064,128]{2,1,0:T(8,128)(2,1)S(1)}, u32[]{:S(2)}, u32[]{:S(2)}) collective-permute-start(s16[1,2064,128]{2,1,0:T(8,128)(2,1)S(1)} %shard_map.65), channel_id=1, source_target_pairs={{0,1},{1,0},{2,3},{3,2},{4,5},{5,4},{6,7},{7,6},{8,9},{9,8},{10,11... | collective-permute-start | bytes 1585160 | tf_op jit(solution)/shard_map/ppermute | solution.py:429
  68.8 12.7 %collective-permute-start.9 = (s16[1,2064,128]{2,1,0:T(8,128)(2,1)S(1)}, s16[1,2064,128]{2,1,0:T(8,128)(2,1)S(1)}, u32[]{:S(2)}, u32[]{:S(2)}) collective-permute-start(s16[1,2064,128]{2,1,0:T(8,128)(2,1)S(1)} %shard_map.64), channel_id=1, source_target_pairs={{1,2},{2,1},{3,4},{4,3},{5,6},{6,5},{7,8},{8,7},{9,10},{10,9},{11,... | collective-permute-start | bytes 1585160 | tf_op jit(solution)/shard_map/ppermute | solution.py:429
  74.0 13.6 %collective-permute-start.8 = (s16[1,2064,128]{2,1,0:T(8,128)(2,1)S(1)}, s16[1,2064,128]{2,1,0:T(8,128)(2,1)S(1)}, u32[]{:S(2)}, u32[]{:S(2)}) collective-permute-start(s16[1,2064,128]{2,1,0:T(8,128)(2,1)S(1)} %shard_map.63), channel_id=1, source_target_pairs={{1,130},{129,2},{257,386},{385,258},{2,385},{130,257},{258,129},{3... | collective-permute-start | bytes 1585160 | tf_op jit(solution)/shard_map/ppermute | solution.py:434

commit v7 on v6

--- a/solution.py
+++ b/solution.py
@@ -93,7 +93,7 @@
 
 def plan_kernel(
     mine_hbm, their_vmem, pc_hbm, cc_hbm, tiles_hbm, p_hbm,
-    entries, count, small, sidx, tiles, p, pt, acc, sp,
+    entries, count, small, sidx, tiles, p, pt, acc,
     source, mine, their, pc, cc, sem,
 ):
     b, g = place_of("row"), place_of("grp")
@@ -131,7 +131,7 @@
         return 0
 
     lax.fori_loop(0, F * NW // 4, clear, 0)
-    sp[ZERO] = jnp.zeros((2 * T, T), jnp.bfloat16)
+    acc[ZERO] = jnp.zeros((T, T), jnp.float32)
     for c in copies[:-1]:
         c.wait()
 
@@ -196,7 +196,6 @@
             near((5, F, KP, T, T), jnp.bfloat16),
             near((F * KP, T, T), jnp.bfloat16),
             near((NS, T, T), jnp.float32),
-            near((NS, 2 * T, T), jnp.bfloat16),
         ],
         [
             smem(8),
@@ -264,7 +263,12 @@
 OUTER, INNER, OWN = 0, C, 2 * C
 
 
-def form_rows(first, quarters, coded, accs, small, sidx, sp, pt, out, *ex):
+def terms(x):
+    hi = x.astype(jnp.bfloat16)
+    return jnp.concatenate([hi, (x - hi.astype(jnp.float32)).astype(jnp.bfloat16)], axis=0)
+
+
+def form_rows(first, quarters, coded, accs, small, sidx, sums, pt, out, *ex):
     for c in range(C):
 
         def pair(r, _):
@@ -273,7 +277,7 @@
             lhs = jnp.concatenate([tile, tile], axis=1)
             for n, acc in enumerate(accs):
                 k = pr * KD + quarters[0] * KG + 2 * n
-                rhs = jnp.concatenate([sp[sidx[k]], sp[sidx[k + 1]]], axis=1)
+                rhs = jnp.concatenate([terms(sums[sidx[k]]), terms(sums[sidx[k + 1]])], axis=1)
                 pltpu.matmul_push_rhs(rhs, staging_register=(n // 2) % 2, mxu_index=n % 2)
                 pltpu.matmul_acc_lhs(acc, lhs, load_staged_rhs=(n // 2) % 2)
             return 0
@@ -296,7 +300,7 @@
 
 def part_kernel(n, blocks, count, entries, *refs):
     new = refs[: len(blocks)]
-    a, p, acc, _ = refs[-4:]
+    a, p, acc = refs[-3:]
     for block, ref in zip(blocks, new):
         p[block] = ref[...]
     with_sets(lambda sets: entry_loop(n, count, entries, a, p, acc, sets))
@@ -314,21 +318,11 @@
 
 
 def last_kernel(count, entries, small, sidx, their, pt, *refs):
-    _, p, acc, sp, out, ex = refs[-6:]
-
-    def halves(t, _):
-        for u in range(4):
-            n = t * 4 + u
-            x = acc[n]
-            hi = x.astype(jnp.bfloat16)
-            sp[n, 0:T, :] = hi
-            sp[n, T : 2 * T, :] = (x - hi.astype(jnp.float32)).astype(jnp.bfloat16)
-        return 0
+    _, p, acc, out, ex = refs[-5:]
 
     def work(sets):
         entry_loop(LISTS - 1, count, entries, their, p, acc, sets)
-        lax.fori_loop(0, F * NW // 4, halves, 0)
-        form_rows(OWN, (0,), True, sets[0][0][:2], small, sidx, sp, pt, out, ex)
+        form_rows(OWN, (0,), True, sets[0][0][:2], small, sidx, acc, pt, out, ex)
 
     with_sets(work)
 
@@ -342,24 +336,24 @@
         [near(x.shape, x.dtype) for x in state] + [near((1, PACK, T), jnp.int16)],
         [pltpu.VMEM((1, SCALES, T), jnp.float32)],
         alias={first + n: n for n in range(len(state))},
-    )[3:]
-
-
-def coarse_kernel(first, quarters, coded, small, sidx, sp, pt, out, *ex):
+    )[2:]
+
+
+def coarse_kernel(first, quarters, coded, small, sidx, sums, pt, out, *ex):
     def body(*accs):
         for acc in accs:
             pltpu.matmul_pop(acc)
-        form_rows(first, quarters, coded, accs, small, sidx, sp, pt, out, *ex)
+        form_rows(first, quarters, coded, accs, small, sidx, sums, pt, out, *ex)
 
     pl.run_scoped(body, *[pltpu.ACC(n % 2)((T, 2 * T), jnp.float32) for n in range(len(quarters) * KG // 2)])
 
 
-def coarse(first, quarters, coded, tabs, sp, pt):
+def coarse(first, quarters, coded, tabs, sums, pt):
     n = len(quarters)
     out = near((n, PACK, T), jnp.int16) if coded else near((C, KG, T, T), jnp.float32)
     return call(
         functools.partial(coarse_kernel, first, quarters, coded),
-        [("smem", tabs[0]), ("smem", tabs[1]), ("vmem", sp), ("vmem", pt)],
+        [("smem", tabs[0]), ("smem", tabs[1]), ("vmem", sums), ("vmem", pt)],
         [out],
         [pltpu.VMEM((n, SCALES, T), jnp.float32)] if coded else [],
     )[0]
@@ -466,16 +460,16 @@
     turn = along(p_tiles, lambda i: i - 2 if i % 2 == 0 else i + 2)
     beside = along(p_tiles, other)
     keep = along(p_tiles, lambda i: i + 2 if i % 2 == 0 else i - 2)
-    entries, count, small, sidx, a, p, pt, acc, sp = planned(
+    entries, count, small, sidx, a, p, pt, acc = planned(
         a_cols, their_cols, p_cols, c_cols, tiles, p_tiles
     )
-    lists, state = (count, entries), (a, p, acc, sp)
+    lists, state = (count, entries), (a, p, acc)
     state = part(0, lists, state, {1: beside})
     far = along(turn, other)
     state = part(1, lists, state, {2: turn, 3: far})
     state = part(2, lists, state, {4: keep})
-    sp, x = last(lists, (small, sidx), state, their_tiles, pt)
-    rows = ((small, sidx), sp, pt)
+    sums, x = last(lists, (small, sidx), state, their_tiles, pt)
+    rows = ((small, sidx), sums, pt)
     from_second = across(x, second)
     x = coarse(OUTER, (0,), True, *rows)
     from_skew = across(x, second, away)

time: 89.9 us -> 88.3 us (0.982)
  Pallas kernels: 24.1 us -> 22.5 us
    pallas_call x12, Pallas kernels: 24.1 us -> 22.5 us  [call(): pl.pallas_call(kernel, out_shape=[x for _, x in outs], in_specs=[spec[whe...]
  transfers between devices with their start and end apart: 11 -> 11, of which waited for: 5 -> 5; matrix products, arithmetic and copies ran while one was open for 0% -> 0% of each run, Pallas kernels for 15% -> 16%
where the time goes in v7:
time: 88.3 us; the launch traced here: 87.1 us
  starting transfers between devices  44.2 us (50%)
  Pallas kernels  22.5 us (25%)
  waiting for transfers between devices  20.2 us (23%)
    ppermute x6, starting transfers between devices, along(): lax.ppermute(x, 'row', [(i, to(i)) for i in range(n) if 0 <= to(i) < n])  24.5 us
    pallas_call x12, Pallas kernels, call(): pl.pallas_call(kernel, out_shape=[x for _, x in outs], in_specs=[spec[whe...  22.5 us
    ppermute x5, starting transfers between devices, across(): lax.ppermute(x, ('grp', 'row'), [(g * rows + r, to(g, r % 2) * rows + row...  19.7 us
    ppermute x5, waiting for transfers between devices, across(): lax.ppermute(x, ('grp', 'row'), [(g * rows + r, to(g, r % 2) * rows + row...  11.5 us
    ppermute x6, waiting for transfers between devices, along(): lax.ppermute(x, 'row', [(i, to(i)) for i in range(n) if 0 <= to(i) < n])  8.71 us
  transfers between devices with their start and end apart: 11, of which 5 were waited for; matrix products, arithmetic and copies ran while one was open for 0% of the time, Pallas kernels for 16%

profile of v7, /device:TPU:6, one launch (start us, length us, event | category | flops | bytes accessed | tf_op | source)
XLA Modules:
  0.0 87.1 jit_solution(6281422181320595080)
XLA Ops:
  0.0 11.7 %collective-permute-start.3 = (bf16[8,4,128,128]{3,2,1,0:T(8,128)(2,1)}, bf16[8,4,128,128]{3,2,1,0:T(8,128)(2,1)S(1)}, u32[]{:S(2)}, u32[]{:S(2)}) collective-permute-start(bf16[8,4,128,128]{3,2,1,0:T(8,128)(2,1)} %p_hbm.1), channel_id=1, source_target_pairs={{1,3},{2,0},{3,5},{4,2},{5,7},{6,4},{7,9},{8,6},{9,11},{10,8},{11,... | collective-permute-start | bytes 3145736 | tf_op jit(solution)/shard_map/ppermute | solution.py:423
  11.7 3.5 %collective-permute-start.1 = (bf16[56,128,128]{2,1,0:T(8,128)(2,1)}, bf16[56,128,128]{2,1,0:T(8,128)(2,1)S(1)}, u32[]{:S(2)}, u32[]{:S(2)}) collective-permute-start(bf16[56,128,128]{2,1,0:T(8,128)(2,1)} %bitcast.6), channel_id=1, source_target_pairs={{0,128},{128,0},{256,384},{384,256},{1,385},{129,257},{257,129},{3... | collective-permute-start | bytes 5505032 | tf_op jit(solution)/shard_map/ppermute | solution.py:428
  15.2 1.9 %collective-permute-start.5 = (bf16[8,4,128,128]{3,2,1,0:T(8,128)(2,1)}, bf16[8,4,128,128]{3,2,1,0:T(8,128)(2,1)S(1)}, u32[]{:S(2)}, u32[]{:S(2)}) collective-permute-start(bf16[8,4,128,128]{3,2,1,0:T(8,128)(2,1)} %p_hbm.1), channel_id=1, source_target_pairs={{0,1},{1,0},{2,3},{3,2},{4,5},{5,4},{6,7},{7,6},{8,9},{9,8},{10,11... | collective-permute-start | bytes 3145736 | tf_op jit(solution)/shard_map/ppermute | solution.py:423
  17.1 7.2 %collective-permute-done.3.refs_0_ = bf16[8,4,128,128]{3,2,1,0:T(8,128)(2,1)S(1)} collective-permute-done((bf16[8,4,128,128]{3,2,1,0:T(8,128)(2,1)}, bf16[8,4,128,128]{3,2,1,0:T(8,128)(2,1)S(1)}, u32[]{:S(2)}, u32[]{:S(2)}) %collective-permute-start.3) | collective-permute-done | bytes 1048608 | tf_op jit(solution)/shard_map/ppermute | solution.py:423
  24.3 1.9 %collective-permute-start.4 = (bf16[8,4,128,128]{3,2,1,0:T(8,128)(2,1)S(1)}, bf16[8,4,128,128]{3,2,1,0:T(8,128)(2,1)S(1)}, u32[]{:S(2)}, u32[]{:S(2)}) collective-permute-start(bf16[8,4,128,128]{3,2,1,0:T(8,128)(2,1)S(1)} %collective-permute-done.3.refs_0_), channel_id=1, source_target_pairs={{0,1},{1,0},{2,3},{3,2},{4,5},{5,4},{6,7},{7,6},{8,9},{9,8},{10,11... | collective-permute-start | bytes 3145736 | tf_op jit(solution)/shard_map/ppermute | solution.py:423
  26.2 1.9 %collective-permute-start.2 = (bf16[8,4,128,128]{3,2,1,0:T(8,128)(2,1)}, bf16[8,4,128,128]{3,2,1,0:T(8,128)(2,1)S(1)}, u32[]{:S(2)}, u32[]{:S(2)}) collective-permute-start(bf16[8,4,128,128]{3,2,1,0:T(8,128)(2,1)} %p_hbm.1), channel_id=1, source_target_pairs={{0,2},{2,4},{3,1},{4,6},{5,3},{6,8},{7,5},{8,10},{9,7},{10,12},{11... | collective-permute-start | bytes 3145736 | tf_op jit(solution)/shard_map/ppermute | solution.py:423
  28.1 3.5 %collective-permute-start = (s32[8,1,7]{0,1,2:T(1,128)}, s32[8,1,7]{0,1,2:T(1,128)S(1)}, u32[]{:S(2)}, u32[]{:S(2)}) collective-permute-start(s32[8,1,7]{0,1,2:T(1,128)} %param.6), channel_id=1, source_target_pairs={{0,128},{128,0},{256,384},{384,256},{1,385},{129,257},{257,129},{3... | collective-permute-start | bytes 680 | tf_op jit(solution)/shard_map/ppermute | solution.py:428
  31.6 5.4 %collective-permute-done = s32[8,1,7]{0,1,2:T(1,128)S(1)} collective-permute-done((s32[8,1,7]{0,1,2:T(1,128)}, s32[8,1,7]{0,1,2:T(1,128)S(1)}, u32[]{:S(2)}, u32[]{:S(2)}) %collective-permute-start) | collective-permute-done | bytes 256 | tf_op jit(solution)/shard_map/ppermute | solution.py:428
  37.0 4.1 %shard_map.55 = (s32[1360]{0:T(1024)S(4)}, s32[8]{0:T(128)S(4)}, s32[400]{0:T(512)S(4)}, s32[256]{0:T(256)S(4)}, bf16[56,128,128]{2,1,0:T(8,128)(2,1)S(1)}, /*in...) custom-call(s32[7,1,8]{2,1,0:T(1,128)} %bitcast.10, ...), custom_call_target="tpu_custom_call" | custom-call | flops 20000000 | bytes 1000000 | tf_op jit(solution)/shard_map/pallas_call | solution.py:52
  41.2 0.0 collective-permute-done.5.refs_0_
  41.2 1.6 %shard_map.56 = (bf16[56,128,128]{2,1,0:T(8,128)(2,1)S(1)}, bf16[5,8,4,128,128]{4,3,2,1,0:T(8,128)(2,1)S(1)}, f32[226,128,128]{2,1,0:T(8,128)S(1)}) custom-call(s32[8]{0:T(128)S(4)} %get-tuple-element.26.count, s32[1360]{0:T(1024)S(4)} %get-tuple-element.27.entries, ...), custom_call_target="tpu_custom_call", output_to_operand_aliasing={{0}: (3, {}), {1}: (4, {}), {2}: (5, {})} | custom-call | flops 20000000 | bytes 1000000 | tf_op jit(solution)/shard_map/pallas_call | solution.py:52
  42.8 0.0 collective-permute-done.4.refs_1_
  42.8 2.0 %shard_map.57 = (bf16[56,128,128]{2,1,0:T(8,128)(2,1)S(1)}, bf16[5,8,4,128,128]{4,3,2,1,0:T(8,128)(2,1)S(1)}, f32[226,128,128]{2,1,0:T(8,128)S(1)}) custom-call(s32[8]{0:T(128)S(4)} %get-tuple-element.26.count, s32[1360]{0:T(1024)S(4)} %get-tuple-element.27.entries, ...), custom_call_target="tpu_custom_call", output_to_operand_aliasing={{0}: (4, {}), {1}: (5, {}), {2}: (6, {})} | custom-call | flops 20000000 | bytes 1000000 | tf_op jit(solution)/shard_map/pallas_call | solution.py:52
  44.8 0.8 collective-permute-done.2.refs_0_
  45.6 1.2 %shard_map.58 = (bf16[56,128,128]{2,1,0:T(8,128)(2,1)S(1)}, bf16[5,8,4,128,128]{4,3,2,1,0:T(8,128)(2,1)S(1)}, f32[226,128,128]{2,1,0:T(8,128)S(1)}) custom-call(s32[8]{0:T(128)S(4)} %get-tuple-element.26.count, s32[1360]{0:T(1024)S(4)} %get-tuple-element.27.entries, ...), custom_call_target="tpu_custom_call", output_to_operand_aliasing={{0}: (3, {}), {1}: (4, {}), {2}: (5, {})} | custom-call | flops 20000000 | bytes 1000000 | tf_op jit(solution)/shard_map/pallas_call | solution.py:52
  46.7 0.0 collective-permute-done.1.their
  46.7 4.6 %shard_map.59 = (bf16[56,128,128]{2,1,0:T(8,128)(2,1)S(1)}, bf16[5,8,4,128,128]{4,3,2,1,0:T(8,128)(2,1)S(1)}, f32[226,128,128]{2,1,0:T(8,128)S(1)}, s16[1,2064,128]{2,1,0:T(8,128)(2,1)S(1)}) custom-call(s32[8]{0:T(128)S(4)} %get-tuple-element.26.count, ...), custom_call_target="tpu_custom_call", output_to_operand_aliasing={{0}: (6, {}), {1}: (7, {}), {2}: (8, {})} | custom-call | flops 20000000 | bytes 1000000 | tf_op jit(solution)/shard_map/pallas_call | solution.py:52
  51.4 1.5 %shard_map.65 = s16[1,2064,128]{2,1,0:T(8,128)(2,1)S(1)} custom-call(s32[400]{0:T(512)S(4)} %get-tuple-element.24.small, s32[256]{0:T(256)S(4)} %get-tuple-element.25.sidx, f32[226,128,128]{2,1,0:T(8,128)S(1)} %get-tuple-element.41.sums, bf16[32,128,128]{2,1,0:T(8,128)(2,1)S(1)} %get-tuple-element.28.pt), custom_call_target="tpu_custom_call" | custom-call | flops 20000000 | bytes 1000000 | tf_op jit(solution)/shard_map/pallas_call | solution.py:52
  52.9 1.5 %shard_map.61 = s16[1,2064,128]{2,1,0:T(8,128)(2,1)S(1)} custom-call(s32[400]{0:T(512)S(4)} %get-tuple-element.24.small, s32[256]{0:T(256)S(4)} %get-tuple-element.25.sidx, f32[226,128,128]{2,1,0:T(8,128)S(1)} %get-tuple-element.41.sums, bf16[32,128,128]{2,1,0:T(8,128)(2,1)S(1)} %get-tuple-element.28.pt), custom_call_target="tpu_custom_call" | custom-call | flops 20000000 | bytes 1000000 | tf_op jit(solution)/shard_map/pallas_call | solution.py:52
  54.5 5.6 %collective-permute-start.7 = (s16[1,2064,128]{2,1,0:T(8,128)(2,1)S(1)}, s16[1,2064,128]{2,1,0:T(8,128)(2,1)S(1)}, u32[]{:S(2)}, u32[]{:S(2)}) collective-permute-start(s16[1,2064,128]{2,1,0:T(8,128)(2,1)S(1)} %shard_map.61), channel_id=1, source_target_pairs={{0,385},{128,257},{256,129},{384,1},{1,128},{129,0},{257,384},{385... | collective-permute-start | bytes 1585160 | tf_op jit(solution)/shard_map/ppermute | solution.py:428
  60.1 1.9 %collective-permute-start.6 = (s16[1,2064,128]{2,1,0:T(8,128)(2,1)S(1)}, s16[1,2064,128]{2,1,0:T(8,128)(2,1)S(1)}, u32[]{:S(2)}, u32[]{:S(2)}) collective-permute-start(s16[1,2064,128]{2,1,0:T(8,128)(2,1)S(1)} %get-tuple-element.42), channel_id=1, source_target_pairs={{0,384},{128,256},{256,128},{384,0},{1,129},{129,1},{257,385},{385... | collective-permute-start | bytes 1585160 | tf_op jit(solution)/shard_map/ppermute | solution.py:428
  62.0 1.6 %shard_map.64 = s16[1,2064,128]{2,1,0:T(8,128)(2,1)S(1)} custom-call(s32[400]{0:T(512)S(4)} %get-tuple-element.24.small, s32[256]{0:T(256)S(4)} %get-tuple-element.25.sidx, f32[226,128,128]{2,1,0:T(8,128)S(1)} %get-tuple-element.41.sums, bf16[32,128,128]{2,1,0:T(8,128)(2,1)S(1)} %get-tuple-element.28.pt), custom_call_target="tpu_custom_call" | custom-call | flops 20000000 | bytes 1000000 | tf_op jit(solution)/shard_map/pallas_call | solution.py:52
  63.7 1.6 %shard_map.63 = s16[1,2064,128]{2,1,0:T(8,128)(2,1)S(1)} custom-call(s32[400]{0:T(512)S(4)} %get-tuple-element.24.small, s32[256]{0:T(256)S(4)} %get-tuple-element.25.sidx, f32[226,128,128]{2,1,0:T(8,128)S(1)} %get-tuple-element.41.sums, bf16[32,128,128]{2,1,0:T(8,128)(2,1)S(1)} %get-tuple-element.28.pt), custom_call_target="tpu_custom_call" | custom-call | flops 20000000 | bytes 1000000 | tf_op jit(solution)/shard_map/pallas_call | solution.py:52
  65.3 1.9 %collective-permute-start.10 = (s16[1,2064,128]{2,1,0:T(8,128)(2,1)S(1)}, s16[1,2064,128]{2,1,0:T(8,128)(2,1)S(1)}, u32[]{:S(2)}, u32[]{:S(2)}) collective-permute-start(s16[1,2064,128]{2,1,0:T(8,128)(2,1)S(1)} %shard_map.65), channel_id=1, source_target_pairs={{0,1},{1,0},{2,3},{3,2},{4,5},{5,4},{6,7},{7,6},{8,9},{9,8},{10,11... | collective-permute-start | bytes 1585160 | tf_op jit(solution)/shard_map/ppermute | solution.py:423
  67.2 5.2 %collective-permute-start.9 = (s16[1,2064,128]{2,1,0:T(8,128)(2,1)S(1)}, s16[1,2064,128]{2,1,0:T(8,128)(2,1)S(1)}, u32[]{:S(2)}, u32[]{:S(2)}) collective-permute-start(s16[1,2064,128]{2,1,0:T(8,128)(2,1)S(1)} %shard_map.64), channel_id=1, source_target_pairs={{1,2},{2,1},{3,4},{4,3},{5,6},{6,5},{7,8},{8,7},{9,10},{10,9},{11,... | collective-permute-start | bytes 1585160 | tf_op jit(solution)/shard_map/ppermute | solution.py:423
  72.4 5.1 %collective-permute-start.8 = (s16[1,2064,128]{2,1,0:T(8,128)(2,1)S(1)}, s16[1,2064,128]{2,1,0:T(8,128)(2,1)S(1)}, u32[]{:S(2)}, u32[]{:S(2)}) collective-permute-start(s16[1,2064,128]{2,1,0:T(8,128)(2,1)S(1)} %shard_map.63), channel_id=1, source_target_pairs={{1,130},{129,2},{257,386},{385,258},{2,385},{130,257},{258,129},{3... | collective-permute-start | bytes 1585160 | tf_op jit(solution)/shard_map/ppermute | solution.py:428
  77.6 1.2 %shard_map.60.own = f32[4,4,128,128]{3,2,1,0:T(8,128)S(1)} custom-call(s32[400]{0:T(512)S(4)} %get-tuple-element.24.small, s32[256]{0:T(256)S(4)} %get-tuple-element.25.sidx, f32[226,128,128]{2,1,0:T(8,128)S(1)} %get-tuple-element.41.sums, bf16[32,128,128]{2,1,0:T(8,128)(2,1)S(1)} %get-tuple-element.28.pt), custom_call_target="tpu_custom_call" | custom-call | flops 20000000 | bytes 1000000 | tf_op jit(solution)/shard_map/pallas_call | solution.py:52
  78.8 0.0 collective-permute-done.7.refs_1_
  78.8 0.0 collective-permute-done.6.refs_0_
  78.8 0.3 shard_map.62.own
  79.1 0.0 collective-permute-done.10.refs_2_
  79.1 0.8 collective-permute-done.9.refs_1_
  79.9 6.1 %collective-permute-done.8.refs_0_ = s16[1,2064,128]{2,1,0:T(8,128)(2,1)S(1)} collective-permute-done((s16[1,2064,128]{2,1,0:T(8,128)(2,1)S(1)}, s16[1,2064,128]{2,1,0:T(8,128)(2,1)S(1)}, u32[]{:S(2)}, u32[]{:S(2)}) %collective-permute-start.8) | collective-permute-done | bytes 528416 | tf_op jit(solution)/shard_map/ppermute | solution.py:428
  86.0 1.2 %shard_map.66 = f32[4,4,128,128]{3,2,1,0:T(8,128)} custom-call(f32[4,4,128,128]{3,2,1,0:T(8,128)S(1)} %shard_map.62.own, s16[1,2064,128]{2,1,0:T(8,128)(2,1)S(1)} %collective-permute-done.8.refs_0_, s16[1,2064,128]{2,1,0:T(8,128)(2,1)S(1)} %collective-permute-done.9.refs_1_, s16[1,2064,128]{2,1,0:T(8,128)(2,1)S(1)} %collective-permute-done.10.refs_2_), custom_call_target="tpu_custom_call" | custom-call | flops 20000000 | bytes 1000000 | tf_op jit(solution)/shard_map/pallas_call | solution.py:52
Async XLA Ops:
  0.0 24.3 %collective-permute-start.3 = (bf16[8,4,128,128]{3,2,1,0:T(8,128)(2,1)}, bf16[8,4,128,128]{3,2,1,0:T(8,128)(2,1)S(1)}, u32[]{:S(2)}, u32[]{:S(2)}) collective-permute-start(bf16[8,4,128,128]{3,2,1,0:T(8,128)(2,1)} %p_hbm.1), channel_id=1, source_target_pairs={{1,3},{2,0},{3,5},{4,2},{5,7},{6,4},{7,9},{8,6},{9,11},{10,8},{11,... | collective-permute-start | bytes 3145736 | tf_op jit(solution)/shard_map/ppermute | solution.py:423
  11.7 35.1 %collective-permute-start.1 = (bf16[56,128,128]{2,1,0:T(8,128)(2,1)}, bf16[56,128,128]{2,1,0:T(8,128)(2,1)S(1)}, u32[]{:S(2)}, u32[]{:S(2)}) collective-permute-start(bf16[56,128,128]{2,1,0:T(8,128)(2,1)} %bitcast.6), channel_id=1, source_target_pairs={{0,128},{128,0},{256,384},{384,256},{1,385},{129,257},{257,129},{3... | collective-permute-start | bytes 5505032 | tf_op jit(solution)/shard_map/ppermute | solution.py:428
  15.2 26.0 %collective-permute-start.5 = (bf16[8,4,128,128]{3,2,1,0:T(8,128)(2,1)}, bf16[8,4,128,128]{3,2,1,0:T(8,128)(2,1)S(1)}, u32[]{:S(2)}, u32[]{:S(2)}) collective-permute-start(bf16[8,4,128,128]{3,2,1,0:T(8,128)(2,1)} %p_hbm.1), channel_id=1, source_target_pairs={{0,1},{1,0},{2,3},{3,2},{4,5},{5,4},{6,7},{7,6},{8,9},{9,8},{10,11... | collective-permute-start | bytes 3145736 | tf_op jit(solution)/shard_map/ppermute | solution.py:423
  24.3 18.5 %collective-permute-start.4 = (bf16[8,4,128,128]{3,2,1,0:T(8,128)(2,1)S(1)}, bf16[8,4,128,128]{3,2,1,0:T(8,128)(2,1)S(1)}, u32[]{:S(2)}, u32[]{:S(2)}) collective-permute-start(bf16[8,4,128,128]{3,2,1,0:T(8,128)(2,1)S(1)} %collective-permute-done.3.refs_0_), channel_id=1, source_target_pairs={{0,1},{1,0},{2,3},{3,2},{4,5},{5,4},{6,7},{7,6},{8,9},{9,8},{10,11... | collective-permute-start | bytes 3145736 | tf_op jit(solution)/shard_map/ppermute | solution.py:423
  26.2 19.4 %collective-permute-start.2 = (bf16[8,4,128,128]{3,2,1,0:T(8,128)(2,1)}, bf16[8,4,128,128]{3,2,1,0:T(8,128)(2,1)S(1)}, u32[]{:S(2)}, u32[]{:S(2)}) collective-permute-start(bf16[8,4,128,128]{3,2,1,0:T(8,128)(2,1)} %p_hbm.1), channel_id=1, source_target_pairs={{0,2},{2,4},{3,1},{4,6},{5,3},{6,8},{7,5},{8,10},{9,7},{10,12},{11... | collective-permute-start | bytes 3145736 | tf_op jit(solution)/shard_map/ppermute | solution.py:423
  28.1 8.9 %collective-permute-start = (s32[8,1,7]{0,1,2:T(1,128)}, s32[8,1,7]{0,1,2:T(1,128)S(1)}, u32[]{:S(2)}, u32[]{:S(2)}) collective-permute-start(s32[8,1,7]{0,1,2:T(1,128)} %param.6), channel_id=1, source_target_pairs={{0,128},{128,0},{256,384},{384,256},{1,385},{129,257},{257,129},{3... | collective-permute-start | bytes 680 | tf_op jit(solution)/shard_map/ppermute | solution.py:428
  54.5 24.3 %collective-permute-start.7 = (s16[1,2064,128]{2,1,0:T(8,128)(2,1)S(1)}, s16[1,2064,128]{2,1,0:T(8,128)(2,1)S(1)}, u32[]{:S(2)}, u32[]{:S(2)}) collective-permute-start(s16[1,2064,128]{2,1,0:T(8,128)(2,1)S(1)} %shard_map.61), channel_id=1, source_target_pairs={{0,385},{128,257},{256,129},{384,1},{1,128},{129,0},{257,384},{385... | collective-permute-start | bytes 1585160 | tf_op jit(solution)/shard_map/ppermute | solution.py:428
  60.1 18.7 %collective-permute-start.6 = (s16[1,2064,128]{2,1,0:T(8,128)(2,1)S(1)}, s16[1,2064,128]{2,1,0:T(8,128)(2,1)S(1)}, u32[]{:S(2)}, u32[]{:S(2)}) collective-permute-start(s16[1,2064,128]{2,1,0:T(8,128)(2,1)S(1)} %get-tuple-element.42), channel_id=1, source_target_pairs={{0,384},{128,256},{256,128},{384,0},{1,129},{129,1},{257,385},{385... | collective-permute-start | bytes 1585160 | tf_op jit(solution)/shard_map/ppermute | solution.py:428
  65.3 13.8 %collective-permute-start.10 = (s16[1,2064,128]{2,1,0:T(8,128)(2,1)S(1)}, s16[1,2064,128]{2,1,0:T(8,128)(2,1)S(1)}, u32[]{:S(2)}, u32[]{:S(2)}) collective-permute-start(s16[1,2064,128]{2,1,0:T(8,128)(2,1)S(1)} %shard_map.65), channel_id=1, source_target_pairs={{0,1},{1,0},{2,3},{3,2},{4,5},{5,4},{6,7},{7,6},{8,9},{9,8},{10,11... | collective-permute-start | bytes 1585160 | tf_op jit(solution)/shard_map/ppermute | solution.py:423
  67.2 12.7 %collective-permute-start.9 = (s16[1,2064,128]{2,1,0:T(8,128)(2,1)S(1)}, s16[1,2064,128]{2,1,0:T(8,128)(2,1)S(1)}, u32[]{:S(2)}, u32[]{:S(2)}) collective-permute-start(s16[1,2064,128]{2,1,0:T(8,128)(2,1)S(1)} %shard_map.64), channel_id=1, source_target_pairs={{1,2},{2,1},{3,4},{4,3},{5,6},{6,5},{7,8},{8,7},{9,10},{10,9},{11,... | collective-permute-start | bytes 1585160 | tf_op jit(solution)/shard_map/ppermute | solution.py:423
  72.4 13.6 %collective-permute-start.8 = (s16[1,2064,128]{2,1,0:T(8,128)(2,1)S(1)}, s16[1,2064,128]{2,1,0:T(8,128)(2,1)S(1)}, u32[]{:S(2)}, u32[]{:S(2)}) collective-permute-start(s16[1,2064,128]{2,1,0:T(8,128)(2,1)S(1)} %shard_map.63), channel_id=1, source_target_pairs={{1,130},{129,2},{257,386},{385,258},{2,385},{130,257},{258,129},{3... | collective-permute-start | bytes 1585160 | tf_op jit(solution)/shard_map/ppermute | solution.py:428

commit v8 on v7

--- a/solution.py
+++ b/solution.py
@@ -268,22 +268,9 @@
     return jnp.concatenate([hi, (x - hi.astype(jnp.float32)).astype(jnp.bfloat16)], axis=0)
 
 
-def form_rows(first, quarters, coded, accs, small, sidx, sums, pt, out, *ex):
-    for c in range(C):
-
-        def pair(r, _):
-            pr = small[PLIST + (first + c) * (F * KP) + r]
-            tile = pt[pr]
-            lhs = jnp.concatenate([tile, tile], axis=1)
-            for n, acc in enumerate(accs):
-                k = pr * KD + quarters[0] * KG + 2 * n
-                rhs = jnp.concatenate([terms(sums[sidx[k]]), terms(sums[sidx[k + 1]])], axis=1)
-                pltpu.matmul_push_rhs(rhs, staging_register=(n // 2) % 2, mxu_index=n % 2)
-                pltpu.matmul_acc_lhs(acc, lhs, load_staged_rhs=(n // 2) % 2)
-            return 0
-
-        lax.fori_loop(0, small[PAIRS + first + c], pair, 0)
-        for n, acc in enumerate(accs):
+def form_rows(first, quarters, coded, sets, small, sidx, sums, pt, out, *ex, add=()):
+    def take(c):
+        for n, acc in enumerate(sets[c % 2]):
             x = pltpu.matmul_pop(acc)
             for e in range(2):
                 q, k = divmod(2 * n + e, KG)
@@ -292,7 +279,28 @@
                     t = c * KG + k
                     out[q, t * T : (t + 1) * T, :] = code(y, ex[0].at[q], t)
                 else:
+                    t = c * KG + k
+                    for m, x_m in enumerate(add):
+                        y = y + widen(x_m[t * T : (t + 1) * T, :]) * ex[0][m, t : t + 1, :]
                     out[c, k] = y
+
+    for c in range(C):
+
+        def pair(r, _):
+            pr = small[PLIST + (first + c) * (F * KP) + r]
+            tile = pt[pr]
+            lhs = jnp.concatenate([tile, tile], axis=1)
+            for n, acc in enumerate(sets[c % 2]):
+                k = pr * KD + quarters[0] * KG + 2 * n
+                rhs = jnp.concatenate([terms(sums[sidx[k]]), terms(sums[sidx[k + 1]])], axis=1)
+                pltpu.matmul_push_rhs(rhs, staging_register=(n // 2) % 2, mxu_index=n % 2)
+                pltpu.matmul_acc_lhs(acc, lhs, load_staged_rhs=(n // 2) % 2)
+            return 0
+
+        lax.fori_loop(0, small[PAIRS + first + c], pair, 0)
+        if c:
+            take(c - 1)
+    take(C - 1)
     if coded:
         for q in range(len(quarters)):
             out[q, ROWS:PACK, :] = ex[0][q].astype(jnp.int32).astype(jnp.int16)
@@ -322,7 +330,7 @@
 
     def work(sets):
         entry_loop(LISTS - 1, count, entries, their, p, acc, sets)
-        form_rows(OWN, (0,), True, sets[0][0][:2], small, sidx, acc, pt, out, ex)
+        form_rows(OWN, (0,), True, [low[:2] for low, _ in sets], small, sidx, acc, pt, out, ex)
 
     with_sets(work)
 
@@ -339,23 +347,30 @@
     )[2:]
 
 
-def coarse_kernel(first, quarters, coded, small, sidx, sums, pt, out, *ex):
+def coarse_kernel(first, quarters, coded, received, small, sidx, sums, pt, *refs):
+    add, (out, *ex) = refs[:received], refs[received:]
+    add = [x.at[x.shape[0] - 1] for x in add]
+    for n, x in enumerate(add):
+        scale(ex[0].at[n], x[ROWS:PACK, :])
+
     def body(*accs):
         for acc in accs:
             pltpu.matmul_pop(acc)
-        form_rows(first, quarters, coded, accs, small, sidx, sums, pt, out, *ex)
-
-    pl.run_scoped(body, *[pltpu.ACC(n % 2)((T, 2 * T), jnp.float32) for n in range(len(quarters) * KG // 2)])
-
-
-def coarse(first, quarters, coded, tabs, sums, pt):
+        many = len(accs) // 2
+        form_rows(first, quarters, coded, (accs[:many], accs[many:]), small, sidx, sums, pt, out, *ex, add=add)
+
+    many = len(quarters) * KG // 2
+    pl.run_scoped(body, *[pltpu.ACC(n % 2)((T, 2 * T), jnp.float32) for _ in range(2) for n in range(many)])
+
+
+def coarse(first, quarters, coded, tabs, sums, pt, received=()):
     n = len(quarters)
     out = near((n, PACK, T), jnp.int16) if coded else near((C, KG, T, T), jnp.float32)
     return call(
-        functools.partial(coarse_kernel, first, quarters, coded),
-        [("smem", tabs[0]), ("smem", tabs[1]), ("vmem", sums), ("vmem", pt)],
+        functools.partial(coarse_kernel, first, quarters, coded, len(received)),
+        [("smem", tabs[0]), ("smem", tabs[1])] + [("vmem", x) for x in (sums, pt, *received)],
         [out],
-        [pltpu.VMEM((n, SCALES, T), jnp.float32)] if coded else [],
+        [pltpu.VMEM((n if coded else len(received), SCALES, T), jnp.float32)],
     )[0]
 
 
@@ -365,27 +380,6 @@
 
 def scale(ref, rows):
     ref[...] = jnp.exp2(widen(rows)) * (1.0 / LEVELS)
-
-
-def add_kernel(own, *refs):
-    *coded, out, ex = refs
-    coded = [x.at[x.shape[0] - 1] for x in coded]
-    for n, x in enumerate(coded):
-        scale(ex.at[n], x[ROWS:PACK, :])
-    for t, c, k, rows in tiles():
-        y = own[c, k]
-        for n, x in enumerate(coded):
-            y = y + widen(x[rows, :]) * ex[n, t : t + 1, :]
-        out[c, k] = y
-
-
-def added(own, coded):
-    return call(
-        add_kernel,
-        [("vmem", x) for x in (own, *coded)],
-        [near(own.shape, own.dtype)],
-        [pltpu.VMEM((len(coded), SCALES, T), jnp.float32)],
-    )[0]
 
 
 def finish_kernel(own, *refs):
@@ -479,9 +473,8 @@
     outer = along(x, away)
     x = coarse(INNER, (1,), True, *rows)
     inner = along(x, other)
-    own = coarse(OWN, (1,), False, *rows)
-    mine = added(own, (from_second, from_side))
-    return finished(mine, (from_skew, outer, inner))
+    own = coarse(OWN, (1,), False, *rows, (from_second, from_skew))
+    return finished(own, (from_side, outer, inner))
 
 
 def solution(mesh):

time: 88.3 us -> 84 us (0.951)
  starting transfers between devices: 44.2 us -> 42.6 us
  waiting for transfers between devices: 20.2 us -> 18.8 us
  Pallas kernels: 22.5 us -> 21.2 us
    ppermute x5, waiting for transfers between devices: 11.5 us -> 6.45 us  [across(): lax.ppermute(x, ('grp', 'row'), [(g * rows + r, to(g, r % 2) * rows + row...]
    ppermute x6, waiting for transfers between devices: 8.71 us -> 12.4 us  [along(): lax.ppermute(x, 'row', [(i, to(i)) for i in range(n) if 0 <= to(i) < n])]
    ppermute x6, starting transfers between devices: 24.5 us -> 21.2 us  [along(): lax.ppermute(x, 'row', [(i, to(i)) for i in range(n) if 0 <= to(i) < n])]
    ppermute x5, starting transfers between devices: 19.7 us -> 21.4 us  [across(): lax.ppermute(x, ('grp', 'row'), [(g * rows + r, to(g, r % 2) * rows + row...]
    pallas_call x12 -> x11, Pallas kernels: 22.5 us -> 21.2 us  [call(): pl.pallas_call(kernel, out_shape=[x for _, x in outs], in_specs=[spec[whe...]
where the time goes in v8:
time: 84 us; the launch traced here: 82.9 us
  starting transfers between devices  42.6 us (51%)
  Pallas kernels  21.2 us (25%)
  waiting for transfers between devices  18.8 us (22%)
    ppermute x5, starting transfers between devices, across(): lax.ppermute(x, ('grp', 'row'), [(g * rows + r, to(g, r % 2) * rows + row...  21.4 us
    ppermute x6, starting transfers between devices, along(): lax.ppermute(x, 'row', [(i, to(i)) for i in range(n) if 0 <= to(i) < n])  21.2 us
    pallas_call x11, Pallas kernels, call(): pl.pallas_call(kernel, out_shape=[x for _, x in outs], in_specs=[spec[whe...  21.2 us
    ppermute x6, waiting for transfers between devices, along(): lax.ppermute(x, 'row', [(i, to(i)) for i in range(n) if 0 <= to(i) < n])  12.4 us
    ppermute x5, waiting for transfers between devices, across(): lax.ppermute(x, ('grp', 'row'), [(g * rows + r, to(g, r % 2) * rows + row...  6.45 us
  transfers between devices with their start and end apart: 11, of which 5 were waited for; matrix products, arithmetic and copies ran while one was open for 0% of the time, Pallas kernels for 16%

profile of v8, /device:TPU:6, one launch (start us, length us, event | category | flops | bytes accessed | tf_op | source)
XLA Modules:
  0.0 82.9 jit_solution(7116791125370456238)
XLA Ops:
  0.0 11.7 %collective-permute-start.3 = (bf16[8,4,128,128]{3,2,1,0:T(8,128)(2,1)}, bf16[8,4,128,128]{3,2,1,0:T(8,128)(2,1)S(1)}, u32[]{:S(2)}, u32[]{:S(2)}) collective-permute-start(bf16[8,4,128,128]{3,2,1,0:T(8,128)(2,1)} %p_hbm.1), channel_id=1, source_target_pairs={{1,3},{2,0},{3,5},{4,2},{5,7},{6,4},{7,9},{8,6},{9,11},{10,8},{11,... | collective-permute-start | bytes 3145736 | tf_op jit(solution)/shard_map/ppermute | solution.py:417
  11.7 3.5 %collective-permute-start.1 = (bf16[56,128,128]{2,1,0:T(8,128)(2,1)}, bf16[56,128,128]{2,1,0:T(8,128)(2,1)S(1)}, u32[]{:S(2)}, u32[]{:S(2)}) collective-permute-start(bf16[56,128,128]{2,1,0:T(8,128)(2,1)} %bitcast.6), channel_id=1, source_target_pairs={{0,128},{128,0},{256,384},{384,256},{1,385},{129,257},{257,129},{3... | collective-permute-start | bytes 5505032 | tf_op jit(solution)/shard_map/ppermute | solution.py:422
  15.2 1.9 %collective-permute-start.5 = (bf16[8,4,128,128]{3,2,1,0:T(8,128)(2,1)}, bf16[8,4,128,128]{3,2,1,0:T(8,128)(2,1)S(1)}, u32[]{:S(2)}, u32[]{:S(2)}) collective-permute-start(bf16[8,4,128,128]{3,2,1,0:T(8,128)(2,1)} %p_hbm.1), channel_id=1, source_target_pairs={{0,1},{1,0},{2,3},{3,2},{4,5},{5,4},{6,7},{7,6},{8,9},{9,8},{10,11... | collective-permute-start | bytes 3145736 | tf_op jit(solution)/shard_map/ppermute | solution.py:417
  17.1 7.2 %collective-permute-done.3.refs_0_ = bf16[8,4,128,128]{3,2,1,0:T(8,128)(2,1)S(1)} collective-permute-done((bf16[8,4,128,128]{3,2,1,0:T(8,128)(2,1)}, bf16[8,4,128,128]{3,2,1,0:T(8,128)(2,1)S(1)}, u32[]{:S(2)}, u32[]{:S(2)}) %collective-permute-start.3) | collective-permute-done | bytes 1048608 | tf_op jit(solution)/shard_map/ppermute | solution.py:417
  24.3 1.9 %collective-permute-start.4 = (bf16[8,4,128,128]{3,2,1,0:T(8,128)(2,1)S(1)}, bf16[8,4,128,128]{3,2,1,0:T(8,128)(2,1)S(1)}, u32[]{:S(2)}, u32[]{:S(2)}) collective-permute-start(bf16[8,4,128,128]{3,2,1,0:T(8,128)(2,1)S(1)} %collective-permute-done.3.refs_0_), channel_id=1, source_target_pairs={{0,1},{1,0},{2,3},{3,2},{4,5},{5,4},{6,7},{7,6},{8,9},{9,8},{10,11... | collective-permute-start | bytes 3145736 | tf_op jit(solution)/shard_map/ppermute | solution.py:417
  26.2 1.9 %collective-permute-start.2 = (bf16[8,4,128,128]{3,2,1,0:T(8,128)(2,1)}, bf16[8,4,128,128]{3,2,1,0:T(8,128)(2,1)S(1)}, u32[]{:S(2)}, u32[]{:S(2)}) collective-permute-start(bf16[8,4,128,128]{3,2,1,0:T(8,128)(2,1)} %p_hbm.1), channel_id=1, source_target_pairs={{0,2},{2,4},{3,1},{4,6},{5,3},{6,8},{7,5},{8,10},{9,7},{10,12},{11... | collective-permute-start | bytes 3145736 | tf_op jit(solution)/shard_map/ppermute | solution.py:417
  28.1 3.5 %collective-permute-start = (s32[8,1,7]{0,1,2:T(1,128)}, s32[8,1,7]{0,1,2:T(1,128)S(1)}, u32[]{:S(2)}, u32[]{:S(2)}) collective-permute-start(s32[8,1,7]{0,1,2:T(1,128)} %param.6), channel_id=1, source_target_pairs={{0,128},{128,0},{256,384},{384,256},{1,385},{129,257},{257,129},{3... | collective-permute-start | bytes 680 | tf_op jit(solution)/shard_map/ppermute | solution.py:422
  31.6 5.4 %collective-permute-done = s32[8,1,7]{0,1,2:T(1,128)S(1)} collective-permute-done((s32[8,1,7]{0,1,2:T(1,128)}, s32[8,1,7]{0,1,2:T(1,128)S(1)}, u32[]{:S(2)}, u32[]{:S(2)}) %collective-permute-start) | collective-permute-done | bytes 256 | tf_op jit(solution)/shard_map/ppermute | solution.py:422
  37.0 4.1 %shard_map.55 = (s32[1360]{0:T(1024)S(4)}, s32[8]{0:T(128)S(4)}, s32[400]{0:T(512)S(4)}, s32[256]{0:T(256)S(4)}, bf16[56,128,128]{2,1,0:T(8,128)(2,1)S(1)}, /*in...) custom-call(s32[7,1,8]{2,1,0:T(1,128)} %bitcast.10, ...), custom_call_target="tpu_custom_call" | custom-call | flops 20000000 | bytes 1000000 | tf_op jit(solution)/shard_map/pallas_call | solution.py:52
  41.2 0.0 collective-permute-done.5.refs_0_
  41.2 1.6 %shard_map.56 = (bf16[56,128,128]{2,1,0:T(8,128)(2,1)S(1)}, bf16[5,8,4,128,128]{4,3,2,1,0:T(8,128)(2,1)S(1)}, f32[226,128,128]{2,1,0:T(8,128)S(1)}) custom-call(s32[8]{0:T(128)S(4)} %get-tuple-element.26.count, s32[1360]{0:T(1024)S(4)} %get-tuple-element.27.entries, ...), custom_call_target="tpu_custom_call", output_to_operand_aliasing={{0}: (3, {}), {1}: (4, {}), {2}: (5, {})} | custom-call | flops 20000000 | bytes 1000000 | tf_op jit(solution)/shard_map/pallas_call | solution.py:52
  42.8 0.0 collective-permute-done.4.refs_1_
  42.8 2.0 %shard_map.57 = (bf16[56,128,128]{2,1,0:T(8,128)(2,1)S(1)}, bf16[5,8,4,128,128]{4,3,2,1,0:T(8,128)(2,1)S(1)}, f32[226,128,128]{2,1,0:T(8,128)S(1)}) custom-call(s32[8]{0:T(128)S(4)} %get-tuple-element.26.count, s32[1360]{0:T(1024)S(4)} %get-tuple-element.27.entries, ...), custom_call_target="tpu_custom_call", output_to_operand_aliasing={{0}: (4, {}), {1}: (5, {}), {2}: (6, {})} | custom-call | flops 20000000 | bytes 1000000 | tf_op jit(solution)/shard_map/pallas_call | solution.py:52
  44.8 0.8 collective-permute-done.2.refs_0_
  45.6 1.2 %shard_map.58 = (bf16[56,128,128]{2,1,0:T(8,128)(2,1)S(1)}, bf16[5,8,4,128,128]{4,3,2,1,0:T(8,128)(2,1)S(1)}, f32[226,128,128]{2,1,0:T(8,128)S(1)}) custom-call(s32[8]{0:T(128)S(4)} %get-tuple-element.26.count, s32[1360]{0:T(1024)S(4)} %get-tuple-element.27.entries, ...), custom_call_target="tpu_custom_call", output_to_operand_aliasing={{0}: (3, {}), {1}: (4, {}), {2}: (5, {})} | custom-call | flops 20000000 | bytes 1000000 | tf_op jit(solution)/shard_map/pallas_call | solution.py:52
  46.7 0.0 collective-permute-done.1.their
  46.7 4.5 %shard_map.59 = (bf16[56,128,128]{2,1,0:T(8,128)(2,1)S(1)}, bf16[5,8,4,128,128]{4,3,2,1,0:T(8,128)(2,1)S(1)}, f32[226,128,128]{2,1,0:T(8,128)S(1)}, s16[1,2064,128]{2,1,0:T(8,128)(2,1)S(1)}) custom-call(s32[8]{0:T(128)S(4)} %get-tuple-element.26.count, ...), custom_call_target="tpu_custom_call", output_to_operand_aliasing={{0}: (6, {}), {1}: (7, {}), {2}: (8, {})} | custom-call | flops 20000000 | bytes 1000000 | tf_op jit(solution)/shard_map/pallas_call | solution.py:52
  51.2 1.2 %shard_map.64 = s16[1,2064,128]{2,1,0:T(8,128)(2,1)S(1)} custom-call(s32[400]{0:T(512)S(4)} %get-tuple-element.24.small, s32[256]{0:T(256)S(4)} %get-tuple-element.25.sidx, f32[226,128,128]{2,1,0:T(8,128)S(1)} %get-tuple-element.41.sums, bf16[32,128,128]{2,1,0:T(8,128)(2,1)S(1)} %get-tuple-element.28.pt), custom_call_target="tpu_custom_call" | custom-call | flops 20000000 | bytes 1000000 | tf_op jit(solution)/shard_map/pallas_call | solution.py:52
  52.5 1.5 %shard_map.60 = s16[1,2064,128]{2,1,0:T(8,128)(2,1)S(1)} custom-call(s32[400]{0:T(512)S(4)} %get-tuple-element.24.small, s32[256]{0:T(256)S(4)} %get-tuple-element.25.sidx, f32[226,128,128]{2,1,0:T(8,128)S(1)} %get-tuple-element.41.sums, bf16[32,128,128]{2,1,0:T(8,128)(2,1)S(1)} %get-tuple-element.28.pt), custom_call_target="tpu_custom_call" | custom-call | flops 20000000 | bytes 1000000 | tf_op jit(solution)/shard_map/pallas_call | solution.py:52
  54.0 7.3 %collective-permute-start.7 = (s16[1,2064,128]{2,1,0:T(8,128)(2,1)S(1)}, s16[1,2064,128]{2,1,0:T(8,128)(2,1)S(1)}, u32[]{:S(2)}, u32[]{:S(2)}) collective-permute-start(s16[1,2064,128]{2,1,0:T(8,128)(2,1)S(1)} %shard_map.60), channel_id=1, source_target_pairs={{1,130},{129,2},{257,386},{385,258},{2,385},{130,257},{258,129},{3... | collective-permute-start | bytes 1585160 | tf_op jit(solution)/shard_map/ppermute | solution.py:422
  61.2 2.1 %collective-permute-start.6 = (s16[1,2064,128]{2,1,0:T(8,128)(2,1)S(1)}, s16[1,2064,128]{2,1,0:T(8,128)(2,1)S(1)}, u32[]{:S(2)}, u32[]{:S(2)}) collective-permute-start(s16[1,2064,128]{2,1,0:T(8,128)(2,1)S(1)} %get-tuple-element.42), channel_id=1, source_target_pairs={{0,384},{128,256},{256,128},{384,0},{1,129},{129,1},{257,385},{385... | collective-permute-start | bytes 1585160 | tf_op jit(solution)/shard_map/ppermute | solution.py:422
  63.4 1.5 %shard_map.63 = s16[1,2064,128]{2,1,0:T(8,128)(2,1)S(1)} custom-call(s32[400]{0:T(512)S(4)} %get-tuple-element.24.small, s32[256]{0:T(256)S(4)} %get-tuple-element.25.sidx, f32[226,128,128]{2,1,0:T(8,128)S(1)} %get-tuple-element.41.sums, bf16[32,128,128]{2,1,0:T(8,128)(2,1)S(1)} %get-tuple-element.28.pt), custom_call_target="tpu_custom_call" | custom-call | flops 20000000 | bytes 1000000 | tf_op jit(solution)/shard_map/pallas_call | solution.py:52
  64.9 1.2 %shard_map.62 = s16[1,2064,128]{2,1,0:T(8,128)(2,1)S(1)} custom-call(s32[400]{0:T(512)S(4)} %get-tuple-element.24.small, s32[256]{0:T(256)S(4)} %get-tuple-element.25.sidx, f32[226,128,128]{2,1,0:T(8,128)S(1)} %get-tuple-element.41.sums, bf16[32,128,128]{2,1,0:T(8,128)(2,1)S(1)} %get-tuple-element.28.pt), custom_call_target="tpu_custom_call" | custom-call | flops 20000000 | bytes 1000000 | tf_op jit(solution)/shard_map/pallas_call | solution.py:52
  66.1 1.9 %collective-permute-start.10 = (s16[1,2064,128]{2,1,0:T(8,128)(2,1)S(1)}, s16[1,2064,128]{2,1,0:T(8,128)(2,1)S(1)}, u32[]{:S(2)}, u32[]{:S(2)}) collective-permute-start(s16[1,2064,128]{2,1,0:T(8,128)(2,1)S(1)} %shard_map.64), channel_id=1, source_target_pairs={{0,1},{1,0},{2,3},{3,2},{4,5},{5,4},{6,7},{7,6},{8,9},{9,8},{10,11... | collective-permute-start | bytes 1585160 | tf_op jit(solution)/shard_map/ppermute | solution.py:417
  68.0 1.9 %collective-permute-start.9 = (s16[1,2064,128]{2,1,0:T(8,128)(2,1)S(1)}, s16[1,2064,128]{2,1,0:T(8,128)(2,1)S(1)}, u32[]{:S(2)}, u32[]{:S(2)}) collective-permute-start(s16[1,2064,128]{2,1,0:T(8,128)(2,1)S(1)} %shard_map.63), channel_id=1, source_target_pairs={{1,2},{2,1},{3,4},{4,3},{5,6},{6,5},{7,8},{8,7},{9,10},{10,9},{11,... | collective-permute-start | bytes 1585160 | tf_op jit(solution)/shard_map/ppermute | solution.py:417
  70.0 5.0 %collective-permute-start.8 = (s16[1,2064,128]{2,1,0:T(8,128)(2,1)S(1)}, s16[1,2064,128]{2,1,0:T(8,128)(2,1)S(1)}, u32[]{:S(2)}, u32[]{:S(2)}) collective-permute-start(s16[1,2064,128]{2,1,0:T(8,128)(2,1)S(1)} %shard_map.62), channel_id=1, source_target_pairs={{0,385},{128,257},{256,129},{384,1},{1,128},{129,0},{257,384},{385... | collective-permute-start | bytes 1585160 | tf_op jit(solution)/shard_map/ppermute | solution.py:422
  75.0 0.0 collective-permute-done.7.refs_1_
  75.0 0.0 collective-permute-done.6.refs_0_
  75.0 1.3 %shard_map.61.own = f32[4,4,128,128]{3,2,1,0:T(8,128)S(1)} custom-call(s32[400]{0:T(512)S(4)} %get-tuple-element.24.small, s32[256]{0:T(256)S(4)} %get-tuple-element.25.sidx, f32[226,128,128]{2,1,0:T(8,128)S(1)} %get-tuple-element.41.sums, bf16[32,128,128]{2,1,0:T(8,128)(2,1)S(1)} %get-tuple-element.28.pt, ...), custom_call_target="tpu_custom_call" | custom-call | flops 20000000 | bytes 1000000 | tf_op jit(solution)/shard_map/pallas_call | solution.py:52
  76.3 0.0 collective-permute-done.10.refs_2_
  76.3 4.4 %collective-permute-done.9.refs_1_ = s16[1,2064,128]{2,1,0:T(8,128)(2,1)S(1)} collective-permute-done((s16[1,2064,128]{2,1,0:T(8,128)(2,1)S(1)}, s16[1,2064,128]{2,1,0:T(8,128)(2,1)S(1)}, u32[]{:S(2)}, u32[]{:S(2)}) %collective-permute-start.9) | collective-permute-done | bytes 528416 | tf_op jit(solution)/shard_map/ppermute | solution.py:417
  80.7 1.0 %collective-permute-done.8.refs_0_ = s16[1,2064,128]{2,1,0:T(8,128)(2,1)S(1)} collective-permute-done((s16[1,2064,128]{2,1,0:T(8,128)(2,1)S(1)}, s16[1,2064,128]{2,1,0:T(8,128)(2,1)S(1)}, u32[]{:S(2)}, u32[]{:S(2)}) %collective-permute-start.8) | collective-permute-done | bytes 528416 | tf_op jit(solution)/shard_map/ppermute | solution.py:422
  81.7 1.2 %shard_map.65 = f32[4,4,128,128]{3,2,1,0:T(8,128)} custom-call(f32[4,4,128,128]{3,2,1,0:T(8,128)S(1)} %shard_map.61.own, s16[1,2064,128]{2,1,0:T(8,128)(2,1)S(1)} %collective-permute-done.8.refs_0_, s16[1,2064,128]{2,1,0:T(8,128)(2,1)S(1)} %collective-permute-done.9.refs_1_, s16[1,2064,128]{2,1,0:T(8,128)(2,1)S(1)} %collective-permute-done.10.refs_2_), custom_call_target="tpu_custom_call" | custom-call | flops 20000000 | bytes 1000000 | tf_op jit(solution)/shard_map/pallas_call | solution.py:52
Async XLA Ops:
  0.0 24.3 %collective-permute-start.3 = (bf16[8,4,128,128]{3,2,1,0:T(8,128)(2,1)}, bf16[8,4,128,128]{3,2,1,0:T(8,128)(2,1)S(1)}, u32[]{:S(2)}, u32[]{:S(2)}) collective-permute-start(bf16[8,4,128,128]{3,2,1,0:T(8,128)(2,1)} %p_hbm.1), channel_id=1, source_target_pairs={{1,3},{2,0},{3,5},{4,2},{5,7},{6,4},{7,9},{8,6},{9,11},{10,8},{11,... | collective-permute-start | bytes 3145736 | tf_op jit(solution)/shard_map/ppermute | solution.py:417
  11.7 35.1 %collective-permute-start.1 = (bf16[56,128,128]{2,1,0:T(8,128)(2,1)}, bf16[56,128,128]{2,1,0:T(8,128)(2,1)S(1)}, u32[]{:S(2)}, u32[]{:S(2)}) collective-permute-start(bf16[56,128,128]{2,1,0:T(8,128)(2,1)} %bitcast.6), channel_id=1, source_target_pairs={{0,128},{128,0},{256,384},{384,256},{1,385},{129,257},{257,129},{3... | collective-permute-start | bytes 5505032 | tf_op jit(solution)/shard_map/ppermute | solution.py:422
  15.2 26.0 %collective-permute-start.5 = (bf16[8,4,128,128]{3,2,1,0:T(8,128)(2,1)}, bf16[8,4,128,128]{3,2,1,0:T(8,128)(2,1)S(1)}, u32[]{:S(2)}, u32[]{:S(2)}) collective-permute-start(bf16[8,4,128,128]{3,2,1,0:T(8,128)(2,1)} %p_hbm.1), channel_id=1, source_target_pairs={{0,1},{1,0},{2,3},{3,2},{4,5},{5,4},{6,7},{7,6},{8,9},{9,8},{10,11... | collective-permute-start | bytes 3145736 | tf_op jit(solution)/shard_map/ppermute | solution.py:417
  24.3 18.5 %collective-permute-start.4 = (bf16[8,4,128,128]{3,2,1,0:T(8,128)(2,1)S(1)}, bf16[8,4,128,128]{3,2,1,0:T(8,128)(2,1)S(1)}, u32[]{:S(2)}, u32[]{:S(2)}) collective-permute-start(bf16[8,4,128,128]{3,2,1,0:T(8,128)(2,1)S(1)} %collective-permute-done.3.refs_0_), channel_id=1, source_target_pairs={{0,1},{1,0},{2,3},{3,2},{4,5},{5,4},{6,7},{7,6},{8,9},{9,8},{10,11... | collective-permute-start | bytes 3145736 | tf_op jit(solution)/shard_map/ppermute | solution.py:417
  26.2 19.4 %collective-permute-start.2 = (bf16[8,4,128,128]{3,2,1,0:T(8,128)(2,1)}, bf16[8,4,128,128]{3,2,1,0:T(8,128)(2,1)S(1)}, u32[]{:S(2)}, u32[]{:S(2)}) collective-permute-start(bf16[8,4,128,128]{3,2,1,0:T(8,128)(2,1)} %p_hbm.1), channel_id=1, source_target_pairs={{0,2},{2,4},{3,1},{4,6},{5,3},{6,8},{7,5},{8,10},{9,7},{10,12},{11... | collective-permute-start | bytes 3145736 | tf_op jit(solution)/shard_map/ppermute | solution.py:417
  28.1 8.9 %collective-permute-start = (s32[8,1,7]{0,1,2:T(1,128)}, s32[8,1,7]{0,1,2:T(1,128)S(1)}, u32[]{:S(2)}, u32[]{:S(2)}) collective-permute-start(s32[8,1,7]{0,1,2:T(1,128)} %param.6), channel_id=1, source_target_pairs={{0,128},{128,0},{256,384},{384,256},{1,385},{129,257},{257,129},{3... | collective-permute-start | bytes 680 | tf_op jit(solution)/shard_map/ppermute | solution.py:422
  54.0 21.0 %collective-permute-start.7 = (s16[1,2064,128]{2,1,0:T(8,128)(2,1)S(1)}, s16[1,2064,128]{2,1,0:T(8,128)(2,1)S(1)}, u32[]{:S(2)}, u32[]{:S(2)}) collective-permute-start(s16[1,2064,128]{2,1,0:T(8,128)(2,1)S(1)} %shard_map.60), channel_id=1, source_target_pairs={{1,130},{129,2},{257,386},{385,258},{2,385},{130,257},{258,129},{3... | collective-permute-start | bytes 1585160 | tf_op jit(solution)/shard_map/ppermute | solution.py:422
  61.2 13.8 %collective-permute-start.6 = (s16[1,2064,128]{2,1,0:T(8,128)(2,1)S(1)}, s16[1,2064,128]{2,1,0:T(8,128)(2,1)S(1)}, u32[]{:S(2)}, u32[]{:S(2)}) collective-permute-start(s16[1,2064,128]{2,1,0:T(8,128)(2,1)S(1)} %get-tuple-element.42), channel_id=1, source_target_pairs={{0,384},{128,256},{256,128},{384,0},{1,129},{129,1},{257,385},{385... | collective-permute-start | bytes 1585160 | tf_op jit(solution)/shard_map/ppermute | solution.py:422
  66.1 10.2 %collective-permute-start.10 = (s16[1,2064,128]{2,1,0:T(8,128)(2,1)S(1)}, s16[1,2064,128]{2,1,0:T(8,128)(2,1)S(1)}, u32[]{:S(2)}, u32[]{:S(2)}) collective-permute-start(s16[1,2064,128]{2,1,0:T(8,128)(2,1)S(1)} %shard_map.64), channel_id=1, source_target_pairs={{0,1},{1,0},{2,3},{3,2},{4,5},{5,4},{6,7},{7,6},{8,9},{9,8},{10,11... | collective-permute-start | bytes 1585160 | tf_op jit(solution)/shard_map/ppermute | solution.py:417
  68.0 12.7 %collective-permute-start.9 = (s16[1,2064,128]{2,1,0:T(8,128)(2,1)S(1)}, s16[1,2064,128]{2,1,0:T(8,128)(2,1)S(1)}, u32[]{:S(2)}, u32[]{:S(2)}) collective-permute-start(s16[1,2064,128]{2,1,0:T(8,128)(2,1)S(1)} %shard_map.63), channel_id=1, source_target_pairs={{1,2},{2,1},{3,4},{4,3},{5,6},{6,5},{7,8},{8,7},{9,10},{10,9},{11,... | collective-permute-start | bytes 1585160 | tf_op jit(solution)/shard_map/ppermute | solution.py:417
  70.0 11.7 %collective-permute-start.8 = (s16[1,2064,128]{2,1,0:T(8,128)(2,1)S(1)}, s16[1,2064,128]{2,1,0:T(8,128)(2,1)S(1)}, u32[]{:S(2)}, u32[]{:S(2)}) collective-permute-start(s16[1,2064,128]{2,1,0:T(8,128)(2,1)S(1)} %shard_map.62), channel_id=1, source_target_pairs={{0,385},{128,257},{256,129},{384,1},{1,128},{129,0},{257,384},{385... | collective-permute-start | bytes 1585160 | tf_op jit(solution)/shard_map/ppermute | solution.py:422
